TPU v7x, 128 devices: a whole 4x4x4 slice. The times are simulated.
128 devices in a mesh: seq: 16 (over x, y_lo, core), tp: 8 (over z, y_hi).
Axes of the slice: x: 4, y: 4 (y_hi: 2, y_lo: 2; y = y_hi * 2 + y_lo), z: 4, core: 2. Of those that a mesh axis runs over, the one named last changes fastest.
Arguments:
- x_old: bfloat16 [8192, 4608], P('seq', 'tp'), may hold values from -6 to 6
- old_blocks: int32 [16], replicated, may hold values from 1 to 4, 32 in all
- new_blocks: int32 [16], replicated, may hold values from 1 to 4, 32 in all
- order: int32 [16], replicated, may hold values from 0 to 15, as said below
- pre_gain: float32 [4608], replicated, may hold values from 0.25 to 1.75
- post_gain: float32 [4608], replicated, may hold values from 0.25 to 1.75
- w_query: bfloat16 [4608, 4096], P('seq', 'tp'), may hold values from -0.59765625 to 0.59765625
- w_key: bfloat16 [4608, 2048], P('seq', 'tp'), may hold values from -0.09375 to 0.09375
- w_value: bfloat16 [4608, 2048], P('seq', 'tp'), may hold values from -0.09375 to 0.09375
- w_out_t: bfloat16 [4608, 4096], P('seq', 'tp'), may hold values from -0.09375 to 0.09375
Outputs:
- layer_out: bfloat16 [8192, 4608], P(('seq', 'tp'))
Inputs may be any that keep to these rules, and one draw needn't show every extreme that they name: `old_blocks`: counts of 128-row blocks, at least one each; they sum to 32, and the largest is exactly 4. `new_blocks`: counts of 128-row blocks, at least one each; they sum to 32, and the largest is exactly 4. A permutation of the seq indices with order[15] = 0 and order[7] = 15; the other indices, taken in increasing order, hold 1 to 14 in increasing order, except that aligned pairs of them (first and second, third and fourth, and so on) are swapped or not, pair by pair.
All inputs are finite; a program needn't handle non-finite values.
Results may differ from a plain program's by a relative error of at most 0.013.
Values may be sent and summed in bfloat16 or wider, within the bound.
A program may use at most 128 MiB of HBM per device.

v0:
```python
import math

import jax
import jax.numpy as jnp
from jax import lax
from jax.sharding import Mesh
from jax.sharding import PartitionSpec as P

D = 4608
HEADS = 32
HEAD = 128
BLOCK = 128
TP = ("tp_0", "tp_1")
SEQ_TP = ("seq", "tp_0", "tp_1")


EPS = 1e-06


def in_one_piece(arrays, axis, dim, along):
    widths = [a.shape[along] for a in arrays]
    both = jnp.concatenate(arrays, axis=along)
    whole = lax.all_gather(both, axis, axis=dim, tiled=True)
    return tuple(jnp.split(whole, [sum(widths[:k]) for k in range(1, len(widths))], axis=along))


def sum_by_axis(terms, axes):
    so_far = terms.astype(jnp.bfloat16)
    for axis in axes:
        so_far = lax.psum_scatter(so_far, axis, scatter_dimension=0, tiled=True)
    return so_far.astype(jnp.float32)


def offsets(blocks):
    return (jnp.cumsum(blocks) - blocks) * BLOCK


def rotate(values, places):
    half = values.shape[-1] // 2
    inverse = jnp.exp(
        jnp.arange(half, dtype=jnp.float32) * (-2.0 * math.log(10000.0) / values.shape[-1])
    )
    angles = places.astype(jnp.float32)[:, None] * inverse[None, :]
    cosine = jnp.cos(angles)[:, None, :]
    sine = jnp.sin(angles)[:, None, :]
    first = values[..., :half]
    second = values[..., half:]
    return jnp.concatenate(
        [first * cosine - second * sine, second * cosine + first * sine], axis=-1
    )


def rms_scale(values, gain):
    return values * lax.rsqrt(jnp.mean(values * values, axis=-1, keepdims=True) + EPS) * gain


def per_device(
    x_old, old_blocks, new_blocks, order, pre_gain, post_gain, w_query, w_key, w_value, w_out_t
):
    seq_count = lax.axis_size("seq")
    tp_count = lax.axis_size(TP)
    capacity = x_old.shape[0]
    seq_index = lax.axis_index("seq")
    tp_index = lax.axis_index(TP)
    old_start = offsets(old_blocks)
    new_start = offsets(new_blocks)
    new_count = new_blocks * BLOCK
    slot_ids = jnp.arange(capacity, dtype=jnp.int32)
    device_ids = jnp.arange(seq_count, dtype=jnp.int32)
    my_start = new_start[seq_index]
    my_count = new_count[seq_index]
    gathered = lax.all_gather(x_old, "seq", axis=0, tiled=True)
    wanted = my_start + slot_ids
    shard = jnp.sum((old_start[None, :] <= wanted[:, None]).astype(jnp.int32), axis=1) - 1
    match_shard = device_ids[None, :] == shard[:, None]
    holder = jnp.sum(
        device_ids[None, :] * (order[None, :] == shard[:, None]).astype(jnp.int32), axis=1
    )
    shard_start = jnp.sum(jnp.where(match_shard, old_start[None, :], 0), axis=1)
    source = jnp.clip(holder * capacity + wanted - shard_start, 0, seq_count * capacity - 1)
    own_rows = jnp.where(
        (slot_ids < my_count)[:, None], gathered[source], jnp.zeros((), jnp.bfloat16)
    )
    full_rows = lax.all_gather(own_rows, TP, axis=1, tiled=True)
    resident_f = full_rows.astype(jnp.float32)
    normed = rms_scale(resident_f, pre_gain).astype(jnp.bfloat16)
    query_full, key_full, value_full, out_full = in_one_piece(
        (w_query, w_key, w_value, w_out_t), "seq", 0, 1
    )
    query_raw = jnp.dot(normed, query_full, preferred_element_type=jnp.float32)
    key_raw = jnp.dot(normed, key_full, preferred_element_type=jnp.float32)
    value_raw = jnp.dot(normed, value_full, preferred_element_type=jnp.float32)
    local_heads = query_raw.shape[1] // HEAD
    local_kv = key_raw.shape[1] // HEAD
    group = local_heads // local_kv
    positions = my_start + slot_ids
    query_rot = (
        rotate(query_raw.reshape(capacity, local_heads, HEAD), positions) * (D // HEADS) ** (-0.5)
    ).astype(jnp.bfloat16)
    query_four = query_rot.reshape(capacity, local_kv, group, HEAD)
    key_rot = (
        rotate(key_raw.reshape(capacity, local_kv, HEAD), positions)
        .astype(jnp.bfloat16)
        .reshape(capacity, local_kv * HEAD)
    )
    value_b = value_raw.astype(jnp.bfloat16)
    start_state = (
        jnp.zeros((capacity, local_kv, group, HEAD), jnp.float32),
        jnp.zeros((local_kv, group, capacity), jnp.float32),
    )
    key_piece, value_piece = in_one_piece((key_rot, value_b), "seq", 0, 1)
    piece_rows = key_piece.shape[0]

    def one_block(carry_in, offset):
        numer, denom = carry_in
        key_block = lax.dynamic_slice_in_dim(key_piece, offset, capacity, 0).reshape(
            capacity, local_kv, HEAD
        )
        value_block = lax.dynamic_slice_in_dim(value_piece, offset, capacity, 0).reshape(
            capacity, local_kv, HEAD
        )
        global_ids = offset + jnp.arange(capacity, dtype=jnp.int32)
        owner = global_ids // capacity
        within = global_ids - owner * capacity
        onehot = owner[:, None] == device_ids[None, :]
        key_pos = jnp.sum(jnp.where(onehot, new_start[None, :], 0), axis=1) + within
        key_live = within < jnp.sum(jnp.where(onehot, new_count[None, :], 0), axis=1)
        allowed = key_live[None, :] & (key_pos[None, :] <= positions[:, None])
        score = jnp.einsum(
            "qcgd,kcd->cgqk", query_four, key_block, preferred_element_type=jnp.float32
        )
        weight = jnp.where(allowed[None, None, :, :], jnp.exp(50.0 * jnp.tanh(score / 50.0)), 0.0)
        denom = denom + jnp.sum(weight, axis=3)
        numer = numer + jnp.einsum(
            "cgqk,kcd->qcgd",
            weight.astype(jnp.bfloat16),
            value_block,
            preferred_element_type=jnp.float32,
        )
        return (numer, denom)

    numer, denom = lax.fori_loop(
        0,
        piece_rows // capacity,
        lambda turn, state: one_block(state, turn * capacity),
        start_state,
    )
    context = (
        (numer / jnp.transpose(denom, (2, 0, 1))[:, :, :, None])
        .astype(jnp.bfloat16)
        .reshape(capacity, local_heads * HEAD)
    )
    share = capacity // tp_count
    projected = sum_by_axis(
        lax.dot_general(
            context, out_full, (((1,), (1,)), ((), ())), preferred_element_type=jnp.float32
        ),
        TP,
    )
    first_row = tp_index * share
    residual = lax.dynamic_slice_in_dim(resident_f, first_row, share, 0)
    refreshed = residual + rms_scale(projected, post_gain)
    live = first_row + jnp.arange(share, dtype=jnp.int32) < my_count
    return jnp.where(live[:, None], refreshed, 0.0).astype(jnp.bfloat16)


def solution(mesh):
    torus = Mesh(mesh.devices.reshape(mesh.shape["seq"], 4, 2), ("seq", "tp_0", "tp_1"))
    in_specs = (
        P("seq", TP),
        P(),
        P(),
        P(),
        P(),
        P(),
        P("seq", TP),
        P("seq", TP),
        P("seq", TP),
        P("seq", TP),
    )
    out_specs = P(SEQ_TP, None)
    return jax.shard_map(
        per_device, mesh=torus, in_specs=in_specs, out_specs=out_specs, check_vma=False
    )
```

profile of v0, /device:TPU:1, one launch (start us, length us, event | category | flops | bytes accessed | tf_op | source)
XLA Modules:
  0.0 493.3 jit_solution(17339269859793845897)
XLA Ops:
  6.5 2.2 copy.36
  15.9 58.7 %all-gather.5.cloned.1.call-done = bf16[8192,576]{1,0:T(8,128)(2,1)} async-done(((bf16[512,576]{1,0:T(8,128)(2,1)}), bf16[8192,576]{1,0:T(8,128)(2,1)}) %all-gather.5.cloned.1.call-update) | async-done | bytes 9437200 | tf_op jit(solution)/shard_map/all_gather | solution.py:72
  74.6 7.5 %gather_fusion = bf16[512,576]{1,0:T(8,128)(2,1)S(1)} fusion(bf16[8192,576]{1,0:T(8,128)(2,1)} %all-gather.5.cloned.1.call-done, s32[1024]{0:T(1024)S(1)} %pad_clamp_fusion), kind=kCustom, calls=%fused_computation | custom fusion | bytes 1181696 | tf_op jit(solution)/shard_map/gather | solution.py:82
  85.0 73.8 %all-gather.7.cloned.1.call-done = bf16[512,4608]{0,1:T(8,128)(2,1)} async-done(((bf16[512,576]{0,1:T(8,128)(2,1)}), bf16[512,4608]{0,1:T(8,128)(2,1)}) %all-gather.7.cloned.1.call-update) | async-done | bytes 4718608 | tf_op jit(solution)/shard_map/all_gather | solution.py:84
  158.8 6.8 %copy.40 = bf16[512,4608]{1,0:T(8,128)(2,1)} copy(bf16[512,4608]{0,1:T(8,128)(2,1)} %all-gather.7.cloned.1.call-done) | data formatting | bytes 9437184 | tf_op jit(solution)/shard_map/all_gather | solution.py:84
  165.6 3.3 multiply_reduce_fusion
  168.9 69.7 %all-gather.9.cloned.1.call-done = bf16[4608,1536]{1,0:T(8,128)(2,1)} async-done(((bf16[288,1536]{1,0:T(8,128)(2,1)}), bf16[4608,1536]{1,0:T(8,128)(2,1)}) %all-gather.9.cloned.1.call-update) | async-done | bytes 14155792 | tf_op jit(solution)/shard_map/all_gather | solution.py:23
  238.6 4.8 fusion.32
  243.6 4.8 fusion.34
  249.5 6.5 %fusion.28 = f32[512,512]{0,1:T(8,128)S(1)} fusion(bf16[4608,1536]{1,0:T(8,128)(2,1)} %all-gather.9.cloned.1.call-done, f32[4608]{0:T(1024)S(1)} %copy-done.6, f32[512]{0:T(512)S(1)} %add_rsqrt_fusion, bf16[512,4608]{1,0:T(8,128)(2,1)} %copy.40), kind=kOutput, calls=%fused_computation.39 | convolution fusion | flops 2425356288 | bytes 10506240 | tf_op jit(solution)/shard_map/dot_general | solution.py:90
  257.3 45.0 %all-gather.11.cloned.1.call-done = bf16[8192,512]{0,1:T(8,128)(2,1)} async-done(((bf16[512,512]{0,1:T(8,128)(2,1)}), bf16[8192,512]{0,1:T(8,128)(2,1)}) %all-gather.11.cloned.1.call-update) | async-done | bytes 8388624 | tf_op jit(solution)/shard_map/all_gather | solution.py:23
  302.2 5.9 %fusion.44 = (bf16[8192,256]{0,1:T(8,128)(2,1)}, bf16[8192,256]{0,1:T(8,128)(2,1)}) fusion(bf16[8192,512]{0,1:T(8,128)(2,1)} %all-gather.11.cloned.1.call-done), kind=kLoop, calls=%fused_computation.84 | loop fusion | bytes 16777216 | tf_op jit(solution)/shard_map/split | solution.py:24
  308.2 88.0 %while.18 = (s32[]{:T(128)}, f32[512,2,2,128]{0,3,2,1:T(8,128)S(1)}, f32[2,2,512]{2,1,0:T(2,128)S(1)}, bf16[8192,256]{0,1:T(8,128)(2,1)}, s32[16]{0:T(128)S(1)},...) while((s32[]{:T(128)}, ...), condition=%wide.region_10.11_spmd.clone, body=%wide.region_6.10_spmd.clone.sunk | while | flops 546378240 | bytes 13423954 | solution.py:142
  310.2 1.8 fusion.63
  312.0 1.6 fusion.64
  315.7 1.8 fusion.63
  317.5 1.6 fusion.64
  321.2 1.8 fusion.63
  323.0 1.6 fusion.64
  326.7 1.8 fusion.63
  328.5 1.6 fusion.64
  332.2 1.8 fusion.63
  334.0 1.6 fusion.64
  337.7 1.8 fusion.63
  343.2 1.8 fusion.63
  345.0 1.6 fusion.64
  348.7 1.8 fusion.63
  350.5 1.6 fusion.64
  354.2 1.8 fusion.63
  356.0 1.6 fusion.64
  359.7 1.8 fusion.63
  361.5 1.6 fusion.64
  365.2 1.8 fusion.63
  367.0 1.6 fusion.64
  370.7 1.8 fusion.63
  372.5 1.6 fusion.64
  376.2 1.8 fusion.63
  378.0 1.6 fusion.64
  381.7 1.8 fusion.63
  383.5 1.6 fusion.64
  387.2 1.8 fusion.63
  389.0 1.6 fusion.64
  392.7 1.8 fusion.63
  396.3 6.7 %convolution_convert_fusion = bf16[512,4608]{1,0:T(8,128)(2,1)} fusion(bf16[512,512]{0,1:T(8,128)(2,1)S(1)} %bitcast.65, bf16[4608,1536]{1,0:T(8,128)(2,1)} %all-gather.9.cloned.1.call-done), kind=kOutput, calls=%fused_computation.37 | convolution fusion | flops 2418278400 | bytes 9961472 | tf_op jit(solution)/shard_map/dot_general | solution.py:155
  403.1 51.9 %reduce-scatter.3.cloned.1.call-done = bf16[128,4608]{1,0:T(8,128)(2,1)} async-done(((bf16[512,4608]{1,0:T(8,128)(2,1)}), bf16[128,4608]{1,0:T(8,128)(2,1)}) %reduce-scatter.3.cloned.1.call-update) | async-done | bytes 1179664 | tf_op jit(solution)/shard_map/reduce_scatter | solution.py:30
  455.6 7.2 %convert_element_type.53 = f32[512,4608]{1,0:T(8,128)} convert(bf16[512,4608]{1,0:T(8,128)(2,1)} %copy.40) | non-fusion elementwise | flops 2359296 | bytes 14155776 | tf_op jit(solution)/shard_map/convert_element_type | solution.py:85
  462.8 19.7 %reduce-scatter.5.cloned.1.call-done = bf16[64,4608]{1,0:T(8,128)(2,1)} async-done(((bf16[128,4608]{1,0:T(8,128)(2,1)}), bf16[64,4608]{1,0:T(8,128)(2,1)}) %reduce-scatter.5.cloned.1.call-update) | async-done | bytes 589840 | tf_op jit(solution)/shard_map/reduce_scatter | solution.py:30
  483.9 2.6 fusion.41
  (177 shorter events, 50.3 us)
Async XLA Ops:
  6.5 68.0 %all-gather.5.cloned.1.call-start = ((), (), s32[]{:S(2)}) async-start(), calls=%async_computation.2 | async-start | bytes 11141120 | tf_op jit(solution)/shard_map/all_gather | solution.py:72
  8.7 74.6 %copy-start.1 = (bf16[288,512]{1,0:T(8,128)(2,1)S(1)}, bf16[288,512]{1,0:T(8,128)(2,1)}, u32[]{:S(2)}) copy-start(bf16[288,512]{1,0:T(8,128)(2,1)} %param.21) | copy-start | bytes 884740
  8.7 74.6 %copy-start.2 = (bf16[288,512]{1,0:T(8,128)(2,1)S(1)}, bf16[288,512]{1,0:T(8,128)(2,1)}, u32[]{:S(2)}) copy-start(bf16[288,512]{1,0:T(8,128)(2,1)} %param.18) | copy-start | bytes 884740
  8.8 74.6 %copy-start.3 = (bf16[288,256]{1,0:T(8,128)(2,1)S(1)}, bf16[288,256]{1,0:T(8,128)(2,1)}, u32[]{:S(2)}) copy-start(bf16[288,256]{1,0:T(8,128)(2,1)} %param.20) | copy-start | bytes 442372
  8.8 74.6 %copy-start.4 = (bf16[288,256]{1,0:T(8,128)(2,1)S(1)}, bf16[288,256]{1,0:T(8,128)(2,1)}, u32[]{:S(2)}) copy-start(bf16[288,256]{1,0:T(8,128)(2,1)} %param.19) | copy-start | bytes 442372
  8.8 150.0 %all-gather.7.cloned.1.call-start = ((), (), s32[]{:S(2)}) async-start(), calls=%async_computation.3 | async-start | bytes 5308416 | tf_op jit(solution)/shard_map/all_gather | solution.py:84
  83.3 155.3 %all-gather.9.cloned.1.call-start = ((), (), s32[]{:S(2)}) async-start(), calls=%async_computation.4 | async-start | bytes 15040512 | tf_op jit(solution)/shard_map/all_gather | solution.py:23
  84.4 217.9 %all-gather.11.cloned.1.call-start = ((), (), s32[]{:S(2)}) async-start(), calls=%async_computation.5 | async-start | bytes 8912896 | tf_op jit(solution)/shard_map/all_gather | solution.py:23
  165.6 73.0 %copy-start.6 = (f32[4608]{0:T(1024)S(1)}, f32[4608]{0:T(1024)}, u32[]{:S(2)}) copy-start(f32[4608]{0:T(1024)} %param.16) | copy-start | bytes 55300
  249.3 205.7 %reduce-scatter.3.cloned.1.call-start = ((), (), s32[]{:S(2)}) async-start(), calls=%async_computation.6 | async-start | bytes 5898240 | tf_op jit(solution)/shard_map/reduce_scatter | solution.py:30
  257.3 50.9 %copy-start = (f32[512,2,2,128]{0,3,2,1:T(8,128)S(1)}, f32[512,2,2,128]{0,3,2,1:T(8,128)}, u32[]{:S(2)}) copy-start(f32[512,2,2,128]{0,3,2,1:T(8,128)} %custom-call) | copy-start | bytes 3145732
  403.0 79.5 %reduce-scatter.5.cloned.1.call-start = ((), (), s32[]{:S(2)}) async-start(), calls=%async_computation.7 | async-start | bytes 1769472 | tf_op jit(solution)/shard_map/reduce_scatter | solution.py:30
  455.6 28.2 %copy-start.5 = (f32[4608]{0:T(1024)S(1)}, f32[4608]{0:T(1024)}, u32[]{:S(2)}) copy-start(f32[4608]{0:T(1024)} %param.17) | copy-start | bytes 55300
Sparse Core Ops, SparseCore 0:
  9.0 65.4 all-gather.4
  83.4 75.3 all-gather.6
  160.5 78.0 all-gather.8
  249.4 52.8 all-gather.10
  403.1 51.7 reduce-scatter.2
  457.1 25.3 reduce-scatter.4
where the time goes:
time: 494 us; the launch traced here: 493 us
  waiting for transfers between devices  319 us (65%)
  matrix products  77.3 us (16%)
  local copies, waits for them, and re-layouts  44 us (9%)
  other arithmetic  37.9 us (8%)
  between operations  13.8 us (3%)
    all_gather x2, waiting for transfers between devices, in_one_piece(): whole = lax.all_gather(both, axis, axis=dim, tiled=True)  115 us
    all_gather x1, waiting for transfers between devices, per_device(): full_rows = lax.all_gather(own_rows, TP, axis=1, tiled=True)  73.8 us
    reduce_scatter x2, waiting for transfers between devices, sum_by_axis(): so_far = lax.psum_scatter(so_far, axis, scatter_dimension=0, tiled=True)  71.6 us
    all_gather x1, waiting for transfers between devices, per_device(): gathered = lax.all_gather(x_old, 'seq', axis=0, tiled=True)  58.7 us
    dot_general x16, matrix products, one_block(): jnp.einsum('qcgd,kcd->cgqk', query_four, key_block, preferred_element_typ...  28.1 us
    dot_general x16, matrix products, one_block(): jnp.einsum('cgqk,kcd->qcgd', weight.astype(jnp.bfloat16), value_block, pr...  26.3 us
    dynamic_slice x16, local copies, waits for them, and re-layouts, one_block(): lax.dynamic_slice_in_dim(key_piece, offset, capacity, 0)  17.2 us
    add x17, other arithmetic, per_device(): wanted = my_start + slot_ids  9.9 us
  transfers between devices with their start and end apart: 6, of which 6 were waited for; matrix products, arithmetic and copies ran while one was open for 7% of the time, Pallas kernels for 0%

commit v1 on v0

v1 whole, which is shorter than its diff:
```python
import functools
import math

import jax
import jax.numpy as jnp
from jax import lax
from jax.experimental import pallas as pl
from jax.experimental.pallas import tpu as pltpu
from jax.sharding import Mesh
from jax.sharding import PartitionSpec as P

D = 4608
HEADS = 32
HEAD = 128
BLOCK = 128
EPS = 1e-06
BF = jnp.bfloat16
F32 = jnp.float32
VM = pltpu.VMEM
DMA = pltpu.SemaphoreType.DMA


def kept(at, c):
    return 2 * at + lax.rem(at + c, 2)


def coords():
    return tuple(lax.axis_index(name) for name in ("x", "yl", "c", "z", "yh"))


def copy_to(src, dst, send_sem, recv_sem, device):
    return pltpu.make_async_remote_copy(
        src_ref=src,
        dst_ref=dst,
        send_sem=send_sem,
        recv_sem=recv_sem,
        device_id=device,
        device_id_type=pl.DeviceIdType.MESH,
    )


def greet(devices):
    sem = pltpu.get_barrier_semaphore()
    for device in devices:
        pl.semaphore_signal(sem, inc=1, device_id=device, device_id_type=pl.DeviceIdType.MESH)
    pl.semaphore_wait(sem, len(devices))


def mod4(v):
    return lax.rem(v + 4, 4)


class Gather4:
    def __init__(self, views, axis, me, send, recv):
        one, two = me + 1 - 2 * lax.rem(me, 2), 3 - me
        far = two + 1 - 2 * lax.rem(two, 2)
        self.moves = [
            (me, one, 0, one),
            (me, two, 1, two),
            (me, two, 0, two),
            (me, one, 1, one),
            (one, far, 0, two),
            (two, far, 1, one),
        ]
        self.views, self.axis, self.send, self.recv = views, axis, send, recv

    def each(self, move, got):
        sent, received, half, partner = self.moves[move]
        for n, view in enumerate(self.views):
            ref = view(received if got else sent, half)
            at = n * 6 + move
            yield copy_to(ref, ref, self.send.at[at], self.recv.at[at], {self.axis: partner})

    def go(self, *moves):
        for move in moves:
            for copy in self.each(move, False):
                copy.start()

    def got(self, *moves):
        for move in moves:
            for copy in self.each(move, True):
                copy.wait_recv()

    def sent(self):
        for move in range(6):
            for copy in self.each(move, False):
                copy.wait_send()


def rows(ref, start, size, unit=16):
    return ref.at[pl.ds(pl.multiple_of(start, unit), size)]


def lanes(start, size):
    return pl.ds(pl.multiple_of(start, 128), size)


def kernel_in(
    old_ref, order_ref, xt, gain, cos, sin, wq_in, wk_in, wv_in, wo_in,
    q_out, kv_out, xs, wo,
    wq, wk, wv, slots, landed, normed, squares, near, other, to_y, from_y, mine,
    s_w, s_one, r_one, s_two, r_two, s_three, r_three, s_wg, r_wg, s_z, r_z, s_q, r_q, s_c, r_c, s_y, r_y,
):
    x, yl, c, z, yh = coords()
    at = pl.ds(pl.multiple_of(x * 288, 16), 288)
    owns = [
        pltpu.make_async_copy(src, dst.at[at], s_w.at[n])
        for n, (src, dst) in enumerate(((wq_in, wq), (wk_in, wk), (wv_in, wv), (wo_in, wo)))
    ]
    for copy in owns:
        copy.start()
    starts, total = [], 0
    for m in range(16):
        starts.append(total)
        total = total + old_ref[m]
    k = order_ref[x * 4 + yl * 2 + c]
    first = sum([jnp.where(k > m, old_ref[m], 0) for m in range(15)])
    for r in range(4):
        b = lax.rem(r - first + 64, 4)
        for h in range(2):
            part = [xt[h * 288:(h + 1) * 288, n * 128:(n + 1) * 128] for n in range(4)]
            low = jnp.where(b == 0, part[0], part[1])
            slots[r * 2 + h] = jnp.where(b < 2, low, jnp.where(b == 2, part[2], part[3]))
    ring_peers = [
        {"x": lax.rem(x + dx, 4), "c": c + dc - 2 * c * dc} for dx in range(4) for dc in range(2)
    ][1:]
    y_one = {"yl": 1 - yl}
    y_two = {"yl": 1 - yl, "yh": 1 - yh}
    group = [
        {"z": lax.rem(z + dz, 4), "yl": yl + dy - 2 * yl * dy, "c": c + dc - 2 * c * dc}
        for dz in range(4) for dy in range(2) for dc in range(2)
    ][1:]
    greet(ring_peers + [y_two] + group)
    here = x * 2 + c
    landed[here] = slots[here]
    one = []
    for d, peer in enumerate(ring_peers, 1):
        copy = copy_to(slots.at[peer["x"] * 2 + peer["c"]], landed.at[here], s_one.at[d], r_one.at[d], peer)
        copy.start()
        one.append(copy)
    for copy in owns:
        copy.wait()

    def half_rows(ref):
        return lambda chunk, half: rows(ref, chunk * 288 + half * 144, 144)

    weights = Gather4([half_rows(r) for r in (wq, wk, wv, wo)], "x", x, s_wg, r_wg)
    weights.go(0, 1, 2, 3)
    straight = yl == yh
    two, three = [], []
    for d in range(8):
        dx, dc = d // 2, d % 2
        slot = mod4(x - dx) * 2 + c + dc - 2 * c * dc
        if d > 0:
            copy_to(slots.at[slot], landed.at[slot], s_one.at[d], r_one.at[d], y_one).wait_recv()
        copy = copy_to(landed.at[slot], landed.at[8 + slot], s_two.at[d], r_two.at[d], y_two)
        copy.start()
        two.append(copy)
        copy = copy_to(landed.at[slot], landed.at[16 + slot], s_three.at[d], r_three.at[d], y_one)
        relay = copy_to(landed.at[8 + slot], landed.at[16 + slot], s_three.at[d], r_three.at[d], y_one)
        three.append((copy, relay))
        pl.when(jnp.logical_not(straight))(copy.start)
    for d in range(8):
        two[d].wait_recv()
        pl.when(straight)(three[d][1].start)
    weights.got(0, 1)
    weights.go(4, 5)
    for d in range(8):
        three[d][0].wait_recv()
    me = z * 4 + yl * 2 + c
    first_buffer = jnp.where(straight, 0, 1)
    for place in range(8):
        g = x + 4 * kept(place % 4, place // 4)
        shard = sum([jnp.where(starts[m] <= g, 1, 0) for m in range(16)]) - 1
        holder = sum([jnp.where(order_ref[p] == shard, p, 0) for p in range(16)])
        y_source = lax.rem(lax.div(holder, 2), 2)
        source = jnp.where(y_source == yh, first_buffer, 2) * 8 + lax.div(holder, 4) * 2 + lax.rem(holder, 2)
        block = landed[source]
        xs[pl.ds(pl.multiple_of(z * 288, 16), 288), place * 128:(place + 1) * 128] = block
        wide = block.astype(F32)
        squares[me, place:place + 1, :] = jnp.sum(wide * wide, axis=0, keepdims=True)
    gather = Gather4([half_rows(xs)], "z", z, s_z, r_z)
    gather.go(0, 1, 2, 3)
    sums = []
    for e, peer in enumerate(group, 1):
        copy = copy_to(squares.at[me], squares.at[me], s_q.at[e], r_q.at[e], peer)
        copy.start()
        sums.append(copy)
    gather.got(0, 1)
    gather.go(4, 5)
    for copy in sums:
        copy.wait_recv()
    gather.got(2, 3, 4, 5)
    weights.got(2, 3, 4, 5)
    factor = lax.rsqrt(jnp.sum(squares[...], axis=0) * (1.0 / D) + EPS)
    for place in range(8):
        scale = factor[place:place + 1, :]

        def norm_rows(n, _, place=place, scale=scale):
            part = pl.ds(pl.multiple_of(n * 144, 16), 144)
            at = (part, slice(place * 128, (place + 1) * 128))
            normed[at] = (xs[at].astype(F32) * scale * gain[part, :]).astype(BF)
            return 0

        lax.fori_loop(0, 8, norm_rows, 0)

    def quarter(dst, y, core):
        right = normed[:, lanes(core * 512, 512)]

        def dot(left):
            return lax.dot_general(left, right, (((0,), (0,)), ((), ())), preferred_element_type=F32)

        dst[0:256, :] = dot(wq[:, lanes(y * 256, 256)])
        dst[256:384, :] = dot(wk[:, lanes(y * 128, 128)])
        dst[384:512, :] = dot(wv[:, lanes(y * 128, 128)])

    core = {"c": 1 - c}
    quarter(near.at[0], 1 - yl, 1 - c)
    to_core = [copy_to(near.at[n], other.at[n], s_c.at[n], r_c.at[n], core) for n in range(2)]
    to_core[0].start()
    quarter(mine, 1 - yl, c)
    to_core[0].wait_recv()
    to_partner = []
    for n in range(4):
        part = slice(n * 128, (n + 1) * 128)
        to_y[part, :] = (mine[part, :] + other[0, part, :]).astype(BF)
        copy = copy_to(to_y.at[part], from_y.at[part], s_y.at[n], r_y.at[n], y_one)
        to_partner.append(copy)
        copy.start()
    quarter(near.at[1], yl, 1 - c)
    to_core[1].start()
    quarter(mine, yl, c)
    to_core[1].wait_recv()
    scale_q = (D // HEADS) ** (-0.5)
    for n in range(4):
        part = slice(n * 128, (n + 1) * 128)
        to_partner[n].wait_recv()
        value = mine[part, :] + other[1, part, :] + from_y[part, :].astype(F32)
        if n < 3:
            a, b = value[:64], value[64:]
            value = jnp.concatenate([a * cos[...] - b * sin[...], b * cos[...] + a * sin[...]], axis=0)
        if n < 2:
            q_out[part, :] = (value * scale_q).astype(BF)
        else:
            for p in range(4):
                kv_out[p, (n - 2) * 128:(n - 1) * 128, :] = value[:, p * 128:(p + 1) * 128].astype(BF)
    for copy in one + two + sums + to_core + to_partner:
        copy.wait_send()
    for copy, _ in three:
        copy.wait_send()
    weights.sent()
    gather.sent()


def run_in(old_blocks, order, xt, gain, cos, sin, w_query, w_key, w_value, w_out_t):
    smem = pl.BlockSpec(memory_space=pltpu.SMEM)
    vmem = pl.BlockSpec(memory_space=pltpu.VMEM)
    hbm = pl.BlockSpec(memory_space=pltpu.HBM)
    return pl.pallas_call(
        kernel_in,
        name="project",
        out_shape=[
            jax.ShapeDtypeStruct((256, 512), BF),
            jax.ShapeDtypeStruct((4, 256, 128), BF),
            jax.ShapeDtypeStruct((1152, 1024), BF),
            jax.ShapeDtypeStruct((1152, 512), BF),
        ],
        in_specs=[smem, smem, vmem, vmem, vmem, vmem, hbm, hbm, hbm, hbm],
        out_specs=[vmem] * 4,
        scratch_shapes=[
            VM((1152, 512), BF), VM((1152, 256), BF), VM((1152, 256), BF),
            VM((8, 288, 128), BF), VM((24, 288, 128), BF), VM((1152, 1024), BF), VM((16, 8, 128), F32),
            VM((2, 512, 512), F32), VM((2, 512, 512), F32), VM((512, 512), BF), VM((512, 512), BF), VM((512, 512), F32),
            DMA((4,)), DMA((8,)), DMA((8,)), DMA((8,)), DMA((8,)), DMA((8,)), DMA((8,)),
            DMA((24,)), DMA((24,)), DMA((6,)), DMA((6,)), DMA((16,)), DMA((16,)), DMA((2,)), DMA((2,)), DMA((4,)), DMA((4,)),
        ],
        compiler_params=pltpu.CompilerParams(collective_id=0, has_side_effects=True, vmem_limit_bytes=60 * 2**20),
    )(old_blocks, order, xt, gain, cos, sin, w_query, w_key, w_value, w_out_t)


def kernel_attend(q_ref, kv_ref, ctx, kvs, qs, acc, den, s_x, r_x, s_c, r_c, s_y, r_y, s_o, r_o):
    x, yl, c, z, yh = coords()
    for p in range(4):
        kvs[kept(p, c), :, lanes(x * 128, 128)] = kv_ref[p]
    core, y_one = {"c": 1 - c}, {"yl": 1 - yl}
    greet([{"x": x + 1 - 2 * lax.rem(x, 2)}, {"x": 3 - x}, core, y_one])

    def block(n):
        return lambda chunk, half: kvs.at[kept(half * 2 + n, c), :, lanes(chunk * 128, 128)]

    gather = Gather4([block(n) for n in range(2)], "x", x, s_x, r_x)
    gather.go(0, 1, 2, 3)
    for p in range(4):
        for h in range(2):
            part = q_ref[h * 128:(h + 1) * 128, p * 128:(p + 1) * 128].astype(F32)
            qs[p, h * 128:(h + 1) * 128, :] = part.T.astype(BF)
    acc[...] = jnp.zeros_like(acc)
    den[...] = jnp.zeros_like(den)
    gather.got(0, 1)
    gather.go(4, 5)
    gather.got(2, 4, 3, 5)
    across = []
    for p in range(4):
        ref = kvs.at[kept(p, c)]
        copy = copy_to(ref, ref, s_c.at[p], r_c.at[p], core)
        copy.start()
        across.append(copy)

    def tile(p, group, masked):
        keys = kvs[group, :128, :]
        values = kvs[group, 128:, :]
        for h in range(2):
            part = slice(h * 128, (h + 1) * 128)
            score = jnp.dot(qs[p, part, :], keys, preferred_element_type=F32)
            weight = jnp.exp(50.0 * jnp.tanh(score * (1.0 / 50.0)))
            if masked:
                row = lax.broadcasted_iota(jnp.int32, (128, 512), 0) + x * 128
                col = lax.broadcasted_iota(jnp.int32, (128, 512), 1)
                weight = jnp.where(col <= row, weight, 0.0)
            den[p, part, :] += (weight[:, :128] + weight[:, 128:256]) + (weight[:, 256:384] + weight[:, 384:])
            acc[p, part, :] += lax.dot_general(
                weight.astype(BF), values, (((1,), (1,)), ((), ())), preferred_element_type=F32
            )

    def same_core(p, _):
        def earlier(e, _):
            tile(p, kept(e, c), False)
            return 0

        lax.fori_loop(0, p, earlier, 0)
        tile(p, kept(p, c), True)
        return 0

    lax.fori_loop(0, 4, same_core, 0)
    for p in range(4):
        ref = kvs.at[kept(p, 1 - c)]
        copy_to(ref, ref, s_c.at[p], r_c.at[p], core).wait_recv()

    def other_core(p, _):
        def earlier(e, _):
            tile(p, kept(e, 1 - c), False)
            return 0

        lax.fori_loop(0, p + lax.rem(p + c, 2), earlier, 0)
        return 0

    lax.fori_loop(0, 4, other_core, 0)
    for p in range(4):
        for h in range(2):
            part = slice(h * 128, (h + 1) * 128)
            total = jnp.sum(den[p, part, :], axis=1, keepdims=True)
            value = (acc[p, part, :] / total).astype(BF)
            cols = lanes(yl * 256 + h * 128, 128)
            ctx[c * 4 + p, :, cols] = value[:64]
            ctx[8 + c * 4 + p, :, cols] = value[64:]

    def region(core_at, y_at, half):
        return ctx.at[pl.ds(half * 8 + core_at * 4, 4), :, lanes(y_at * 256, 256)]

    to_y, to_core = [], []
    for half in range(2):
        ref = region(c, yl, half)
        copy = copy_to(ref, ref, s_y.at[half], r_y.at[half], y_one)
        copy.start()
        to_y.append(copy)
    for half in range(2):
        ref = region(c, yl, half)
        copy = copy_to(ref, ref, s_o.at[half], r_o.at[half], core)
        copy.start()
        to_core.append(copy)
    for half in range(2):
        ref = region(c, 1 - yl, half)
        copy_to(ref, ref, s_y.at[half], r_y.at[half], y_one).wait_recv()
        copy = copy_to(ref, ref, s_o.at[2 + half], r_o.at[2 + half], core)
        copy.start()
        to_core.append(copy)
    for n in range(4):
        ref = region(1 - c, yl if n < 2 else 1 - yl, n % 2)
        copy_to(ref, ref, s_o.at[n], r_o.at[n], core).wait_recv()
    for copy in across + to_y + to_core:
        copy.wait_send()
    gather.sent()


def run_attend(q, kv):
    vmem = pl.BlockSpec(memory_space=pltpu.VMEM)
    return pl.pallas_call(
        kernel_attend,
        name="attend",
        out_shape=jax.ShapeDtypeStruct((16, 64, 512), BF),
        in_specs=[vmem, vmem],
        out_specs=vmem,
        scratch_shapes=[
            VM((8, 256, 512), BF), VM((4, 256, 128), BF), VM((4, 256, 128), F32), VM((4, 256, 128), F32),
            DMA((12,)), DMA((12,)), DMA((4,)), DMA((4,)), DMA((2,)), DMA((2,)), DMA((4,)), DMA((4,)),
        ],
        compiler_params=pltpu.CompilerParams(collective_id=1, has_side_effects=True, vmem_limit_bytes=40 * 2**20),
    )(q, kv)


def kernel_out(
    new_ref, ctx, xs, wo, gain, fin,
    send_a, send_b, got_a, got_b, more_a, more_b, more_got_a, more_got_b, total, half_out, relay, half_in,
    squares, fresh, f1, f1_got, f2,
    s_1, r_1, s_2, r_2, s_y, r_y, s_q, r_q, s_f, r_f, s_g, r_g, s_c, r_c,
):
    x, yl, c, z, yh = coords()
    core = {"c": 1 - c}
    y_one, y_two = {"yl": 1 - yl}, {"yl": 1 - yl, "yh": 1 - yh}
    group = [
        {"z": lax.rem(z + dz, 4), "yl": yl + dy - 2 * yl * dy, "c": c + dc - 2 * c * dc}
        for dz in range(4) for dy in range(2) for dc in range(2)
    ][1:]
    others = [{"x": lax.rem(x + dx, 4)} for dx in range(1, 4)]
    greet(group + others + [y_two])
    one, two = z + 1 - 2 * lax.rem(z, 2), 3 - z
    far = two + 1 - 2 * lax.rem(two, 2)

    def piece(chunk, half):
        left = wo[pl.ds(pl.multiple_of(chunk * 288, 16), 288), :]
        right = ctx[half * 8:(half + 1) * 8].reshape(512, 512)
        return lax.dot_general(left, right, (((1,), (1,)), ((), ())), preferred_element_type=F32)

    first = []
    send_a[1] = piece(far, 0).astype(BF)
    send_b[1] = piece(far, 1).astype(BF)
    for n, (src, dst, peer) in enumerate(((send_a, got_a, one), (send_b, got_b, two))):
        first.append(copy_to(src.at[1], dst.at[1], s_1.at[n], r_1.at[n], {"z": peer}))
        first[-1].start()
    send_a[0] = piece(one, 0).astype(BF)
    send_b[0] = piece(two, 1).astype(BF)
    for n, (src, dst, peer) in enumerate(((send_a, got_a, one), (send_b, got_b, two))):
        first.append(copy_to(src.at[0], dst.at[0], s_1.at[2 + n], r_1.at[2 + n], {"z": peer}))
        first[-1].start()
    total[0] = piece(two, 0)
    total[1] = piece(one, 1)
    second = []
    for n, (src, got, dst, peer) in enumerate(
        ((more_a, got_a, more_got_a, two), (more_b, got_b, more_got_b, one))
    ):
        first[n].wait_recv()
        src[...] = (total[n] + got[1].astype(F32)).astype(BF)
        second.append(copy_to(src, dst, s_2.at[n], r_2.at[n], {"z": peer}))
        second[-1].start()
    total[0] = piece(z, 0)
    total[1] = piece(z, 1)
    for n, got in enumerate((got_a, got_b)):
        first[2 + n].wait_recv()
        total[n] = total[n] + got[0].astype(F32)
    for n, got in enumerate((more_got_a, more_got_b)):
        second[n].wait_recv()
        total[n] = total[n] + got[...].astype(F32)
    half_out[...] = total[1 - yh].astype(BF)
    hop = []
    for n, peer in enumerate((y_one, y_two)):
        part = slice(n * 144, (n + 1) * 144)
        hop.append(copy_to(half_out.at[part], relay.at[part], s_y.at[n], r_y.at[n], peer))
        hop[-1].start()
    for n, peer in enumerate((y_two, y_one)):
        part = slice(n * 144, (n + 1) * 144)
        hop[n].wait_recv()
        hop.append(copy_to(relay.at[part], half_in.at[part], s_y.at[2 + n], r_y.at[2 + n], peer))
        hop[-1].start()
    for n in range(2):
        hop[2 + n].wait_recv()
    me = z * 4 + yl * 2 + c
    for m in range(4):
        cols = slice(m * 128, (m + 1) * 128)
        value = total[yh, :, cols] + half_in[:, cols].astype(F32)
        total[yh, :, cols] = value
        squares[me, m:m + 1, :] = jnp.sum(value * value, axis=0, keepdims=True)
    sums = []
    for e, peer in enumerate(group, 1):
        copy = copy_to(squares.at[me], squares.at[me], s_q.at[e], r_q.at[e], peer)
        copy.start()
        sums.append(copy)
    low = lax.broadcasted_iota(jnp.int32, (288, 128), 1) < 64

    def pair(m):
        at = pl.ds(pl.multiple_of(z * 288, 16), 288)
        a = xs[at, m * 256:m * 256 + 128].astype(F32)
        b = xs[at, m * 256 + 128:m * 256 + 256].astype(F32)
        upper, lower = pltpu.roll(a, 64, 1), pltpu.roll(b, 64, 1)
        return jnp.where(low, jnp.where(yh == 0, a, upper), jnp.where(yh == 0, lower, b))

    for copy in sums:
        copy.wait_recv()
    factor = lax.rsqrt(jnp.sum(squares[...], axis=0) * (1.0 / D) + EPS)
    for m in range(4):
        fresh[m] = pair(m) + total[yh, :, m * 128:(m + 1) * 128] * factor[m:m + 1, :] * gain[...]
    starts, so_far = [], 0
    for j in range(16):
        starts.append(so_far)
        so_far = so_far + new_ref[j]
    for n in range(8):
        sides = []
        for side in range(2):
            j = 2 * n + side
            within = lax.rem(x - starts[j] + 64, 4)
            i = jnp.minimum(lax.div(starts[j] + within - x, 4), 7)
            at = lax.div(i, 2)
            place = lax.rem(i + at, 2) * 4 + at
            value = fresh[lax.div(place, 2)]
            value = jnp.where(lax.rem(place, 2) == side, value, pltpu.roll(value, 64, 1))
            sides.append(jnp.where(within < new_ref[j], value, 0.0))
        f1[n] = jnp.where(low, sides[0], sides[1]).astype(BF)
    here = pl.ds(x * 2, 2)
    f1_got[here] = f1[here]
    over_x = []
    for d, peer in enumerate(others):
        copy = copy_to(f1.at[pl.ds(peer["x"] * 2, 2)], f1_got.at[here], s_f.at[d], r_f.at[d], peer)
        copy.start()
        over_x.append(copy)
    mine = [sum([jnp.where(x * 4 + n > m, new_ref[m], 0) for m in range(15)]) for n in range(4)]
    for copy in over_x:
        copy.wait_recv()
    out = []
    for e in range(8):
        dz, dy = e // 2, e % 2
        tz, ty = lax.rem(z + dz, 4), yl + dy - 2 * yl * dy
        sides = []
        for side in range(2):
            start = jnp.where(ty == 0, mine[side], mine[2 + side])
            sides.append(f1_got[lax.rem(start + tz, 4) * 2 + ty].astype(F32))
        value = jnp.where(low, sides[0], sides[1]).astype(BF)
        at = (z * 2 + yl) * 2 + c
        if e == 0:
            fin[at] = value
        else:
            f2[e] = value
            copy = copy_to(f2.at[e], fin.at[at], s_g.at[e], r_g.at[e], {"z": tz, "yl": ty})
            copy.start()
            out.append(copy)
    swap = []
    for e in range(8):
        dz, dy = e // 2, e % 2
        at = (mod4(z - dz) * 2 + yl + dy - 2 * yl * dy) * 2 + c
        if e > 0:
            copy_to(fin.at[at], fin.at[at], s_g.at[e], r_g.at[e], core).wait_recv()
        copy = copy_to(fin.at[at], fin.at[at], s_c.at[e], r_c.at[e], core)
        copy.start()
        swap.append(copy)
    for copy in swap:
        copy.wait_recv()
    for copy in first + second + hop + sums + over_x + out + swap:
        copy.wait_send()


def run_out(new_blocks, ctx, xs, wo, gain):
    smem = pl.BlockSpec(memory_space=pltpu.SMEM)
    vmem = pl.BlockSpec(memory_space=pltpu.VMEM)
    return pl.pallas_call(
        kernel_out,
        name="finish",
        out_shape=jax.ShapeDtypeStruct((16, 288, 128), BF),
        in_specs=[smem, vmem, vmem, vmem, vmem],
        out_specs=vmem,
        scratch_shapes=[VM((2, 288, 512), BF)] * 4
        + [VM((288, 512), BF)] * 4
        + [VM((2, 288, 512), F32), VM((288, 512), BF), VM((288, 512), BF), VM((288, 512), BF)]
        + [VM((16, 4, 128), F32), VM((4, 288, 128), F32), VM((8, 288, 128), BF), VM((8, 288, 128), BF)]
        + [VM((8, 288, 128), BF)]
        + [DMA((4,)), DMA((4,)), DMA((2,)), DMA((2,)), DMA((4,)), DMA((4,)), DMA((16,)), DMA((16,))]
        + [DMA((3,)), DMA((3,)), DMA((8,)), DMA((8,)), DMA((8,)), DMA((8,))],
        compiler_params=pltpu.CompilerParams(collective_id=2, has_side_effects=True, vmem_limit_bytes=56 * 2**20),
    )(new_blocks, ctx, xs, wo, gain)


def per_device(
    x_old, old_blocks, new_blocks, order, pre_gain, post_gain, w_query, w_key, w_value, w_out_t
):
    x, yl, c, z, yh = coords()
    gain = pre_gain.reshape(4, 2, 2, 288)[:, yl, c].reshape(1152, 1)
    gain = jnp.broadcast_to(gain, (1152, 128))
    gain_out = jnp.broadcast_to(post_gain.reshape(16, 288)[z * 4 + yl * 2 + c][:, None], (288, 128))
    half = HEAD // 2
    inverse = jnp.exp(jnp.arange(half, dtype=F32) * (-2.0 * math.log(10000.0) / HEAD))
    at = jnp.arange(512, dtype=jnp.int32)
    place = at // 128
    block = 2 * place + (place + c) % 2
    positions = (x + 4 * block) * BLOCK + at % 128
    angles = inverse[:, None] * positions.astype(F32)[None, :]
    q, kv, xs, wo = run_in(
        old_blocks, order, x_old.T, gain, jnp.cos(angles), jnp.sin(angles), w_query, w_key, w_value, w_out_t
    )
    ctx = run_attend(q, kv)
    fin = run_out(new_blocks, ctx, xs, wo, gain_out)
    return lax.dynamic_slice(fin, (0, 0, c * 64), (16, 288, 64)).reshape(4608, 64).T


def solution(mesh):
    torus = Mesh(mesh.devices.reshape(4, 2, 2, 4, 2), ("x", "yl", "c", "z", "yh"))
    seq, tp = ("x", "yl", "c"), ("z", "yh")
    both = P(seq, tp)
    in_specs = (both, P(), P(), P(), P(), P(), both, both, both, both)
    return jax.shard_map(
        per_device, mesh=torus, in_specs=in_specs, out_specs=P(seq + tp, None), check_vma=False
    )
```

time: 494 us -> 180 us (0.36)
  waiting for transfers between devices: 319 us -> 0 us
  Pallas kernels: 0 us -> 169 us
  matrix products: 77.3 us -> 0 us
  other arithmetic: 37.9 us -> 1.25 us
  local copies, waits for them, and re-layouts: 44 us -> 9.41 us
  between operations: 13.8 us -> 0.06 us
    all_gather x4 -> x0, waiting for transfers between devices: 247 us -> none  [the longest x2 115 us: in_one_piece(): whole = lax.all_gather(both, axis, axis=dim, tiled=True)]
    pallas_call x0 -> x3, Pallas kernels: none -> 169 us  [the longest x1 76 us: run_in(): pl.pallas_call(kernel_in, name='project', out_shape=[jax.ShapeDtypeStruct...]
    dot_general x36 -> x0, matrix products: 77.3 us -> none  [the longest x16 28.1 us: one_block(): jnp.einsum('qcgd,kcd->cgqk', query_four, key_block, preferred_element_typ...]
    reduce_scatter x2 -> x0, waiting for transfers between devices: 71.6 us -> none  [sum_by_axis(): so_far = lax.psum_scatter(so_far, axis, scatter_dimension=0, tiled=True)]
    dynamic_slice x18 -> x3, local copies, waits for them, and re-layouts: 18.4 us -> 1.73 us  [the longest x1 1.67 us: per_device(): lax.dynamic_slice(fin, (0, 0, c * 64), (16, 288, 64)).reshape(4608, 64)]
    convert_element_type x4 -> x1, other arithmetic: 10.2 us -> 0.02 us  [per_device(): angles = inverse[:, None] * positions.astype(F32)[None, :]]
    add x33 -> x0, other arithmetic: 10.1 us -> none  [the longest x17 9.9 us: per_device(): wanted = my_start + slot_ids]
    gather x1 -> x0, local copies, waits for them, and re-layouts: 7.46 us -> none  [per_device(): gathered[source]]
  transfers between devices with their start and end apart: 6 -> 0, of which waited for: 6 -> 0; matrix products, arithmetic and copies ran while one was open for 7% -> 0% of each run, Pallas kernels for 0% -> 0%
where the time goes in v1:
time: 180 us
  Pallas kernels  169 us (94%)
  local copies, waits for them, and re-layouts  9.41 us (5%)
    pallas_call x1, Pallas kernels, run_in(): pl.pallas_call(kernel_in, name='project', out_shape=[jax.ShapeDtypeStruct...  76 us
    pallas_call x1, Pallas kernels, run_out(): pl.pallas_call(kernel_out, name='finish', out_shape=jax.ShapeDtypeStruct(...  64.1 us
    pallas_call x1, Pallas kernels, run_attend(): pl.pallas_call(kernel_attend, name='attend', out_shape=jax.ShapeDtypeStru...  29.1 us

profile of v1, /device:TPU:1, one launch (start us, length us, event | category | flops | bytes accessed | tf_op | source)
XLA Modules:
  0.0 179.9 jit_solution(559607082086781690)
XLA Ops:
  0.0 0.8 reshape.55
  0.9 0.1 broadcast_in_dim.16
  1.0 0.8 reshape.56
  1.8 0.8 broadcast_in_dim.19.gain
  2.6 1.2 multiply_sine_fusion
  3.8 1.0 broadcast_in_dim.17.gain
  4.8 76.0 %project.1 = (bf16[256,512]{1,0:T(8,128)(2,1)}, bf16[4,256,128]{2,1,0:T(8,128)(2,1)}, bf16[1152,1024]{1,0:T(8,128)(2,1)}, bf16[1152,512]{1,0:T(8,128)(2,1)}) custom-call(s32[16]{0:T(128)} %old_ref.1, s32[16]{0:T(128)} %order_ref.1, bf16[576,512]{1,0:T(8,128)(2,1)} %bitcast.4, f32[1152,128]{1,0:T(8,128)} %broadcast_in_dim.17.gain, ...), custom_call_target="tpu_custom_call" | custom-call | tf_op jit(solution)/shard_map/project/pallas_call | solution.py:259
  80.8 0.0 copy-start.1
  80.8 0.9 copy-done.1
  81.7 0.0 copy-start.2
  81.7 0.9 copy-done.2
  82.7 29.1 %attend.1.ctx = bf16[16,64,512]{2,1,0:T(8,128)(2,1)S(1)} custom-call(bf16[256,512]{1,0:T(8,128)(2,1)S(1)} %copy-done.1, bf16[4,256,128]{2,1,0:T(8,128)(2,1)S(1)} %copy-done.2), custom_call_target="tpu_custom_call" | custom-call | tf_op jit(solution)/shard_map/attend/pallas_call | solution.py:387
  111.8 0.0 copy-start
  111.8 1.0 copy-done
  112.9 64.1 %finish.1 = bf16[16,288,128]{2,1,0:T(8,128)(2,1)} custom-call(s32[16]{0:T(128)} %new_ref.1, bf16[16,64,512]{2,1,0:T(8,128)(2,1)} %copy-done, bf16[1152,1024]{1,0:T(8,128)(2,1)} %get-tuple-element.11.xs, bf16[1152,512]{1,0:T(8,128)(2,1)} %get-tuple-element.12.wo, f32[288,128]{1,0:T(8,128)} %broadcast_in_dim.19.gain), custom_call_target="tpu_custom_call" | custom-call | tf_op jit(solution)/shard_map/finish/pallas_call | solution.py:552
  177.0 1.7 constant_dynamic-slice_fusion
  178.7 1.3 copy.12
  (4 shorter events, 0.1 us)
Async XLA Ops:
  80.8 1.0 copy-start.1
  81.7 0.9 copy-start.2
  111.8 1.0 copy-start

commit v2 on v1

v2 whole, which is shorter than its diff:
```python
import functools
import math

import jax
import jax.numpy as jnp
from jax import lax
from jax.experimental import pallas as pl
from jax.experimental.pallas import tpu as pltpu
from jax.sharding import Mesh
from jax.sharding import PartitionSpec as P

D = 4608
HEADS = 32
HEAD = 128
BLOCK = 128
EPS = 1e-06
BF = jnp.bfloat16
F32 = jnp.float32
VM = pltpu.VMEM
DMA = pltpu.SemaphoreType.DMA


def kept(at, c):
    return 2 * at + lax.rem(at + c, 2)


def coords():
    return tuple(lax.axis_index(name) for name in ("x", "yl", "c", "z", "yh"))


def copy_to(src, dst, send_sem, recv_sem, device):
    return pltpu.make_async_remote_copy(
        src_ref=src,
        dst_ref=dst,
        send_sem=send_sem,
        recv_sem=recv_sem,
        device_id=device,
        device_id_type=pl.DeviceIdType.MESH,
    )


def greet(devices):
    sem = pltpu.get_barrier_semaphore()
    for device in devices:
        pl.semaphore_signal(sem, inc=1, device_id=device, device_id_type=pl.DeviceIdType.MESH)
    pl.semaphore_wait(sem, len(devices))


def mod4(v):
    return lax.rem(v + 4, 4)


class Gather4:
    def __init__(self, views, axis, me, send, recv):
        one, two = me + 1 - 2 * lax.rem(me, 2), 3 - me
        far = two + 1 - 2 * lax.rem(two, 2)
        self.moves = [
            (me, one, 0, one),
            (me, two, 1, two),
            (me, two, 0, two),
            (me, one, 1, one),
            (one, far, 0, two),
            (two, far, 1, one),
        ]
        self.views, self.axis, self.send, self.recv = views, axis, send, recv

    def each(self, move, got):
        sent, received, half, partner = self.moves[move]
        for n, view in enumerate(self.views):
            ref = view(received if got else sent, half)
            at = n * 6 + move
            yield copy_to(ref, ref, self.send.at[at], self.recv.at[at], {self.axis: partner})

    def go(self, *moves):
        for move in moves:
            for copy in self.each(move, False):
                copy.start()

    def got(self, *moves):
        for move in moves:
            for copy in self.each(move, True):
                copy.wait_recv()

    def sent(self):
        for move in range(6):
            for copy in self.each(move, False):
                copy.wait_send()


def rows(ref, start, size, unit=16):
    return ref.at[pl.ds(pl.multiple_of(start, unit), size)]


def lanes(start, size):
    return pl.ds(pl.multiple_of(start, 128), size)


def columns(dst, table, chunk_of, count):
    lane = lax.broadcasted_iota(jnp.int32, (32, 128), 1)

    def body(n, _):
        feature = chunk_of(lax.div(n, 9)) * 288 + lax.rem(n, 9) * 32
        part = table[pl.ds(pl.multiple_of(lax.rem(feature, 128), 32), 32), :]
        value = jnp.sum(jnp.where(lane == lax.div(feature, 128), part, 0.0), axis=1, keepdims=True)
        dst[pl.ds(pl.multiple_of(n * 32, 32), 32), :] = jnp.broadcast_to(value, (32, 128))
        return 0

    lax.fori_loop(0, count * 9, body, 0)


def stage_in(
    old_ref, order_ref, xt, pre_ref, post_ref, wq_in, wk_in, wv_in, wo_in,
    q_out, kv_out, xs, wo, gain_out,
    wq, wk, wv, gain, table, cos, sin, slots, landed_0, landed_1, normed, squares, near, other, to_y, from_y, mine,
    s_w, s_one, r_one, s_two, r_two, s_three, r_three, s_wg, r_wg, s_og, r_og, s_z, r_z, s_q, r_q, s_c, r_c, s_y, r_y,
    send_kv,
):
    x, yl, c, z, yh = coords()
    landed = (landed_0, landed_1)
    at = pl.ds(pl.multiple_of(x * 288, 16), 288)
    owns = [
        pltpu.make_async_copy(src, dst.at[at], s_w.at[n])
        for n, (src, dst) in enumerate(((wq_in, wq), (wk_in, wk), (wv_in, wv), (wo_in, wo)))
    ]
    for copy in owns:
        copy.start()
    starts, total = [], 0
    for m in range(16):
        starts.append(total)
        total = total + old_ref[m]
    k = order_ref[x * 4 + yl * 2 + c]
    first = sum([jnp.where(k > m, old_ref[m], 0) for m in range(15)])
    for r in range(4):
        b = lax.rem(r - first + 64, 4)
        for h in range(2):
            for half in range(2):
                at_rows = slice(h * 288 + half * 144, h * 288 + half * 144 + 144)
                part = [xt[at_rows, n * 128:(n + 1) * 128] for n in range(4)]
                low = jnp.where(b == 0, part[0], part[1])
                slots[half, r * 2 + h] = jnp.where(b < 2, low, jnp.where(b == 2, part[2], part[3]))
    here = x * 2 + c
    for half in range(2):
        landed[half][here] = slots[half, here]
    ring_peers = [
        {"x": lax.rem(x + dx, 4), "c": c + dc - 2 * c * dc} for dx in range(4) for dc in range(2)
    ][1:]
    y_one = {"yl": 1 - yl}
    y_two = {"yl": 1 - yl, "yh": 1 - yh}
    group = [
        {"z": lax.rem(z + dz, 4), "yl": yl + dy - 2 * yl * dy, "c": c + dc - 2 * c * dc}
        for dz in range(4) for dy in range(2) for dc in range(2)
    ][1:]
    greet(ring_peers + [y_two] + group)
    one, two, three = [], [], []
    for half in range(2):
        for d, peer in enumerate(ring_peers, 1):
            n = half * 8 + d
            copy = copy_to(
                slots.at[half, peer["x"] * 2 + peer["c"]], landed[half].at[here], s_one.at[n], r_one.at[n], peer
            )
            copy.start()
            one.append(copy)
    for copy in owns:
        copy.wait()

    def half_rows(ref):
        return lambda chunk, half: rows(ref, chunk * 288 + half * 144, 144)

    weights = Gather4([half_rows(r) for r in (wq, wk, wv)], "x", x, s_wg, r_wg)
    weights.go(0, 1, 2, 3)
    straight = yl == yh
    for half in range(2):
        for d in range(8):
            n = half * 8 + d
            dx, dc = d // 2, d % 2
            slot = mod4(x - dx) * 2 + c + dc - 2 * c * dc
            if d > 0:
                copy_to(slots.at[half, slot], landed[half].at[slot], s_one.at[n], r_one.at[n], y_one).wait_recv()
            copy = copy_to(landed[half].at[slot], landed[half].at[8 + slot], s_two.at[n], r_two.at[n], y_two)
            copy.start()
            two.append(copy)
            copy = copy_to(landed[half].at[slot], landed[half].at[16 + slot], s_three.at[n], r_three.at[n], y_one)
            relay = copy_to(landed[half].at[8 + slot], landed[half].at[16 + slot], s_three.at[n], r_three.at[n], y_one)
            three.append((copy, relay))
            pl.when(jnp.logical_not(straight))(copy.start)
            if half == 1:
                two[d].wait_recv()
                pl.when(straight)(three[d][1].start)
    for n in range(8, 16):
        two[n].wait_recv()
        pl.when(straight)(three[n][1].start)
    weights.got(0, 1)
    weights.go(4, 5)
    wo_all = Gather4([half_rows(wo)], "x", x, s_og, r_og)
    wo_all.go(0, 1, 2, 3)
    me = z * 4 + yl * 2 + c
    first_buffer = jnp.where(straight, 0, 1)
    gather = Gather4([half_rows(xs)], "z", z, s_z, r_z)
    sources = []
    for place in range(8):
        g = x + 4 * kept(place % 4, place // 4)
        shard = sum([jnp.where(starts[m] <= g, 1, 0) for m in range(16)]) - 1
        holder = sum([jnp.where(order_ref[p] == shard, p, 0) for p in range(16)])
        y_source = lax.rem(lax.div(holder, 2), 2)
        sources.append(jnp.where(y_source == yh, first_buffer, 2) * 8 + lax.div(holder, 4) * 2 + lax.rem(holder, 2))
    for half in range(2):
        for n in range(half * 8, half * 8 + 8):
            three[n][0].wait_recv()
        for place in range(8):
            block = landed[half][sources[place]]
            xs[pl.ds(pl.multiple_of(z * 288 + half * 144, 16), 144), place * 128:(place + 1) * 128] = block
            wide = block.astype(F32)
            square = jnp.sum(wide * wide, axis=0, keepdims=True)
            if half == 1:
                square = square + squares[me, place:place + 1, :]
            squares[me, place:place + 1, :] = square
        if half == 0:
            gather.go(0, 2)
        else:
            gather.go(1, 3)
    sums = []
    for e, peer in enumerate(group, 1):
        copy = copy_to(squares.at[me], squares.at[me], s_q.at[e], r_q.at[e], peer)
        copy.start()
        sums.append(copy)
    table[...] = jnp.zeros_like(table)
    table[0:36, :] = pre_ref[...]
    table[...] = table[...].T
    columns(gain, table, lambda n: n * 4 + yl * 2 + c, 4)
    table[...] = jnp.zeros_like(table)
    table[0:36, :] = post_ref[...]
    table[...] = table[...].T
    columns(gain_out, table, lambda n: z * 4 + yl * 2 + c, 1)
    half_head = HEAD // 2
    inverse = jnp.exp(
        lax.broadcasted_iota(jnp.int32, (half_head, 128), 0).astype(F32) * (-2.0 * math.log(10000.0) / HEAD)
    )
    for p in range(4):
        place_of = (x + 4 * kept(p, c)) * BLOCK + lax.broadcasted_iota(jnp.int32, (half_head, 128), 1)
        angle = inverse * place_of.astype(F32)
        cos[:, p * 128:(p + 1) * 128] = jnp.cos(angle)
        sin[:, p * 128:(p + 1) * 128] = jnp.sin(angle)
    gather.got(0)
    gather.go(4)
    gather.got(1)
    gather.go(5)
    for copy in sums:
        copy.wait_recv()
    factor = lax.rsqrt(jnp.sum(squares[...], axis=0) * (1.0 / D) + EPS)

    def norm(chunk):
        for place in range(8):
            scale = factor[place:place + 1, :]

            def norm_rows(n, _, place=place, scale=scale):
                part = pl.ds(pl.multiple_of(chunk * 288 + n * 144, 16), 144)
                at = (part, slice(place * 128, (place + 1) * 128))
                normed[at] = (xs[at].astype(F32) * scale * gain[part, :]).astype(BF)
                return 0

            lax.fori_loop(0, 2, norm_rows, 0)

    def quarter(dst, y, core, late):
        low = lax.div(z, 2)
        part = pl.ds(pl.multiple_of((1 - low if late else low) * 576, 16), 576)
        right = normed[part, lanes(core * 512, 512)]

        def dot(left):
            return lax.dot_general(left, right, (((0,), (0,)), ((), ())), preferred_element_type=F32)

        for to, left in (
            (slice(0, 256), wq[part, lanes(y * 256, 256)]),
            (slice(256, 384), wk[part, lanes(y * 128, 128)]),
            (slice(384, 512), wv[part, lanes(y * 128, 128)]),
        ):
            if late:
                dst[to, :] += dot(left)
            else:
                dst[to, :] = dot(left)

    norm(z)
    gather.got(3)
    norm(z + 1 - 2 * lax.rem(z, 2))
    weights.got(2, 3, 4, 5)
    corners = [
        (near.at[0], 1 - yl, 1 - c), (mine.at[0], 1 - yl, c), (near.at[1], yl, 1 - c), (mine.at[1], yl, c),
    ]
    for dst, y, core in corners:
        quarter(dst, y, core, False)
    gather.got(2)
    norm(3 - z)
    wo_all.got(0, 1)
    wo_all.go(4, 5)
    gather.got(4, 5)
    far = 3 - z
    norm(far + 1 - 2 * lax.rem(far, 2))
    core = {"c": 1 - c}
    to_core = [copy_to(near.at[n], other.at[n], s_c.at[n], r_c.at[n], core) for n in range(2)]
    quarter(*corners[0], True)
    to_core[0].start()
    quarter(*corners[1], True)
    to_core[0].wait_recv()
    to_partner = {}
    for n in (2, 3, 0, 1):
        part = slice(n * 128, (n + 1) * 128)
        to_y[part, :] = (mine[0, part, :] + other[0, part, :]).astype(BF)
        copy = copy_to(to_y.at[part], from_y.at[part], s_y.at[n], r_y.at[n], y_one)
        to_partner[n] = copy
        copy.start()
    quarter(*corners[2], True)
    to_core[1].start()
    quarter(*corners[3], True)
    to_core[1].wait_recv()
    scale_q = (D // HEADS) ** (-0.5)
    for n in (2, 3, 0, 1):
        part = slice(n * 128, (n + 1) * 128)
        to_partner[n].wait_recv()
        value = mine[1, part, :] + other[1, part, :] + from_y[part, :].astype(F32)
        if n < 3:
            a, b = value[:64], value[64:]
            value = jnp.concatenate([a * cos[...] - b * sin[...], b * cos[...] + a * sin[...]], axis=0)
        if n < 2:
            q_out[part, :] = (value * scale_q).astype(BF)
        else:
            for p in range(4):
                kv_out[p, (n - 2) * 128:(n - 1) * 128, :] = value[:, p * 128:(p + 1) * 128].astype(BF)
        if n == 3:
            send_kv()

    def finish():
        wo_all.got(2, 3, 4, 5)
        for copy in one + two + sums + to_core + list(to_partner.values()):
            copy.wait_send()
        for copy, _ in three:
            copy.wait_send()
        weights.sent()
        wo_all.sent()
        gather.sent()

    return finish


class KeysValues:
    def __init__(self, kv_ref, kvs, s_x, r_x, s_c, r_c):
        x, _, c, _, _ = coords()

        def block(n):
            return lambda chunk, half: kvs.at[kept(half * 2 + n, c), :, lanes(chunk * 128, 128)]

        self.gather = Gather4([block(n) for n in range(2)], "x", x, s_x, r_x)
        self.kv_ref, self.kvs, self.s_c, self.r_c = kv_ref, kvs, s_c, r_c
        self.across = []

    def send(self):
        x, _, c, _, _ = coords()
        for p in range(4):
            self.kvs[kept(p, c), :, lanes(x * 128, 128)] = self.kv_ref[p]
        self.gather.go(0, 1, 2, 3)

    def core_copies(self, late, mine):
        x, _, c, _, _ = coords()
        low = lax.div(x, 2)
        cols = lanes((1 - low if late else low) * 256, 256)
        for p in range(4):
            ref = self.kvs.at[kept(p, c if mine else 1 - c), :, cols]
            n = p + 4 * late
            yield copy_to(ref, ref, self.s_c.at[n], self.r_c.at[n], {"c": 1 - c})

    def to_core(self, late):
        for copy in self.core_copies(late, True):
            copy.start()
            self.across.append(copy)

    def from_core(self):
        for late in (0, 1):
            for copy in self.core_copies(late, False):
                copy.wait_recv()


def stage_attend(q_ref, ctx, keys_values, kvs, qs, acc, den, s_y, r_y, s_o, r_o):
    x, yl, c, z, yh = coords()
    core, y_one = {"c": 1 - c}, {"yl": 1 - yl}
    gather = keys_values.gather
    for p in range(4):
        for h in range(2):
            part = q_ref[h * 128:(h + 1) * 128, p * 128:(p + 1) * 128].astype(F32)
            qs[p, h * 128:(h + 1) * 128, :] = part.T.astype(BF)
    acc[...] = jnp.zeros_like(acc)
    den[...] = jnp.zeros_like(den)
    gather.got(0)
    gather.go(4)
    gather.got(1)
    gather.go(5)
    gather.got(3)
    keys_values.to_core(0)

    def tile(p, group, masked, start, width):
        cols = lanes(start, width)
        for h in range(2):
            part = slice(h * 128, (h + 1) * 128)
            score = jnp.dot(qs[p, part, :], kvs[group, :128, cols], preferred_element_type=F32)
            weight = jnp.exp(50.0 * jnp.tanh(score * (1.0 / 50.0)))
            if masked:
                row = lax.broadcasted_iota(jnp.int32, (128, width), 0) + x * 128
                col = lax.broadcasted_iota(jnp.int32, (128, width), 1) + start
                weight = jnp.where(col <= row, weight, 0.0)
            den[p, part, :] += sum([weight[:, n:n + 128] for n in range(0, width, 128)])
            acc[p, part, :] += lax.dot_general(
                weight.astype(BF), kvs[group, 128:, cols], (((1,), (1,)), ((), ())), preferred_element_type=F32
            )

    def same_core(start):
        def place(p, _):
            def earlier(e, _):
                tile(p, kept(e, c), False, start, 256)
                return 0

            lax.fori_loop(0, p, earlier, 0)
            tile(p, kept(p, c), True, start, 256)
            return 0

        lax.fori_loop(0, 4, place, 0)

    low = lax.div(x, 2)
    same_core(low * 256)
    gather.got(2, 4, 5)
    keys_values.to_core(1)
    same_core(256 - low * 256)
    keys_values.from_core()
    def region(core_at, y_at, at, size):
        return ctx.at[pl.ds(at + core_at * 4, size), :, lanes(y_at * 256, 256)]

    to_y, to_core = [], []
    for p in range(4):

        def earlier(e, _, p=p):
            tile(p, kept(e, 1 - c), False, 0, 512)
            return 0

        lax.fori_loop(0, p + lax.rem(p + c, 2), earlier, 0)
        for h in range(2):
            part = slice(h * 128, (h + 1) * 128)
            total = jnp.sum(den[p, part, :], axis=1, keepdims=True)
            value = (acc[p, part, :] / total).astype(BF)
            cols = lanes(yl * 256 + h * 128, 128)
            ctx[c * 4 + p, :, cols] = value[:64]
            ctx[8 + c * 4 + p, :, cols] = value[64:]
        for half in range(2):
            ref = region(c, yl, half * 8 + p, 1)
            copy = copy_to(ref, ref, s_y.at[half * 4 + p], r_y.at[half * 4 + p], y_one)
            copy.start()
            to_y.append(copy)
    for half in range(2):
        ref = region(c, yl, half * 8, 4)
        copy = copy_to(ref, ref, s_o.at[half], r_o.at[half], core)
        copy.start()
        to_core.append(copy)
    for half in range(2):
        for p in range(4):
            ref = region(c, 1 - yl, half * 8 + p, 1)
            copy_to(ref, ref, s_y.at[half * 4 + p], r_y.at[half * 4 + p], y_one).wait_recv()
        ref = region(c, 1 - yl, half * 8, 4)
        copy = copy_to(ref, ref, s_o.at[2 + half], r_o.at[2 + half], core)
        copy.start()
        to_core.append(copy)
    for n in range(4):
        ref = region(1 - c, yl if n < 2 else 1 - yl, (n % 2) * 8, 4)
        copy_to(ref, ref, s_o.at[n], r_o.at[n], core).wait_recv()

    def finish():
        for copy in keys_values.across + to_y + to_core:
            copy.wait_send()
        gather.sent()

    return finish


class Reduce4:
    def __init__(self, z, send, got, more, more_got, s_1, r_1, s_2, r_2):
        self.one, self.two = z + 1 - 2 * lax.rem(z, 2), 3 - z
        self.far = self.two + 1 - 2 * lax.rem(self.two, 2)
        self.send, self.got, self.more, self.more_got = send, got, more, more_got
        self.sems = (s_1, r_1, s_2, r_2)
        self.first, self.second = {}, []

    def partner(self, part, step):
        return {"z": self.one if part == step else self.two}

    def chunk(self, part, slot):
        return self.far if slot == 1 else (self.two if part else self.one)

    def give(self, part, slot, value):
        self.send[part, slot] = value
        n = part * 2 + slot
        copy = copy_to(
            self.send.at[part, slot], self.got.at[part, slot], self.sems[0].at[n], self.sems[1].at[n], self.partner(part, 0)
        )
        copy.start()
        self.first[part, slot] = copy

    def pass_on(self, part, value):
        self.first[part, 1].wait_recv()
        self.more[part] = (value + self.got[part, 1].astype(F32)).astype(BF)
        copy = copy_to(
            self.more.at[part], self.more_got.at[part], self.sems[2].at[part], self.sems[3].at[part], self.partner(part, 1)
        )
        copy.start()
        self.second.append(copy)

    def own(self, part, value):
        self.first[part, 0].wait_recv()
        value = value + self.got[part, 0].astype(F32)
        self.second[part].wait_recv()
        return value + self.more_got[part].astype(F32)

    def sent(self):
        for copy in list(self.first.values()) + self.second:
            copy.wait_send()


def stage_out(
    new_ref, ctx, xs, wo, gain, fin,
    a_send, a_got, a_more, a_more_got, b_send, b_got, b_more, b_more_got,
    y_send, y_relay, y_got, h_send, h_relay, h_got, own_a, own_b, total,
    squares, fresh, f1, f2, f1_got_0, f1_got_1,
    a_s1, a_r1, a_s2, a_r2, b_s1, b_r1, b_s2, b_r2, s_y, r_y, s_h, r_h, s_q, r_q, s_f, r_f, s_g, r_g, s_c, r_c,
):
    x, yl, c, z, yh = coords()
    core = {"c": 1 - c}
    y_one, y_two = {"yl": 1 - yl}, {"yl": 1 - yl, "yh": 1 - yh}
    group = [
        {"z": lax.rem(z + dz, 4), "yl": yl + dy - 2 * yl * dy, "c": c + dc - 2 * c * dc}
        for dz in range(4) for dy in range(2) for dc in range(2)
    ][1:]
    others = [{"x": lax.rem(x + dx, 4)} for dx in range(1, 4)]
    f1_got = (f1_got_0, f1_got_1)

    def piece(chunk, half, part):
        left = wo[pl.ds(pl.multiple_of(chunk * 288 + part * 144, 16), 144), :]
        right = ctx[pl.ds(half * 8, 8)].reshape(512, 512)
        return lax.dot_general(left, right, (((1,), (1,)), ((), ())), preferred_element_type=F32)

    hop, pass_hop = {}, {}
    for n in range(4):
        y_send[n] = piece(n, 1 - yh, 1).astype(BF)
        hop[n] = copy_to(y_send.at[n], y_relay.at[n], s_y.at[n], r_y.at[n], y_two if n % 2 else y_one)
        hop[n].start()
    first = Reduce4(z, a_send, a_got, a_more, a_more_got, a_s1, a_r1, a_s2, a_r2)
    for slot in (1, 0):
        for part in range(2):
            first.give(part, slot, piece(first.chunk(part, slot), part, 0).astype(BF))
    own_a[0] = piece(first.two, 0, 0)
    own_a[1] = piece(first.one, 1, 0)

    def forward(n):
        hop[n].wait_recv()
        pass_hop[n] = copy_to(y_relay.at[n], y_got.at[n], s_y.at[4 + n], r_y.at[4 + n], y_one if n % 2 else y_two)
        pass_hop[n].start()

    forward(0)
    forward(1)
    for part in range(2):
        first.pass_on(part, own_a[part])
    own_a[0] = piece(z, 0, 0)
    own_a[1] = piece(z, 1, 0)
    forward(2)
    forward(3)
    for n in range(4):
        own_b[n] = piece(n, yh, 1)
    for part in range(2):
        own_a[part] = first.own(part, own_a[part])
    h_send[...] = own_a[1 - yh].astype(BF)
    spans = (slice(0, 80), slice(80, 144))
    last = []
    for n, peer in enumerate((y_one, y_two)):
        last.append(copy_to(h_send.at[spans[n]], h_relay.at[spans[n]], s_h.at[n], r_h.at[n], peer))
        last[-1].start()
    second = Reduce4(z, b_send, b_got, b_more, b_more_got, b_s1, b_r1, b_s2, b_r2)
    for n in range(4):
        pass_hop[n].wait_recv()
        own_b[n] = own_b[n] + y_got[n].astype(F32)
    cols = (slice(0, 256), slice(256, 512))
    for slot in (1, 0):
        for part in range(2):
            second.give(part, slot, own_b[second.chunk(part, slot), :, cols[part]].astype(BF))
    for n, peer in enumerate((y_two, y_one)):
        last[n].wait_recv()
        last.append(copy_to(h_relay.at[spans[n]], h_got.at[spans[n]], s_h.at[2 + n], r_h.at[2 + n], peer))
        last[-1].start()
    second.pass_on(0, own_b[second.two, :, cols[0]])
    second.pass_on(1, own_b[second.one, :, cols[1]])
    for part in range(2):
        total[144:, cols[part]] = second.own(part, own_b[z, :, cols[part]])
    last[2].wait_recv()
    last[3].wait_recv()
    total[:144, :] = own_a[yh] + h_got[...].astype(F32)
    me = z * 4 + yl * 2 + c
    for m in range(4):
        value = total[:, m * 128:(m + 1) * 128]
        squares[me, m:m + 1, :] = jnp.sum(value * value, axis=0, keepdims=True)
    sums = []
    for e, peer in enumerate(group, 1):
        copy = copy_to(squares.at[me], squares.at[me], s_q.at[e], r_q.at[e], peer)
        copy.start()
        sums.append(copy)
    low = lax.broadcasted_iota(jnp.int32, (144, 128), 1) < 64

    def pair(m, part):
        at = pl.ds(pl.multiple_of(z * 288 + part * 144, 16), 144)
        a = xs[at, m * 256:m * 256 + 128].astype(F32)
        b = xs[at, m * 256 + 128:m * 256 + 256].astype(F32)
        upper, lower = pltpu.roll(a, 64, 1), pltpu.roll(b, 64, 1)
        return jnp.where(low, jnp.where(yh == 0, a, upper), jnp.where(yh == 0, lower, b))

    for part in range(2):
        for m in range(4):
            fresh[part, m] = pair(m, part)
    for copy in sums:
        copy.wait_recv()
    factor = lax.rsqrt(jnp.sum(squares[...], axis=0) * (1.0 / D) + EPS)
    starts, so_far = [], 0
    for j in range(16):
        starts.append(so_far)
        so_far = so_far + new_ref[j]
    here = pl.ds(x * 2, 2)
    over_x = []
    for part in range(2):
        rows_of = slice(part * 144, part * 144 + 144)
        for m in range(4):
            value = total[rows_of, m * 128:(m + 1) * 128] * factor[m:m + 1, :] * gain[rows_of, :]
            fresh[part, m] = fresh[part, m] + value
        for n in range(8):
            sides = []
            for side in range(2):
                j = 2 * n + side
                within = lax.rem(x - starts[j] + 64, 4)
                i = jnp.minimum(lax.div(starts[j] + within - x, 4), 7)
                at = lax.div(i, 2)
                place = lax.rem(i + at, 2) * 4 + at
                value = fresh[part, lax.div(place, 2)]
                value = jnp.where(lax.rem(place, 2) == side, value, pltpu.roll(value, 64, 1))
                sides.append(jnp.where(within < new_ref[j], value, 0.0))
            f1[part, n] = jnp.where(low, sides[0], sides[1]).astype(BF)
        f1_got[part][here] = f1[part, here]
        for d, peer in enumerate(others):
            n = part * 3 + d
            copy = copy_to(f1.at[part, pl.ds(peer["x"] * 2, 2)], f1_got[part].at[here], s_f.at[n], r_f.at[n], peer)
            copy.start()
            over_x.append(copy)
    mine = [sum([jnp.where(x * 4 + n > m, new_ref[m], 0) for m in range(15)]) for n in range(4)]
    out, swap = [], []
    for part in range(2):
        rows_of = slice(part * 144, part * 144 + 144)
        for copy in over_x[part * 3:part * 3 + 3]:
            copy.wait_recv()
        for e in range(8):
            n = part * 8 + e
            dz, dy = e // 2, e % 2
            tz, ty = lax.rem(z + dz, 4), yl + dy - 2 * yl * dy
            sides = []
            for side in range(2):
                start = jnp.where(ty == 0, mine[side], mine[2 + side])
                sides.append(f1_got[part][lax.rem(start + tz, 4) * 2 + ty].astype(F32))
            value = jnp.where(low, sides[0], sides[1]).astype(BF)
            at = (z * 2 + yl) * 2 + c
            if e == 0:
                fin[at, rows_of, :] = value
            else:
                f2[part, e] = value
                copy = copy_to(f2.at[part, e], fin.at[at, rows_of], s_g.at[n], r_g.at[n], {"z": tz, "yl": ty})
                copy.start()
                out.append(copy)
    for part in range(2):
        rows_of = slice(part * 144, part * 144 + 144)
        for e in range(8):
            n = part * 8 + e
            dz, dy = e // 2, e % 2
            at = (mod4(z - dz) * 2 + yl + dy - 2 * yl * dy) * 2 + c
            ref = fin.at[at, rows_of]
            if e > 0:
                copy_to(ref, ref, s_g.at[n], r_g.at[n], core).wait_recv()
            copy = copy_to(ref, ref, s_c.at[n], r_c.at[n], core)
            copy.start()
            swap.append(copy)
    for copy in swap:
        copy.wait_recv()
    first.sent()
    second.sent()
    for copy in list(hop.values()) + list(pass_hop.values()) + last + sums + over_x + out + swap:
        copy.wait_send()


STAGE_IN = [
    VM((1152, 512), BF), VM((1152, 256), BF), VM((1152, 256), BF),
    VM((1152, 128), F32), VM((128, 128), F32), VM((64, 512), F32), VM((64, 512), F32),
    VM((2, 8, 144, 128), BF), VM((24, 144, 128), BF), VM((24, 144, 128), BF), VM((1152, 1024), BF), VM((16, 8, 128), F32),
    VM((2, 512, 512), F32), VM((2, 512, 512), F32), VM((512, 512), BF), VM((512, 512), BF), VM((2, 512, 512), F32),
    DMA((4,)), DMA((16,)), DMA((16,)), DMA((16,)), DMA((16,)), DMA((16,)), DMA((16,)),
    DMA((18,)), DMA((18,)), DMA((6,)), DMA((6,)), DMA((6,)), DMA((6,)), DMA((16,)), DMA((16,)),
    DMA((2,)), DMA((2,)), DMA((4,)), DMA((4,)),
]
STAGE_ATTEND = [
    VM((4, 256, 128), BF), VM((4, 256, 128), F32), VM((4, 256, 128), F32),
    DMA((8,)), DMA((8,)), DMA((4,)), DMA((4,)),
]
STAGE_OUT = (
    [VM((2, 2, 144, 512), BF), VM((2, 2, 144, 512), BF), VM((2, 144, 512), BF), VM((2, 144, 512), BF)]
    + [VM((2, 2, 144, 256), BF), VM((2, 2, 144, 256), BF), VM((2, 144, 256), BF), VM((2, 144, 256), BF)]
    + [VM((4, 144, 512), BF)] * 3
    + [VM((144, 512), BF)] * 3
    + [VM((2, 144, 512), F32), VM((4, 144, 512), F32), VM((288, 512), F32)]
    + [VM((16, 4, 128), F32), VM((2, 4, 144, 128), F32)]
    + [VM((2, 8, 144, 128), BF)] * 2
    + [VM((8, 144, 128), BF)] * 2
    + [DMA((4,)), DMA((4,)), DMA((2,)), DMA((2,))] * 2
    + [DMA((8,)), DMA((8,)), DMA((4,)), DMA((4,)), DMA((16,)), DMA((16,)), DMA((6,)), DMA((6,))]
    + [DMA((16,)), DMA((16,)), DMA((16,)), DMA((16,))]
)
SHARED = [
    VM((256, 512), BF), VM((4, 256, 128), BF), VM((1152, 1024), BF), VM((1152, 512), BF), VM((16, 64, 512), BF),
    VM((288, 128), F32), VM((8, 256, 512), BF), DMA((12,)), DMA((12,)), DMA((8,)), DMA((8,)),
]


def kernel(old_ref, new_ref, order_ref, xt, pre_ref, post_ref, wq_in, wk_in, wv_in, wo_in, fin, *scratch):
    q, kv, xs, wo, ctx, gain_out, kvs, s_x, r_x, s_c, r_c = scratch[:11]
    scratch = scratch[11:]
    keys_values = KeysValues(kv, kvs, s_x, r_x, s_c, r_c)
    own_in, scratch = scratch[:len(STAGE_IN)], scratch[len(STAGE_IN):]
    own_attend, own_out = scratch[:len(STAGE_ATTEND)], scratch[len(STAGE_ATTEND):]
    end_in = stage_in(
        old_ref, order_ref, xt, pre_ref, post_ref, wq_in, wk_in, wv_in, wo_in, q, kv, xs, wo, gain_out, *own_in,
        keys_values.send,
    )
    end_attend = stage_attend(q, ctx, keys_values, kvs, *own_attend)
    end_in()
    stage_out(new_ref, ctx, xs, wo, gain_out, fin, *own_out)
    end_attend()


def run(old_blocks, new_blocks, order, xt, pre_gain, post_gain, w_query, w_key, w_value, w_out_t):
    smem = pl.BlockSpec(memory_space=pltpu.SMEM)
    vmem = pl.BlockSpec(memory_space=pltpu.VMEM)
    hbm = pl.BlockSpec(memory_space=pltpu.HBM)
    return pl.pallas_call(
        kernel,
        name="sublayer",
        out_shape=jax.ShapeDtypeStruct((16, 288, 128), BF),
        in_specs=[smem, smem, smem, vmem, vmem, vmem, hbm, hbm, hbm, hbm],
        out_specs=vmem,
        scratch_shapes=SHARED + STAGE_IN + STAGE_ATTEND + STAGE_OUT,
        compiler_params=pltpu.CompilerParams(collective_id=0, has_side_effects=True, vmem_limit_bytes=62 * 2**20),
    )(old_blocks, new_blocks, order, xt, pre_gain, post_gain, w_query, w_key, w_value, w_out_t)


def per_device(
    x_old, old_blocks, new_blocks, order, pre_gain, post_gain, w_query, w_key, w_value, w_out_t
):
    c = lax.axis_index("c")
    fin = run(
        old_blocks, new_blocks, order, x_old.T, pre_gain.reshape(36, 128), post_gain.reshape(36, 128),
        w_query, w_key, w_value, w_out_t,
    )
    return lax.dynamic_slice(fin, (0, 0, c * 64), (16, 288, 64)).reshape(4608, 64).T


def solution(mesh):
    torus = Mesh(mesh.devices.reshape(4, 2, 2, 4, 2), ("x", "yl", "c", "z", "yh"))
    seq, tp = ("x", "yl", "c"), ("z", "yh")
    both = P(seq, tp)
    in_specs = (both, P(), P(), P(), P(), P(), both, both, both, both)
    return jax.shard_map(
        per_device, mesh=torus, in_specs=in_specs, out_specs=P(seq + tp, None), check_vma=False
    )
```

time: 180 us -> 138 us (0.77)
  Pallas kernels: 169 us -> 135 us
  local copies, waits for them, and re-layouts: 9.41 us -> 2.94 us
    pallas_call x3 -> x1, Pallas kernels: 169 us -> 135 us  [run(): pl.pallas_call(kernel, name='sublayer', out_shape=jax.ShapeDtypeStruct((1...]
    unnamed x6 -> x0, local copies, waits for them, and re-layouts: 2.9 us -> none
    broadcast_in_dim x3 -> x0, local copies, waits for them, and re-layouts: 1.88 us -> none  [the longest x2 1.11 us: per_device(): gain = jnp.broadcast_to(gain, (1152, 128))]
where the time goes in v2:
time: 138 us
  Pallas kernels  135 us (98%)
  local copies, waits for them, and re-layouts  2.94 us (2%)
    pallas_call x1, Pallas kernels, run(): pl.pallas_call(kernel, name='sublayer', out_shape=jax.ShapeDtypeStruct((1...  135 us

profile of v2, /device:TPU:1, one launch (start us, length us, event | category | flops | bytes accessed | tf_op | source)
XLA Modules:
  0.0 137.5 jit_solution(1196270715419261356)
XLA Ops:
  0.0 134.6 %sublayer.1 = bf16[16,288,128]{2,1,0:T(8,128)(2,1)} custom-call(s32[16]{0:T(128)} %old_ref.1, s32[16]{0:T(128)} %new_ref.1, s32[16]{0:T(128)} %order_ref.1, bf16[576,512]{1,0:T(8,128)(2,1)} %bitcast.6, f32[36,128]{1,0:T(8,128)} %bitcast.7, f32[36,128]{1,0:T(8,128)} %bitcast.8, bf16[288,512]{1,0:T(8,128)(2,1)} %wq_in.1, bf16[288,256]{1,0:T(8,128)(2,1)} %wk_in.1, ...), custom_call_target="tpu_custom_call" | custom-call | tf_op jit(solution)/shard_map/sublayer/pallas_call | solution.py:745
  134.6 1.7 %constant_dynamic-slice_fusion = bf16[16,288,64]{2,1,0:T(8,128)(2,1)S(1)} fusion(bf16[16,288,128]{2,1,0:T(8,128)(2,1)} %sublayer.1, s32[]{:T(128)S(6)} %select_n.3), kind=kLoop, calls=%fused_computation | loop fusion | bytes 1179652 | tf_op jit(solution)/shard_map/dynamic_slice | solution.py:764
  136.2 1.3 copy.12

commit v3 on v2

v3 whole, which is shorter than its diff:
```python
import functools
import math

import jax
import jax.numpy as jnp
from jax import lax
from jax.experimental import pallas as pl
from jax.experimental.pallas import tpu as pltpu
from jax.sharding import Mesh
from jax.sharding import PartitionSpec as P

D = 4608
HEADS = 32
HEAD = 128
BLOCK = 128
EPS = 1e-06
BF = jnp.bfloat16
F32 = jnp.float32
VM = pltpu.VMEM
OUT = (160, 128)
PARTS = 3
WIDE = 288 // PARTS
DMA = pltpu.SemaphoreType.DMA


def kept(at, c):
    return 2 * at + lax.rem(at + c, 2)


def coords():
    return tuple(lax.axis_index(name) for name in ("x", "yl", "c", "z", "yh"))


def copy_to(src, dst, send_sem, recv_sem, device):
    return pltpu.make_async_remote_copy(
        src_ref=src,
        dst_ref=dst,
        send_sem=send_sem,
        recv_sem=recv_sem,
        device_id=device,
        device_id_type=pl.DeviceIdType.MESH,
    )


def greet(devices):
    sem = pltpu.get_barrier_semaphore()
    for device in devices:
        pl.semaphore_signal(sem, inc=1, device_id=device, device_id_type=pl.DeviceIdType.MESH)


def greeted(devices):
    pl.semaphore_wait(pltpu.get_barrier_semaphore(), len(devices))


def mod4(v):
    return lax.rem(v + 4, 4)


class Gather4:
    def __init__(self, views, axis, me, send, recv):
        one, two = me + 1 - 2 * lax.rem(me, 2), 3 - me
        far = two + 1 - 2 * lax.rem(two, 2)
        self.moves = [
            (me, one, 0, one),
            (me, two, 1, two),
            (me, two, 0, two),
            (me, one, 1, one),
            (one, far, 0, two),
            (two, far, 1, one),
        ]
        self.views, self.axis, self.send, self.recv = views, axis, send, recv

    def each(self, move, got):
        sent, received, half, partner = self.moves[move]
        for n, view in enumerate(self.views):
            ref = view(received if got else sent, half)
            at = n * 6 + move
            yield copy_to(ref, ref, self.send.at[at], self.recv.at[at], {self.axis: partner})

    def go(self, *moves):
        for move in moves:
            for copy in self.each(move, False):
                copy.start()

    def got(self, *moves):
        for move in moves:
            for copy in self.each(move, True):
                copy.wait_recv()

    def sent(self):
        for move in range(6):
            for copy in self.each(move, False):
                copy.wait_send()


def rows(ref, start, size, unit=16):
    return ref.at[pl.ds(pl.multiple_of(start, unit), size)]


def lanes(start, size):
    return pl.ds(pl.multiple_of(start, 128), size)


def columns(dst, table, chunk_of, count):
    lane = lax.broadcasted_iota(jnp.int32, (32, 128), 1)

    def body(n, _):
        feature = chunk_of(lax.div(n, 9)) * 288 + lax.rem(n, 9) * 32
        part = table[pl.ds(pl.multiple_of(lax.rem(feature, 128), 32), 32), :]
        value = jnp.sum(jnp.where(lane == lax.div(feature, 128), part, 0.0), axis=1, keepdims=True)
        dst[pl.ds(pl.multiple_of(n * 32, 32), 32), :] = jnp.broadcast_to(value, (32, 128))
        return 0

    lax.fori_loop(0, count * 9, body, 0)


def stage_in(
    old_ref, order_ref, xt_in, pre_ref, post_ref, wq_in, wk_in, wv_in, wo_in,
    q_out, kv_out, xs, wo, gain_out,
    wq, wk, wv, gain, table, cos, sin, xt, slots, landed_0, landed_1, landed_2, normed, squares, near, other, to_y, from_y, mine,
    s_w, s_one, r_one, s_two, r_two, s_three, r_three, s_wg, r_wg, s_og, r_og, s_z, r_z, s_q, r_q, s_c, r_c, s_y, r_y,
    keys_values,
):
    x, yl, c, z, yh = coords()
    landed = (landed_0, landed_1, landed_2)
    ring_peers = [
        {"x": lax.rem(x + dx, 4), "c": c + dc - 2 * c * dc} for dx in range(4) for dc in range(2)
    ][1:]
    y_one = {"yl": 1 - yl}
    y_two = {"yl": 1 - yl, "yh": 1 - yh}
    group = [
        {"z": lax.rem(z + dz, 4), "yl": yl + dy - 2 * yl * dy, "c": c + dc - 2 * c * dc}
        for dz in range(4) for dy in range(2) for dc in range(2)
    ][1:]
    greet(ring_peers + [y_two] + group)
    into = pltpu.make_async_copy(xt_in, xt, s_w.at[5])
    into.start()
    at = pl.ds(pl.multiple_of(x * 288, 16), 288)
    owns = [
        pltpu.make_async_copy(src, dst.at[at], s_w.at[n])
        for n, (src, dst) in enumerate(((wq_in, wq), (wk_in, wk), (wv_in, wv)))
    ]

    def out_rows(chunk, half):
        return rows(wo, half * 4 * OUT[0] + chunk * OUT[half], OUT[half])

    for half in range(2):
        part = wo_in.at[pl.ds(half * OUT[0], OUT[half])]
        owns.append(pltpu.make_async_copy(part, out_rows(x, half), s_w.at[3 + half]))
    for copy in owns:
        copy.start()
    starts, total = [], 0
    for m in range(16):
        starts.append(total)
        total = total + old_ref[m]
    k = order_ref[x * 4 + yl * 2 + c]
    first = sum([jnp.where(k > m, old_ref[m], 0) for m in range(15)])
    into.wait()
    for r in range(4):
        b = lax.rem(r - first + 64, 4)
        for h in range(2):
            for half in range(PARTS):
                at_rows = slice(h * 288 + half * WIDE, h * 288 + half * WIDE + WIDE)
                part = [xt[at_rows, n * 128:(n + 1) * 128] for n in range(4)]
                low = jnp.where(b == 0, part[0], part[1])
                slots[half, r * 2 + h] = jnp.where(b < 2, low, jnp.where(b == 2, part[2], part[3]))
    here = x * 2 + c
    for half in range(PARTS):
        landed[half][here] = slots[half, here]
    greeted(ring_peers + [y_two] + group)
    one, two, three = [], [], []
    for half in range(PARTS):
        for d, peer in enumerate(ring_peers, 1):
            n = half * 8 + d
            copy = copy_to(
                slots.at[half, peer["x"] * 2 + peer["c"]], landed[half].at[here], s_one.at[n], r_one.at[n], peer
            )
            copy.start()
            one.append(copy)
    for copy in owns:
        copy.wait()

    def half_rows(ref):
        return lambda chunk, half: rows(ref, chunk * 288 + half * 144, 144)

    weights = Gather4([half_rows(r) for r in (wq, wk, wv)], "x", x, s_wg, r_wg)
    weights.go(0, 1, 2, 3)
    straight = yl == yh
    for half in range(PARTS):
        for d in range(8):
            n = half * 8 + d
            dx, dc = d // 2, d % 2
            slot = mod4(x - dx) * 2 + c + dc - 2 * c * dc
            if d > 0:
                copy_to(slots.at[half, slot], landed[half].at[slot], s_one.at[n], r_one.at[n], y_one).wait_recv()
            copy = copy_to(landed[half].at[slot], landed[half].at[8 + slot], s_two.at[n], r_two.at[n], y_two)
            copy.start()
            two.append(copy)
            copy = copy_to(landed[half].at[slot], landed[half].at[16 + slot], s_three.at[n], r_three.at[n], y_one)
            relay = copy_to(landed[half].at[8 + slot], landed[half].at[16 + slot], s_three.at[n], r_three.at[n], y_one)
            three.append((copy, relay))
            pl.when(jnp.logical_not(straight))(copy.start)
            if half == 2:
                two[d].wait_recv()
                pl.when(straight)(three[d][1].start)
    me = z * 4 + yl * 2 + c
    first_buffer = jnp.where(straight, 0, 1)

    def part_rows(part):
        return lambda chunk, half: rows(xs, chunk * 288 + part * WIDE + half * (WIDE // 2), WIDE // 2)

    gathers = [
        Gather4([part_rows(part)], "z", z, s_z.at[pl.ds(6 * part, 6)], r_z.at[pl.ds(6 * part, 6)])
        for part in range(PARTS)
    ]
    sources = []
    for place in range(8):
        g = x + 4 * kept(place % 4, place // 4)
        shard = sum([jnp.where(starts[m] <= g, 1, 0) for m in range(16)]) - 1
        holder = sum([jnp.where(order_ref[p] == shard, p, 0) for p in range(16)])
        y_source = lax.rem(lax.div(holder, 2), 2)
        sources.append(jnp.where(y_source == yh, first_buffer, 2) * 8 + lax.div(holder, 4) * 2 + lax.rem(holder, 2))

    def pick(half):
        for n in range(half * 8, half * 8 + 8):
            three[n][0].wait_recv()
        for place in range(8):
            block = landed[half][sources[place]]
            xs[pl.ds(pl.multiple_of(z * 288 + half * WIDE, 32), WIDE), place * 128:(place + 1) * 128] = block
            wide = block.astype(F32)
            square = jnp.sum(wide * wide, axis=0, keepdims=True)
            if half > 0:
                square = square + squares[me, place:place + 1, :]
            squares[me, place:place + 1, :] = square
        gathers[half].go(0, 1, 2, 3)

    for n in range(8, 24):
        if n in (13, 21):
            pick((n - 13) // 8)
        two[n].wait_recv()
        pl.when(straight)(three[n][1].start)
    pick(2)
    weights.got(0, 1)
    weights.go(4, 5)
    wo_all = Gather4([out_rows], "x", x, s_og, r_og)
    wo_all.go(0, 1, 2, 3)
    sums = []
    for e, peer in enumerate(group, 1):
        copy = copy_to(squares.at[me], squares.at[me], s_q.at[e], r_q.at[e], peer)
        copy.start()
        sums.append(copy)
    table[...] = jnp.zeros_like(table)
    table[0:36, :] = pre_ref[...]
    table[...] = table[...].T
    columns(gain, table, lambda n: n * 4 + yl * 2 + c, 4)
    table[...] = jnp.zeros_like(table)
    table[0:36, :] = post_ref[...]
    table[...] = table[...].T
    columns(gain_out, table, lambda n: z * 4 + yl * 2 + c, 1)
    gathers[0].got(0, 1)
    gathers[0].go(4, 5)
    half_head = HEAD // 2
    inverse = jnp.exp(
        lax.broadcasted_iota(jnp.int32, (half_head, 128), 0).astype(F32) * (-2.0 * math.log(10000.0) / HEAD)
    )
    for p in range(4):
        place_of = (x + 4 * kept(p, c)) * BLOCK + lax.broadcasted_iota(jnp.int32, (half_head, 128), 1)
        angle = inverse * place_of.astype(F32)
        cos[:, p * 128:(p + 1) * 128] = jnp.cos(angle)
        sin[:, p * 128:(p + 1) * 128] = jnp.sin(angle)
    for part in (1, 2):
        gathers[part].got(0, 1)
        gathers[part].go(4, 5)
    for copy in sums:
        copy.wait_recv()
    factor = lax.rsqrt(jnp.sum(squares[...], axis=0) * (1.0 / D) + EPS)

    def norm(chunk):
        for place in range(8):
            scale = factor[place:place + 1, :]

            def norm_rows(n, _, place=place, scale=scale):
                part = pl.ds(pl.multiple_of(chunk * 288 + n * 144, 16), 144)
                at = (part, slice(place * 128, (place + 1) * 128))
                normed[at] = (xs[at].astype(F32) * scale * gain[part, :]).astype(BF)
                return 0

            lax.fori_loop(0, 2, norm_rows, 0)

    pieces = {"q": (slice(0, 256), wq, 256), "k": (slice(256, 384), wk, 128), "v": (slice(384, 512), wv, 128)}

    def corner(dst, y, core, late, names="qkv"):
        low = lax.div(z, 2)
        part = pl.ds(pl.multiple_of((1 - low if late else low) * 576, 16), 576)
        right = normed[part, lanes(core * 512, 512)]
        for name in names:
            to, table_of, width = pieces[name]
            left = table_of[part, lanes(y * width, width)]
            value = lax.dot_general(left, right, (((0,), (0,)), ((), ())), preferred_element_type=F32)
            if late:
                dst[to, :] += value
            else:
                dst[to, :] = value

    norm(z)
    for one_part in gathers:
        one_part.got(3)
    norm(z + 1 - 2 * lax.rem(z, 2))
    weights.got(2, 3, 4, 5)
    corners = [
        (near.at[0], 1 - yl, 1 - c), (mine.at[0], 1 - yl, c), (near.at[1], yl, 1 - c), (mine.at[1], yl, c),
    ]
    for dst, y, core in corners:
        corner(dst, y, core, False)
    for one_part in gathers:
        one_part.got(2)
    norm(3 - z)
    wo_all.got(0, 1)
    wo_all.go(4, 5)
    for one_part in gathers:
        one_part.got(4, 5)
    far = 3 - z
    norm(far + 1 - 2 * lax.rem(far, 2))
    core = {"c": 1 - c}
    to_core = {}

    def over_core(n, name):
        to = pieces[name][0]
        at = n * 3 + "kvq".index(name)
        copy = copy_to(near.at[n, to], other.at[n, to], s_c.at[at], r_c.at[at], core)
        copy.start()
        to_core[n, name] = copy

    to_partner = {}
    first_rows, last_rows = slice(0, 256), slice(256, 512)
    k_part, v_part = slice(256, 384), slice(384, 512)
    spans = (
        (0, k_part, first_rows), (1, v_part, first_rows), (2, k_part, last_rows), (3, v_part, last_rows),
        (4, slice(0, 256), first_rows), (5, slice(0, 256), last_rows),
    )

    def over_y(name):
        to_core[0, name].wait_recv()
        to = pieces[name][0]
        to_y[to, :] = (mine[0, to, :] + other[0, to, :]).astype(BF)
        for at, part, cols in {"k": spans[:1], "v": spans[1:4], "q": spans[4:]}[name]:
            copy = copy_to(to_y.at[part, cols], from_y.at[part, cols], s_y.at[at], r_y.at[at], y_one)
            to_partner[at] = copy
            copy.start()

    for name in "kv":
        corner(*corners[0], True, name)
        over_core(0, name)
    corner(*corners[1], True, "kv")
    over_y("k")
    corner(*corners[0], True, "q")
    over_core(0, "q")
    over_y("v")
    corner(*corners[1], True, "q")
    over_y("q")
    corner(*corners[2], True)
    for name in "kvq":
        over_core(1, name)
    corner(*corners[3], True)
    for name in "kvq":
        to_core[1, name].wait_recv()
    scale_q = (D // HEADS) ** (-0.5)

    def summed(part, cols):
        return mine[1, part, cols] + other[1, part, cols] + from_y[part, cols].astype(F32)

    def turned(value, cols):
        a, b = value[:64], value[64:]
        return jnp.concatenate(
            [a * cos[:, cols] - b * sin[:, cols], b * cos[:, cols] + a * sin[:, cols]], axis=0
        ).astype(BF)

    for late, cols in enumerate((first_rows, last_rows)):
        to_partner[2 * late].wait_recv()
        key = turned(summed(k_part, cols), cols)
        to_partner[2 * late + 1].wait_recv()
        value = summed(v_part, cols).astype(BF)
        for p in range(2):
            kv_out[2 * late + p, :128, :] = key[:, p * 128:(p + 1) * 128]
            kv_out[2 * late + p, 128:, :] = value[:, p * 128:(p + 1) * 128]
        keys_values.send(late)
    for late in range(2):
        keys_values.gathers[late].got(0, 1)
        keys_values.gathers[late].go(4, 5)
    for late, cols in enumerate((first_rows, last_rows)):
        to_partner[4 + late].wait_recv()
        for h in range(2):
            part = slice(h * 128, (h + 1) * 128)
            a, b = summed(slice(h * 128, h * 128 + 64), cols), summed(slice(h * 128 + 64, h * 128 + 128), cols)
            turn_a = a * cos[:, cols] - b * sin[:, cols]
            turn_b = b * cos[:, cols] + a * sin[:, cols]
            q_out[part, cols] = (jnp.concatenate([turn_a, turn_b], axis=0) * scale_q).astype(BF)

    def finish():
        wo_all.got(2, 3, 4, 5)
        for copy in one + two + sums + list(to_core.values()) + list(to_partner.values()):
            copy.wait_send()
        for copy, _ in three:
            copy.wait_send()
        weights.sent()
        wo_all.sent()
        for one_part in gathers:
            one_part.sent()

    return finish


class KeysValues:
    def __init__(self, kv_ref, kvs, s_x, r_x, s_c, r_c):
        x, _, c, _, _ = coords()

        def block(late):
            return lambda chunk, half: kvs.at[kept(2 * late + half, c), :, lanes(chunk * 128, 128)]

        self.gathers = [
            Gather4([block(late)], "x", x, s_x.at[pl.ds(6 * late, 6)], r_x.at[pl.ds(6 * late, 6)]) for late in range(2)
        ]
        self.kv_ref, self.kvs, self.s_c, self.r_c = kv_ref, kvs, s_c, r_c
        self.across = []

    def send(self, late):
        x, _, c, _, _ = coords()
        for p in (2 * late, 2 * late + 1):
            self.kvs[kept(p, c), :, lanes(x * 128, 128)] = self.kv_ref[p]
        self.gathers[late].go(0, 1, 2, 3)

    def core_copies(self, late, mine):
        _, _, c, _, _ = coords()
        for p in (2 * late, 2 * late + 1):
            ref = self.kvs.at[kept(p, c if mine else 1 - c)]
            yield copy_to(ref, ref, self.s_c.at[p], self.r_c.at[p], {"c": 1 - c})

    def to_core(self, late):
        self.gathers[late].got(2, 3, 4, 5)
        for copy in self.core_copies(late, True):
            copy.start()
            self.across.append(copy)

    def from_core(self, late):
        for copy in self.core_copies(late, False):
            copy.wait_recv()


def stage_attend(q_ref, ctx, keys_values, kvs, qs, acc, den, s_y, r_y, s_o, r_o):
    x, yl, c, z, yh = coords()
    core, y_one = {"c": 1 - c}, {"yl": 1 - yl}
    for p in range(4):
        for h in range(2):
            part = q_ref[h * 128:(h + 1) * 128, p * 128:(p + 1) * 128].astype(F32)
            qs[p, h * 128:(h + 1) * 128, :] = part.T.astype(BF)
    acc[...] = jnp.zeros_like(acc)
    den[...] = jnp.zeros_like(den)
    keys_values.to_core(0)

    def tiles(pairs, core_at, diagonal=()):
        pairs = [(p, kept(e, core_at), n in diagonal) for n, (p, e) in enumerate(pairs)]
        scores = [jnp.dot(qs[p], kvs[group, :128, :], preferred_element_type=F32) for p, group, _ in pairs]
        for (p, group, masked), score in zip(pairs, scores):
            weight = jnp.exp2((50.0 * math.log2(math.e)) * jnp.tanh(score * (1.0 / 50.0)))
            if masked:
                row = lax.rem(lax.broadcasted_iota(jnp.int32, (256, 512), 0), 128)
                col = lax.broadcasted_iota(jnp.int32, (256, 512), 1)
                weight = jnp.where(col - row <= x * 128, weight, 0.0)
            den[p] += sum([weight[:, n:n + 128] for n in range(0, 512, 128)])
            acc[p] += lax.dot_general(
                weight.astype(BF), kvs[group, 128:, :], (((1,), (1,)), ((), ())), preferred_element_type=F32
            )

    def region(core_at, y_at, at, size):
        return ctx.at[pl.ds(at + core_at * 4, size), :, lanes(y_at * 256, 256)]

    to_y, to_core = [], []

    def put(step):
        for p in (2 * step, 2 * step + 1):
            for h in range(2):
                part = slice(h * 128, (h + 1) * 128)
                total = jnp.sum(den[p, part, :], axis=1, keepdims=True)
                value = (acc[p, part, :] / total).astype(BF)
                cols = lanes(yl * 256 + h * 128, 128)
                ctx[c * 4 + p, :, cols] = value[:64]
                ctx[8 + c * 4 + p, :, cols] = value[64:]
        for peer, send, recv, at in ((y_one, s_y, r_y, to_y), (core, s_o, r_o, to_core)):
            for half in range(2):
                n = half * 2 + step
                ref = region(c, yl, half * 8 + 2 * step, 2)
                copy = copy_to(ref, ref, send.at[n], recv.at[n], peer)
                copy.start()
                at.append(copy)

    def pass_on(step):
        for half in range(2):
            n = half * 2 + step
            ref = region(c, 1 - yl, half * 8 + 2 * step, 2)
            copy_to(ref, ref, s_y.at[n], r_y.at[n], y_one).wait_recv()
            copy = copy_to(ref, ref, s_o.at[4 + n], r_o.at[4 + n], core)
            copy.start()
            to_core.append(copy)

    tiles([(0, 0), (1, 0), (1, 1)], c, (0, 2))
    keys_values.from_core(0)
    tiles([(1 - c, 0), (1, 1 - c)], 1 - c)
    put(0)
    tiles([(2, 0), (2, 1), (3, 0), (3, 1)], c)
    keys_values.to_core(1)
    tiles([(2, 0), (2, 1), (3, 0), (3, 1)], 1 - c)
    tiles([(2, 2), (3, 2), (3, 3)], c, (0, 2))
    keys_values.from_core(1)
    tiles([(3 - c, 2), (3, 3 - c)], 1 - c)
    put(1)
    pass_on(0)
    pass_on(1)
    for n in range(8):
        half, step = (n % 4) // 2, n % 2
        ref = region(1 - c, yl if n < 4 else 1 - yl, half * 8 + 2 * step, 2)
        copy_to(ref, ref, s_o.at[n], r_o.at[n], core).wait_recv()

    def finish():
        for copy in keys_values.across + to_y + to_core:
            copy.wait_send()
        for one_part in keys_values.gathers:
            one_part.sent()

    return finish


class Reduce4:
    def __init__(self, z, send, got, more, more_got, s_1, r_1, s_2, r_2):
        self.one, self.two = z + 1 - 2 * lax.rem(z, 2), 3 - z
        self.far = self.two + 1 - 2 * lax.rem(self.two, 2)
        self.send, self.got, self.more, self.more_got = send, got, more, more_got
        self.sems = (s_1, r_1, s_2, r_2)
        self.first, self.second = {}, []

    def partner(self, part, step):
        return {"z": self.one if part == step else self.two}

    def chunk(self, part, slot):
        return self.far if slot == 1 else (self.two if part else self.one)

    def give(self, part, slot, value):
        self.send[part, slot] = value
        n = part * 2 + slot
        copy = copy_to(
            self.send.at[part, slot], self.got.at[part, slot], self.sems[0].at[n], self.sems[1].at[n], self.partner(part, 0)
        )
        copy.start()
        self.first[part, slot] = copy

    def pass_on(self, part, value):
        self.first[part, 1].wait_recv()
        self.more[part] = (value + self.got[part, 1].astype(F32)).astype(BF)
        copy = copy_to(
            self.more.at[part], self.more_got.at[part], self.sems[2].at[part], self.sems[3].at[part], self.partner(part, 1)
        )
        copy.start()
        self.second.append(copy)

    def own(self, part, value):
        self.first[part, 0].wait_recv()
        value = value + self.got[part, 0].astype(F32)
        self.second[part].wait_recv()
        return value + self.more_got[part].astype(F32)

    def sent(self):
        for copy in list(self.first.values()) + self.second:
            copy.wait_send()


def stage_out(
    new_ref, ctx, xs, wo, gain, fin,
    a_send, a_got, a_more, a_more_got, b_send, b_got, b_more, b_more_got,
    y_send, y_relay, y_got, h_send, h_relay, h_got, own_a, own_b, total,
    squares, fresh, f1, f2, f1_got_0, f1_got_1, f1_got_2,
    a_s1, a_r1, a_s2, a_r2, b_s1, b_r1, b_s2, b_r2, s_y, r_y, s_h, r_h, s_q, r_q, s_f, r_f, s_g, r_g, s_c, r_c,
):
    x, yl, c, z, yh = coords()
    core = {"c": 1 - c}
    y_one, y_two = {"yl": 1 - yl}, {"yl": 1 - yl, "yh": 1 - yh}
    group = [
        {"z": lax.rem(z + dz, 4), "yl": yl + dy - 2 * yl * dy, "c": c + dc - 2 * c * dc}
        for dz in range(4) for dy in range(2) for dc in range(2)
    ][1:]
    others = [{"x": lax.rem(x + dx, 4)} for dx in range(1, 4)]
    f1_got = (f1_got_0, f1_got_1, f1_got_2)

    def sums_of(half, part):
        left = wo[part * 4 * OUT[0]:part * 4 * OUT[0] + 4 * OUT[part], :]
        right = ctx[pl.ds(half * 8, 8)].reshape(512, 512)
        value = lax.dot_general(left, right, (((1,), (1,)), ((), ())), preferred_element_type=F32)
        return value.reshape(4, OUT[part], 512)

    hop, pass_hop = {}, {}
    y_send[...] = sums_of(1 - yh, 1).astype(BF)
    for n in range(4):
        hop[n] = copy_to(y_send.at[n], y_relay.at[n], s_y.at[n], r_y.at[n], y_two if n % 2 else y_one)
        hop[n].start()
    first = Reduce4(z, a_send, a_got, a_more, a_more_got, a_s1, a_r1, a_s2, a_r2)
    for part in range(2):
        own_a[part] = sums_of(part, 0)
        first.give(part, 1, own_a[part, first.chunk(part, 1)].astype(BF))
    for part in range(2):
        first.give(part, 0, own_a[part, first.chunk(part, 0)].astype(BF))
    own_b[...] = sums_of(yh, 1)

    def forward(n):
        hop[n].wait_recv()
        pass_hop[n] = copy_to(y_relay.at[n], y_got.at[n], s_y.at[4 + n], r_y.at[4 + n], y_one if n % 2 else y_two)
        pass_hop[n].start()

    forward(0)
    forward(1)
    for part in range(2):
        first.pass_on(part, own_a[part, first.one if part else first.two])
    forward(2)
    forward(3)
    for part in range(2):
        own_a[part, z] = first.own(part, own_a[part, z])
    h_send[...] = own_a[1 - yh, z].astype(BF)
    spans = (slice(0, 80), slice(80, OUT[0]))
    last = []
    for n, peer in enumerate((y_one, y_two)):
        last.append(copy_to(h_send.at[spans[n]], h_relay.at[spans[n]], s_h.at[n], r_h.at[n], peer))
        last[-1].start()
    second = Reduce4(z, b_send, b_got, b_more, b_more_got, b_s1, b_r1, b_s2, b_r2)
    for n in range(4):
        pass_hop[n].wait_recv()
        own_b[n] = own_b[n] + y_got[n].astype(F32)
    cols = (slice(0, 256), slice(256, 512))
    for slot in (1, 0):
        for part in range(2):
            second.give(part, slot, own_b[second.chunk(part, slot), :, cols[part]].astype(BF))
    for n, peer in enumerate((y_two, y_one)):
        last[n].wait_recv()
        last.append(copy_to(h_relay.at[spans[n]], h_got.at[spans[n]], s_h.at[2 + n], r_h.at[2 + n], peer))
        last[-1].start()
    second.pass_on(0, own_b[second.two, :, cols[0]])
    second.pass_on(1, own_b[second.one, :, cols[1]])
    for part in range(2):
        total[OUT[0]:, cols[part]] = second.own(part, own_b[z, :, cols[part]])
    last[2].wait_recv()
    last[3].wait_recv()
    total[:OUT[0], :] = own_a[yh, z] + h_got[...].astype(F32)
    me = z * 4 + yl * 2 + c
    for m in range(4):
        value = total[:, m * 128:(m + 1) * 128]
        squares[me, m:m + 1, :] = jnp.sum(value * value, axis=0, keepdims=True)
    sums = []
    for e, peer in enumerate(group, 1):
        copy = copy_to(squares.at[me], squares.at[me], s_q.at[e], r_q.at[e], peer)
        copy.start()
        sums.append(copy)
    low = lax.broadcasted_iota(jnp.int32, (WIDE, 128), 1) < 64

    def pair(m, part):
        at = pl.ds(pl.multiple_of(z * 288 + part * WIDE, 32), WIDE)
        a = xs[at, m * 256:m * 256 + 128].astype(F32)
        b = xs[at, m * 256 + 128:m * 256 + 256].astype(F32)
        upper, lower = pltpu.roll(a, 64, 1), pltpu.roll(b, 64, 1)
        return jnp.where(low, jnp.where(yh == 0, a, upper), jnp.where(yh == 0, lower, b))

    for part in range(PARTS):
        for m in range(4):
            fresh[part, m] = pair(m, part)
    for copy in sums:
        copy.wait_recv()
    factor = lax.rsqrt(jnp.sum(squares[...], axis=0) * (1.0 / D) + EPS)
    starts, so_far = [], 0
    for j in range(16):
        starts.append(so_far)
        so_far = so_far + new_ref[j]
    here = pl.ds(x * 2, 2)
    over_x = []
    for part in range(PARTS):
        rows_of = slice(part * WIDE, part * WIDE + WIDE)
        for m in range(4):
            value = total[rows_of, m * 128:(m + 1) * 128] * factor[m:m + 1, :] * gain[rows_of, :]
            fresh[part, m] = fresh[part, m] + value
        for n in range(8):
            sides = []
            for side in range(2):
                j = 2 * n + side
                within = lax.rem(x - starts[j] + 64, 4)
                i = jnp.minimum(lax.div(starts[j] + within - x, 4), 7)
                at = lax.div(i, 2)
                place = lax.rem(i + at, 2) * 4 + at
                value = fresh[part, lax.div(place, 2)]
                value = jnp.where(lax.rem(place, 2) == side, value, pltpu.roll(value, 64, 1))
                sides.append(jnp.where(within < new_ref[j], value, 0.0))
            f1[part, n] = jnp.where(low, sides[0], sides[1]).astype(BF)
        f1_got[part][here] = f1[part, here]
        for d, peer in enumerate(others):
            n = part * 3 + d
            copy = copy_to(f1.at[part, pl.ds(peer["x"] * 2, 2)], f1_got[part].at[here], s_f.at[n], r_f.at[n], peer)
            copy.start()
            over_x.append(copy)
    mine = [sum([jnp.where(x * 4 + n > m, new_ref[m], 0) for m in range(15)]) for n in range(4)]
    out, swap = [], []
    for part in range(PARTS):
        rows_of = slice(part * WIDE, part * WIDE + WIDE)
        for copy in over_x[part * 3:part * 3 + 3]:
            copy.wait_recv()
        for e in range(8):
            n = part * 8 + e
            dz, dy = e // 2, e % 2
            tz, ty = lax.rem(z + dz, 4), yl + dy - 2 * yl * dy
            sides = []
            for side in range(2):
                start = jnp.where(ty == 0, mine[side], mine[2 + side])
                sides.append(f1_got[part][lax.rem(start + tz, 4) * 2 + ty].astype(F32))
            value = jnp.where(low, sides[0], sides[1]).astype(BF)
            at = (z * 2 + yl) * 2 + c
            if e == 0:
                fin[at, rows_of, :] = value
            else:
                f2[part, e] = value
                copy = copy_to(f2.at[part, e], fin.at[at, rows_of], s_g.at[n], r_g.at[n], {"z": tz, "yl": ty})
                copy.start()
                out.append(copy)
    for part in range(PARTS):
        rows_of = slice(part * WIDE, part * WIDE + WIDE)
        for e in range(8):
            n = part * 8 + e
            dz, dy = e // 2, e % 2
            at = (mod4(z - dz) * 2 + yl + dy - 2 * yl * dy) * 2 + c
            ref = fin.at[at, rows_of]
            if e > 0:
                copy_to(ref, ref, s_g.at[n], r_g.at[n], core).wait_recv()
            copy = copy_to(ref, ref, s_c.at[n], r_c.at[n], core)
            copy.start()
            swap.append(copy)
    for copy in swap:
        copy.wait_recv()
    first.sent()
    second.sent()
    for copy in list(hop.values()) + list(pass_hop.values()) + last + sums + over_x + out + swap:
        copy.wait_send()


STAGE_IN = [
    VM((1152, 512), BF), VM((1152, 256), BF), VM((1152, 256), BF),
    VM((1152, 128), F32), VM((128, 128), F32), VM((64, 512), F32), VM((64, 512), F32),
    VM((576, 512), BF), VM((PARTS, 8, WIDE, 128), BF), VM((24, WIDE, 128), BF), VM((24, WIDE, 128), BF), VM((24, WIDE, 128), BF), VM((1152, 1024), BF), VM((16, 8, 128), F32),
    VM((2, 512, 512), F32), VM((2, 512, 512), F32), VM((512, 512), BF), VM((512, 512), BF), VM((2, 512, 512), F32),
    DMA((6,)), DMA((8 * PARTS,)), DMA((8 * PARTS,)), DMA((8 * PARTS,)), DMA((8 * PARTS,)), DMA((8 * PARTS,)), DMA((8 * PARTS,)),
    DMA((18,)), DMA((18,)), DMA((6,)), DMA((6,)), DMA((6 * PARTS,)), DMA((6 * PARTS,)), DMA((16,)), DMA((16,)),
    DMA((6,)), DMA((6,)), DMA((6,)), DMA((6,)),
]
STAGE_ATTEND = [
    VM((4, 256, 128), BF), VM((4, 256, 128), F32), VM((4, 256, 128), F32),
    DMA((4,)), DMA((4,)), DMA((8,)), DMA((8,)),
]
STAGE_OUT = (
    [VM((2, 2, OUT[0], 512), BF), VM((2, 2, OUT[0], 512), BF), VM((2, OUT[0], 512), BF), VM((2, OUT[0], 512), BF)]
    + [VM((2, 2, OUT[1], 256), BF), VM((2, 2, OUT[1], 256), BF), VM((2, OUT[1], 256), BF), VM((2, OUT[1], 256), BF)]
    + [VM((4, OUT[1], 512), BF)] * 3
    + [VM((OUT[0], 512), BF)] * 3
    + [VM((2, 4, OUT[0], 512), F32), VM((4, OUT[1], 512), F32), VM((288, 512), F32)]
    + [VM((16, 4, 128), F32), VM((PARTS, 4, WIDE, 128), F32)]
    + [VM((PARTS, 8, WIDE, 128), BF)] * 2
    + [VM((8, WIDE, 128), BF)] * PARTS
    + [DMA((4,)), DMA((4,)), DMA((2,)), DMA((2,))] * 2
    + [DMA((8,)), DMA((8,)), DMA((4,)), DMA((4,)), DMA((16,)), DMA((16,)), DMA((3 * PARTS,)), DMA((3 * PARTS,))]
    + [DMA((8 * PARTS,))] * 4
)
SHARED = [
    VM((256, 512), BF), VM((4, 256, 128), BF), VM((1152, 1024), BF), VM((1152, 512), BF), VM((16, 64, 512), BF),
    VM((288, 128), F32), VM((8, 256, 512), BF), DMA((12,)), DMA((12,)), DMA((4,)), DMA((4,)),
]


def kernel(old_ref, new_ref, order_ref, xt_in, pre_ref, post_ref, wq_in, wk_in, wv_in, wo_in, fin, *scratch):
    q, kv, xs, wo, ctx, gain_out, kvs, s_x, r_x, s_c, r_c = scratch[:11]
    scratch = scratch[11:]
    keys_values = KeysValues(kv, kvs, s_x, r_x, s_c, r_c)
    own_in, scratch = scratch[:len(STAGE_IN)], scratch[len(STAGE_IN):]
    own_attend, own_out = scratch[:len(STAGE_ATTEND)], scratch[len(STAGE_ATTEND):]
    end_in = stage_in(
        old_ref, order_ref, xt_in, pre_ref, post_ref, wq_in, wk_in, wv_in, wo_in, q, kv, xs, wo, gain_out, *own_in,
        keys_values,
    )
    end_attend = stage_attend(q, ctx, keys_values, kvs, *own_attend)
    end_in()
    stage_out(new_ref, ctx, xs, wo, gain_out, fin, *own_out)
    end_attend()


def run(old_blocks, new_blocks, order, xt, pre_gain, post_gain, w_query, w_key, w_value, w_out_t):
    smem = pl.BlockSpec(memory_space=pltpu.SMEM)
    vmem = pl.BlockSpec(memory_space=pltpu.VMEM)
    hbm = pl.BlockSpec(memory_space=pltpu.HBM)
    return pl.pallas_call(
        kernel,
        name="sublayer",
        out_shape=jax.ShapeDtypeStruct((16, 288, 128), BF),
        in_specs=[smem, smem, smem, hbm, vmem, vmem, hbm, hbm, hbm, hbm],
        out_specs=vmem,
        scratch_shapes=SHARED + STAGE_IN + STAGE_ATTEND + STAGE_OUT,
        compiler_params=pltpu.CompilerParams(collective_id=0, has_side_effects=True, vmem_limit_bytes=62 * 2**20),
    )(old_blocks, new_blocks, order, xt, pre_gain, post_gain, w_query, w_key, w_value, w_out_t)


def per_device(
    x_old, old_blocks, new_blocks, order, pre_gain, post_gain, w_query, w_key, w_value, w_out_t
):
    c = lax.axis_index("c")
    fin = run(
        old_blocks, new_blocks, order, x_old.T, pre_gain.reshape(36, 128), post_gain.reshape(36, 128),
        w_query, w_key, w_value, w_out_t,
    )
    return lax.dynamic_slice(fin, (0, 0, c * 64), (16, 288, 64)).reshape(4608, 64).T


def solution(mesh):
    torus = Mesh(mesh.devices.reshape(4, 2, 2, 4, 2), ("x", "yl", "c", "z", "yh"))
    seq, tp = ("x", "yl", "c"), ("z", "yh")
    both = P(seq, tp)
    in_specs = (both, P(), P(), P(), P(), P(), both, both, both, both)
    return jax.shard_map(
        per_device, mesh=torus, in_specs=in_specs, out_specs=P(seq + tp, None), check_vma=False
    )
```

time: 138 us -> 125 us (0.906)
  Pallas kernels: 135 us -> 121 us
    pallas_call x1, Pallas kernels: 135 us -> 121 us  [run(): pl.pallas_call(kernel, name='sublayer', out_shape=jax.ShapeDtypeStruct((1...]
where the time goes in v3:
time: 125 us; the launch traced here: 124 us
  Pallas kernels  121 us (97%)
  local copies, waits for them, and re-layouts  2.94 us (2%)
    pallas_call x1, Pallas kernels, run(): pl.pallas_call(kernel, name='sublayer', out_shape=jax.ShapeDtypeStruct((1...  121 us

profile of v3, /device:TPU:1, one launch (start us, length us, event | category | flops | bytes accessed | tf_op | source)
XLA Modules:
  0.0 124.3 jit_solution(14976889524249838665)
XLA Ops:
  0.0 121.4 %sublayer.1 = bf16[16,288,128]{2,1,0:T(8,128)(2,1)} custom-call(s32[16]{0:T(128)} %old_ref.1, s32[16]{0:T(128)} %new_ref.1, s32[16]{0:T(128)} %order_ref.1, bf16[576,512]{1,0:T(8,128)(2,1)} %bitcast.6, f32[36,128]{1,0:T(8,128)} %bitcast.7, f32[36,128]{1,0:T(8,128)} %bitcast.8, bf16[288,512]{1,0:T(8,128)(2,1)} %wq_in.1, bf16[288,256]{1,0:T(8,128)(2,1)} %wk_in.1, ...), custom_call_target="tpu_custom_call" | custom-call | tf_op jit(solution)/shard_map/sublayer/pallas_call | solution.py:797
  121.4 1.7 %constant_dynamic-slice_fusion = bf16[16,288,64]{2,1,0:T(8,128)(2,1)S(1)} fusion(bf16[16,288,128]{2,1,0:T(8,128)(2,1)} %sublayer.1, s32[]{:T(128)S(6)} %select_n.3), kind=kLoop, calls=%fused_computation | loop fusion | bytes 1179652 | tf_op jit(solution)/shard_map/dynamic_slice | solution.py:816
  123.0 1.3 %copy.12 = bf16[4608,64]{0,1:T(8,128)(2,1)} copy(bf16[4608,64]{1,0:T(8,128)(2,1)S(1)} %bitcast.5) | data formatting | bytes 1179648 | tf_op jit(solution)/shard_map/reshape | solution.py:816

commit v4 on v3

v4 whole, which is shorter than its diff:
```python
import functools
import math

import jax
import jax.numpy as jnp
from jax import lax
from jax.experimental import pallas as pl
from jax.experimental.pallas import tpu as pltpu
from jax.sharding import Mesh
from jax.sharding import PartitionSpec as P

D = 4608
HEADS = 32
HEAD = 128
BLOCK = 128
EPS = 1e-06
BF = jnp.bfloat16
F32 = jnp.float32
VM = pltpu.VMEM
OUT = (160, 128)
PARTS = 3
WIDE = 288 // PARTS
DMA = pltpu.SemaphoreType.DMA


def kept(at, c):
    return 2 * at + lax.rem(at + c, 2)


def coords():
    return tuple(lax.axis_index(name) for name in ("x", "yl", "c", "z", "yh"))


def copy_to(src, dst, send_sem, recv_sem, device):
    return pltpu.make_async_remote_copy(
        src_ref=src,
        dst_ref=dst,
        send_sem=send_sem,
        recv_sem=recv_sem,
        device_id=device,
        device_id_type=pl.DeviceIdType.MESH,
    )


def greet(devices):
    sem = pltpu.get_barrier_semaphore()
    for device in devices:
        pl.semaphore_signal(sem, inc=1, device_id=device, device_id_type=pl.DeviceIdType.MESH)


def greeted(devices):
    pl.semaphore_wait(pltpu.get_barrier_semaphore(), len(devices))


def mod4(v):
    return lax.rem(v + 4, 4)


def arrived(ref, sem):
    copy_to(ref, ref, sem, sem, {"c": 1 - lax.axis_index("c")}).wait_recv()


def gone(ref, sem):
    copy_to(ref, ref, sem, sem, {"c": 1 - lax.axis_index("c")}).wait_send()


class Gather4:
    def __init__(self, views, axis, me, send, recv, size):
        one, two = me + 1 - 2 * lax.rem(me, 2), 3 - me
        far = two + 1 - 2 * lax.rem(two, 2)
        self.moves = [
            (me, one, 0, one),
            (me, two, 1, two),
            (me, two, 0, two),
            (me, one, 1, one),
            (one, far, 0, two),
            (two, far, 1, one),
        ]
        self.views, self.axis, self.send, self.recv, self.size = views, axis, send, recv, size

    def go(self, *moves):
        for move in moves:
            sent, _, half, partner = self.moves[move]
            for view in self.views:
                ref = view(sent, half)
                copy_to(ref, ref, self.send(move // 4), self.recv(move // 2), {self.axis: partner}).start()

    def start(self):
        self.go(0, 1, 2, 3)

    def relay(self):
        arrived(self.size(2), self.recv(0))
        self.go(4, 5)

    def near(self):
        arrived(self.size(2), self.recv(1))

    def far(self):
        arrived(self.size(2), self.recv(2))

    def sent(self):
        gone(self.size(4), self.send(0))
        gone(self.size(2), self.send(1))


def some(sems, start):
    return lambda n: sems.at[start + n]


def rows(ref, start, size, unit=16):
    return ref.at[pl.ds(pl.multiple_of(start, unit), size)]


def lanes(start, size):
    return pl.ds(pl.multiple_of(start, 128), size)


def columns(dst, table, chunk_of, count):
    lane = lax.broadcasted_iota(jnp.int32, (32, 128), 1)

    def body(n, _):
        feature = chunk_of(lax.div(n, 9)) * 288 + lax.rem(n, 9) * 32
        part = table[pl.ds(pl.multiple_of(lax.rem(feature, 128), 32), 32), :]
        value = jnp.sum(jnp.where(lane == lax.div(feature, 128), part, 0.0), axis=1, keepdims=True)
        dst[pl.ds(pl.multiple_of(n * 32, 32), 32), :] = jnp.broadcast_to(value, (32, 128))
        return 0

    lax.fori_loop(0, count * 9, body, 0)


def stage_in(
    old_ref, order_ref, xt_in, pre_ref, post_ref, wq_in, wk_in, wv_in, wo_in,
    q_out, kv_out, xs, wo, gain_out,
    wq, wk, wv, gain, table, cos, sin, xt, slots, landed_0, landed_1, landed_2, normed, squares, near, other, to_y, from_y, mine,
    s_w, s_one, r_one, s_two, r_two, s_three, r_three, s_wg, r_wg, s_og, r_og, s_z, r_z, s_q, r_q, s_c, r_c, s_y, r_y,
    keys_values,
):
    x, yl, c, z, yh = coords()
    landed = (landed_0, landed_1, landed_2)
    ring_peers = [
        {"x": lax.rem(x + dx, 4), "c": c + dc - 2 * c * dc} for dx in range(4) for dc in range(2)
    ][1:]
    y_one = {"yl": 1 - yl}
    y_two = {"yl": 1 - yl, "yh": 1 - yh}
    group = [
        {"z": lax.rem(z + dz, 4), "yl": yl + dy - 2 * yl * dy, "c": c + dc - 2 * c * dc}
        for dz in range(4) for dy in range(2) for dc in range(2)
    ][1:]
    greet(ring_peers + [y_two] + group)
    into = pltpu.make_async_copy(xt_in, xt, s_w.at[1])
    into.start()
    at = pl.ds(pl.multiple_of(x * 288, 16), 288)
    owns = [
        pltpu.make_async_copy(src, dst.at[at], s_w.at[0]) for src, dst in ((wq_in, wq), (wk_in, wk), (wv_in, wv))
    ]

    def out_rows(chunk, half):
        return rows(wo, half * 4 * OUT[0] + chunk * OUT[half], OUT[half])

    for half in range(2):
        part = wo_in.at[pl.ds(half * OUT[0], OUT[half])]
        owns.append(pltpu.make_async_copy(part, out_rows(x, half), s_w.at[0]))
    for copy in owns:
        copy.start()
    starts, total = [], 0
    for m in range(16):
        starts.append(total)
        total = total + old_ref[m]
    k = order_ref[x * 4 + yl * 2 + c]
    first = sum([jnp.where(k > m, old_ref[m], 0) for m in range(15)])
    into.wait()
    for r in range(4):
        b = lax.rem(r - first + 64, 4)
        for h in range(2):
            for half in range(PARTS):
                at_rows = slice(h * 288 + half * WIDE, h * 288 + half * WIDE + WIDE)
                part = [xt[at_rows, n * 128:(n + 1) * 128] for n in range(4)]
                low = jnp.where(b == 0, part[0], part[1])
                slots[half, r * 2 + h] = jnp.where(b < 2, low, jnp.where(b == 2, part[2], part[3]))
    here = x * 2 + c
    for half in range(PARTS):
        landed[half][here] = slots[half, here]
    greeted(ring_peers + [y_two] + group)
    for half in range(PARTS):
        for d, peer in enumerate(ring_peers, 1):
            copy_to(
                slots.at[half, peer["x"] * 2 + peer["c"]], landed[half].at[here],
                s_one.at[half], r_one.at[half * 4 + d // 2], peer,
            ).start()
    everything = wo.at[pl.ds(0, 864)]
    pltpu.make_async_copy(everything, everything, s_w.at[0]).wait()

    def half_rows(ref):
        return lambda chunk, half: rows(ref, chunk * 288 + half * 144, 144)

    weights = Gather4(
        [half_rows(r) for r in (wq, wk, wv)], "x", x, some(s_wg, 0), some(r_wg, 0), lambda n: wq.at[pl.ds(0, 288 * n)]
    )
    weights.start()
    straight = yl == yh

    def slot_pair(half, dx, where):
        return landed[half].at[pl.ds(where * 8 + mod4(x - dx) * 2, 2)]

    def relay_y(n):
        half, dx = n // 4, n % 4
        arrived(slot_pair(half, dx, 1), r_two.at[n])
        copy = copy_to(slot_pair(half, dx, 1), slot_pair(half, dx, 2), s_three.at[half], r_three.at[half], y_one)
        pl.when(straight)(copy.start)

    for half in range(PARTS):
        for dx in range(4):
            n = half * 4 + dx
            from_x = slot_pair(half, dx, 0) if dx > 0 else landed[half].at[x * 2 + 1 - c]
            arrived(from_x, r_one.at[n])
            copy_to(slot_pair(half, dx, 0), slot_pair(half, dx, 1), s_two.at[half], r_two.at[n], y_two).start()
            copy = copy_to(slot_pair(half, dx, 0), slot_pair(half, dx, 2), s_three.at[half], r_three.at[half], y_one)
            pl.when(jnp.logical_not(straight))(copy.start)
            if half == 2:
                relay_y(dx)
    me = z * 4 + yl * 2 + c
    first_buffer = jnp.where(straight, 0, 1)

    def part_rows(part):
        return lambda chunk, half: rows(xs, chunk * 288 + part * WIDE + half * (WIDE // 2), WIDE // 2)

    gathers = [
        Gather4(
            [part_rows(part)], "z", z, some(s_z, 2 * part), some(r_z, 3 * part),
            lambda n: xs.at[pl.ds(0, (WIDE // 2) * n)],
        )
        for part in range(PARTS)
    ]
    sources = []
    for place in range(8):
        g = x + 4 * kept(place % 4, place // 4)
        shard = sum([jnp.where(starts[m] <= g, 1, 0) for m in range(16)]) - 1
        holder = sum([jnp.where(order_ref[p] == shard, p, 0) for p in range(16)])
        y_source = lax.rem(lax.div(holder, 2), 2)
        sources.append(jnp.where(y_source == yh, first_buffer, 2) * 8 + lax.div(holder, 4) * 2 + lax.rem(holder, 2))

    def pick(half):
        arrived(landed[half].at[pl.ds(16, 8)], r_three.at[half])
        for place in range(8):
            block = landed[half][sources[place]]
            xs[pl.ds(pl.multiple_of(z * 288 + half * WIDE, 32), WIDE), place * 128:(place + 1) * 128] = block
            wide = block.astype(F32)
            square = jnp.sum(wide * wide, axis=0, keepdims=True)
            if half > 0:
                square = square + squares[me, place:place + 1, :]
            squares[me, place:place + 1, :] = square
        gathers[half].start()

    for n in range(4, 12):
        if n in (6, 10):
            pick((n - 6) // 4)
        relay_y(n)
    pick(2)
    weights.relay()
    wo_all = Gather4(
        [out_rows], "x", x, some(s_og, 0), some(r_og, 0), lambda n: wo.at[pl.ds(0, 144 * n)]
    )
    wo_all.start()
    for peer in group:
        copy_to(squares.at[me], squares.at[me], s_q.at[0], r_q.at[0], peer).start()
    table[...] = jnp.zeros_like(table)
    table[0:36, :] = pre_ref[...]
    table[...] = table[...].T
    columns(gain, table, lambda n: n * 4 + yl * 2 + c, 4)
    table[...] = jnp.zeros_like(table)
    table[0:36, :] = post_ref[...]
    table[...] = table[...].T
    columns(gain_out, table, lambda n: z * 4 + yl * 2 + c, 1)
    gathers[0].relay()
    half_head = HEAD // 2
    inverse = jnp.exp(
        lax.broadcasted_iota(jnp.int32, (half_head, 128), 0).astype(F32) * (-2.0 * math.log(10000.0) / HEAD)
    )
    for p in range(4):
        place_of = (x + 4 * kept(p, c)) * BLOCK + lax.broadcasted_iota(jnp.int32, (half_head, 128), 1)
        angle = inverse * place_of.astype(F32)
        cos[:, p * 128:(p + 1) * 128] = jnp.cos(angle)
        sin[:, p * 128:(p + 1) * 128] = jnp.sin(angle)
    for part in (1, 2):
        gathers[part].relay()
    arrived(squares.at[pl.ds(0, 15)], r_q.at[0])
    factor = lax.rsqrt(jnp.sum(squares[...], axis=0) * (1.0 / D) + EPS)

    def norm(chunk):
        for place in range(8):
            scale = factor[place:place + 1, :]

            def norm_rows(n, _, place=place, scale=scale):
                part = pl.ds(pl.multiple_of(chunk * 288 + n * 144, 16), 144)
                at = (part, slice(place * 128, (place + 1) * 128))
                normed[at] = (xs[at].astype(F32) * scale * gain[part, :]).astype(BF)
                return 0

            lax.fori_loop(0, 2, norm_rows, 0)

    pieces = {"q": (slice(0, 256), wq, 256), "k": (slice(256, 384), wk, 128), "v": (slice(384, 512), wv, 128)}

    def corner(dst, y, core, late, names="qkv"):
        low = lax.div(z, 2)
        part = pl.ds(pl.multiple_of((1 - low if late else low) * 576, 16), 576)
        right = normed[part, lanes(core * 512, 512)]
        for name in names:
            to, table_of, width = pieces[name]
            left = table_of[part, lanes(y * width, width)]
            value = lax.dot_general(left, right, (((0,), (0,)), ((), ())), preferred_element_type=F32)
            if late:
                dst[to, :] += value
            else:
                dst[to, :] = value

    norm(z)
    for one_part in gathers:
        one_part.near()
    norm(z + 1 - 2 * lax.rem(z, 2))
    weights.near()
    weights.far()
    corners = [
        (near.at[0], 1 - yl, 1 - c), (mine.at[0], 1 - yl, c), (near.at[1], yl, 1 - c), (mine.at[1], yl, c),
    ]
    for dst, y, core in corners:
        corner(dst, y, core, False)
    norm(3 - z)
    wo_all.relay()
    for one_part in gathers:
        one_part.far()
    far = 3 - z
    norm(far + 1 - 2 * lax.rem(far, 2))
    core = {"c": 1 - c}

    def over_core(n, name):
        to = pieces[name][0]
        recv = r_c.at["kvq".index(name) if n == 0 else 3]
        copy_to(near.at[n, to], other.at[n, to], s_c.at[0], recv, core).start()

    first_rows, last_rows = slice(0, 256), slice(256, 512)
    k_part, v_part = slice(256, 384), slice(384, 512)
    spans = (
        (0, k_part, first_rows), (1, v_part, first_rows), (2, k_part, last_rows), (3, v_part, last_rows),
        (4, slice(0, 256), first_rows), (5, slice(0, 256), last_rows),
    )

    def over_y(name):
        to = pieces[name][0]
        arrived(other.at[0, to], r_c.at["kvq".index(name)])
        to_y[to, :] = (mine[0, to, :] + other[0, to, :]).astype(BF)
        for at, part, cols in {"k": spans[:1], "v": spans[1:4], "q": spans[4:]}[name]:
            copy_to(to_y.at[part, cols], from_y.at[part, cols], s_y.at[0], r_y.at[at // 2 if at < 4 else at - 2], y_one).start()

    for name in "kv":
        corner(*corners[0], True, name)
        over_core(0, name)
    corner(*corners[1], True, "kv")
    over_y("k")
    corner(*corners[0], True, "q")
    over_core(0, "q")
    over_y("v")
    corner(*corners[1], True, "q")
    over_y("q")
    corner(*corners[2], True)
    for name in "kvq":
        over_core(1, name)
    corner(*corners[3], True)
    arrived(other.at[1], r_c.at[3])
    scale_q = (D // HEADS) ** (-0.5)

    def summed(part, cols):
        return mine[1, part, cols] + other[1, part, cols] + from_y[part, cols].astype(F32)

    def turned(value, cols):
        a, b = value[:64], value[64:]
        return jnp.concatenate(
            [a * cos[:, cols] - b * sin[:, cols], b * cos[:, cols] + a * sin[:, cols]], axis=0
        ).astype(BF)

    for late, cols in enumerate((first_rows, last_rows)):
        arrived(from_y.at[pl.ds(256, 256), cols], r_y.at[late])
        key = turned(summed(k_part, cols), cols)
        value = summed(v_part, cols).astype(BF)
        for p in range(2):
            kv_out[2 * late + p, :128, :] = key[:, p * 128:(p + 1) * 128]
            kv_out[2 * late + p, 128:, :] = value[:, p * 128:(p + 1) * 128]
        keys_values.send(late)
    for late in range(2):
        keys_values.gathers[late].relay()
    for late, cols in enumerate((first_rows, last_rows)):
        arrived(from_y.at[pl.ds(0, 256), cols], r_y.at[2 + late])
        for h in range(2):
            part = slice(h * 128, (h + 1) * 128)
            a, b = summed(slice(h * 128, h * 128 + 64), cols), summed(slice(h * 128 + 64, h * 128 + 128), cols)
            turn_a = a * cos[:, cols] - b * sin[:, cols]
            turn_b = b * cos[:, cols] + a * sin[:, cols]
            q_out[part, cols] = (jnp.concatenate([turn_a, turn_b], axis=0) * scale_q).astype(BF)

    def finish():
        wo_all.near()
        wo_all.far()
        for half in range(PARTS):
            gone(slots.at[half, pl.ds(0, 7)], s_one.at[half])
            gone(landed[half].at[pl.ds(0, 8)], s_two.at[half])
            gone(landed[half].at[pl.ds(0, 8)], s_three.at[half])
        gone(squares.at[pl.ds(0, 15)], s_q.at[0])
        gone(near, s_c.at[0])
        gone(to_y, s_y.at[0])
        weights.sent()
        wo_all.sent()
        for one_part in gathers:
            one_part.sent()

    return finish


class KeysValues:
    def __init__(self, kv_ref, kvs, s_x, r_x, s_c, r_c):
        x, _, c, _, _ = coords()

        def block(late):
            return lambda chunk, half: kvs.at[kept(2 * late + half, c), :, lanes(chunk * 128, 128)]

        self.gathers = [
            Gather4(
                [block(late)], "x", x, some(s_x, 2 * late), some(r_x, 3 * late),
                lambda n: kvs.at[0, :, pl.ds(0, 128 * n)],
            )
            for late in range(2)
        ]
        self.kv_ref, self.kvs, self.s_c, self.r_c = kv_ref, kvs, s_c, r_c

    def send(self, late):
        x, _, c, _, _ = coords()
        for p in (2 * late, 2 * late + 1):
            self.kvs[kept(p, c), :, lanes(x * 128, 128)] = self.kv_ref[p]
        self.gathers[late].start()

    def to_core(self, late):
        _, _, c, _, _ = coords()
        self.gathers[late].near()
        self.gathers[late].far()
        for p in (2 * late, 2 * late + 1):
            ref = self.kvs.at[kept(p, c)]
            copy_to(ref, ref, self.s_c.at[0], self.r_c.at[late], {"c": 1 - c}).start()

    def from_core(self, late):
        arrived(self.kvs.at[pl.ds(0, 2)], self.r_c.at[late])

    def sent(self):
        gone(self.kvs.at[pl.ds(0, 4)], self.s_c.at[0])
        for gather in self.gathers:
            gather.sent()


def stage_attend(q_ref, ctx, keys_values, kvs, qs, acc, den, s_y, r_y, s_o, r_o):
    x, yl, c, z, yh = coords()
    core, y_one = {"c": 1 - c}, {"yl": 1 - yl}
    for p in range(4):
        for h in range(2):
            part = q_ref[h * 128:(h + 1) * 128, p * 128:(p + 1) * 128].astype(F32)
            qs[p, h * 128:(h + 1) * 128, :] = part.T.astype(BF)
    acc[...] = jnp.zeros_like(acc)
    den[...] = jnp.zeros_like(den)
    keys_values.to_core(0)

    def tiles(pairs, core_at, diagonal=()):
        pairs = [(p, kept(e, core_at), n in diagonal) for n, (p, e) in enumerate(pairs)]
        scores = [jnp.dot(qs[p], kvs[group, :128, :], preferred_element_type=F32) for p, group, _ in pairs]
        for (p, group, masked), score in zip(pairs, scores):
            weight = jnp.exp2((50.0 * math.log2(math.e)) * jnp.tanh(score * (1.0 / 50.0)))
            if masked:
                row = lax.rem(lax.broadcasted_iota(jnp.int32, (256, 512), 0), 128)
                col = lax.broadcasted_iota(jnp.int32, (256, 512), 1)
                weight = jnp.where(col - row <= x * 128, weight, 0.0)
            den[p] += sum([weight[:, n:n + 128] for n in range(0, 512, 128)])
            acc[p] += lax.dot_general(
                weight.astype(BF), kvs[group, 128:, :], (((1,), (1,)), ((), ())), preferred_element_type=F32
            )

    def region(core_at, y_at, at, size):
        return ctx.at[pl.ds(at + core_at * 4, size), :, lanes(y_at * 256, 256)]

    def put(step):
        for p in (2 * step, 2 * step + 1):
            for h in range(2):
                part = slice(h * 128, (h + 1) * 128)
                total = jnp.sum(den[p, part, :], axis=1, keepdims=True)
                value = (acc[p, part, :] / total).astype(BF)
                cols = lanes(yl * 256 + h * 128, 128)
                ctx[c * 4 + p, :, cols] = value[:64]
                ctx[8 + c * 4 + p, :, cols] = value[64:]
        for half in range(2):
            ref = region(c, yl, half * 8 + 2 * step, 2)
            copy_to(ref, ref, s_y.at[0], r_y.at[step], y_one).start()
            copy_to(ref, ref, s_o.at[0], r_o.at[0], core).start()

    def pass_on(step):
        arrived(ctx.at[pl.ds(0, 4), :, pl.ds(0, 256)], r_y.at[step])
        for half in range(2):
            ref = region(c, 1 - yl, half * 8 + 2 * step, 2)
            copy_to(ref, ref, s_o.at[0], r_o.at[0], core).start()

    tiles([(0, 0), (1, 0), (1, 1)], c, (0, 2))
    keys_values.from_core(0)
    tiles([(1 - c, 0), (1, 1 - c)], 1 - c)
    put(0)
    tiles([(2, 0), (2, 1), (3, 0), (3, 1)], c)
    keys_values.to_core(1)
    tiles([(2, 0), (2, 1), (3, 0), (3, 1)], 1 - c)
    tiles([(2, 2), (3, 2), (3, 3)], c, (0, 2))
    keys_values.from_core(1)
    tiles([(3 - c, 2), (3, 3 - c)], 1 - c)
    put(1)
    pass_on(0)
    pass_on(1)
    arrived(ctx.at[:, :, pl.ds(0, 256)], r_o.at[0])

    def finish():
        gone(ctx.at[pl.ds(0, 8), :, pl.ds(0, 256)], s_y.at[0])
        gone(ctx.at[:, :, pl.ds(0, 256)], s_o.at[0])
        keys_values.sent()

    return finish


class Reduce4:
    def __init__(self, z, send, got, more, more_got, s, r):
        self.one, self.two = z + 1 - 2 * lax.rem(z, 2), 3 - z
        self.far = self.two + 1 - 2 * lax.rem(self.two, 2)
        self.send, self.got, self.more, self.more_got, self.s, self.r = send, got, more, more_got, s, r

    def partner(self, part, step):
        return {"z": self.one if part == step else self.two}

    def chunk(self, part, slot):
        return self.far if slot == 1 else (self.two if part else self.one)

    def give(self, part, slot, value):
        self.send[part, slot] = value
        copy_to(
            self.send.at[part, slot], self.got.at[part, slot], self.s.at[0], self.r.at[slot], self.partner(part, 0)
        ).start()

    def pass_on(self, values):
        arrived(self.got.at[0], self.r.at[1])
        for part, value in enumerate(values):
            self.more[part] = (value + self.got[part, 1].astype(F32)).astype(BF)
            copy_to(
                self.more.at[part], self.more_got.at[part], self.s.at[1], self.r.at[2], self.partner(part, 1)
            ).start()

    def own(self, values):
        arrived(self.got.at[0], self.r.at[0])
        arrived(self.more_got, self.r.at[2])
        return [
            value + self.got[part, 0].astype(F32) + self.more_got[part].astype(F32) for part, value in enumerate(values)
        ]

    def sent(self):
        gone(self.send, self.s.at[0])
        gone(self.more, self.s.at[1])


def stage_out(
    new_ref, ctx, xs, wo, gain, fin,
    a_send, a_got, a_more, a_more_got, b_send, b_got, b_more, b_more_got,
    y_send, y_relay, y_got, h_send, h_relay, h_got, own_a, own_b, total,
    squares, fresh, f1, f2, f1_got_0, f1_got_1, f1_got_2,
    a_s, a_r, b_s, b_r, s_y, r_y, s_h, r_h, s_q, r_q, s_f, r_f, s_g, r_g, s_c, r_c,
):
    x, yl, c, z, yh = coords()
    core = {"c": 1 - c}
    y_one, y_two = {"yl": 1 - yl}, {"yl": 1 - yl, "yh": 1 - yh}
    group = [
        {"z": lax.rem(z + dz, 4), "yl": yl + dy - 2 * yl * dy, "c": c + dc - 2 * c * dc}
        for dz in range(4) for dy in range(2) for dc in range(2)
    ][1:]
    others = [{"x": lax.rem(x + dx, 4)} for dx in range(1, 4)]
    f1_got = (f1_got_0, f1_got_1, f1_got_2)

    def sums_of(half, part):
        left = wo[part * 4 * OUT[0]:part * 4 * OUT[0] + 4 * OUT[part], :]
        right = ctx[pl.ds(half * 8, 8)].reshape(512, 512)
        value = lax.dot_general(left, right, (((1,), (1,)), ((), ())), preferred_element_type=F32)
        return value.reshape(4, OUT[part], 512)

    y_send[...] = sums_of(1 - yh, 1).astype(BF)
    for n in range(4):
        copy_to(y_send.at[n], y_relay.at[n], s_y.at[0], r_y.at[n // 2], y_two if n % 2 else y_one).start()
    first = Reduce4(z, a_send, a_got, a_more, a_more_got, a_s, a_r)
    for part in range(2):
        own_a[part] = sums_of(part, 0)
        first.give(part, 1, own_a[part, first.chunk(part, 1)].astype(BF))
    for part in range(2):
        first.give(part, 0, own_a[part, first.chunk(part, 0)].astype(BF))
    own_b[...] = sums_of(yh, 1)

    def forward(step):
        arrived(y_relay.at[pl.ds(0, 2)], r_y.at[step])
        for n in (2 * step, 2 * step + 1):
            copy_to(y_relay.at[n], y_got.at[n], s_y.at[1], r_y.at[2], y_one if n % 2 else y_two).start()

    forward(0)
    first.pass_on([own_a[0, first.two], own_a[1, first.one]])
    forward(1)
    for part, value in enumerate(first.own([own_a[0, z], own_a[1, z]])):
        own_a[part, z] = value
    h_send[...] = own_a[1 - yh, z].astype(BF)
    spans = (slice(0, 80), slice(80, OUT[0]))
    for n, peer in enumerate((y_one, y_two)):
        copy_to(h_send.at[spans[n]], h_relay.at[spans[n]], s_h.at[0], r_h.at[0], peer).start()
    second = Reduce4(z, b_send, b_got, b_more, b_more_got, b_s, b_r)
    arrived(y_got, r_y.at[2])
    own_b[...] = own_b[...] + y_got[...].astype(F32)
    cols = (slice(0, 256), slice(256, 512))
    for slot in (1, 0):
        for part in range(2):
            second.give(part, slot, own_b[second.chunk(part, slot), :, cols[part]].astype(BF))
    arrived(h_relay, r_h.at[0])
    for n, peer in enumerate((y_two, y_one)):
        copy_to(h_relay.at[spans[n]], h_got.at[spans[n]], s_h.at[1], r_h.at[1], peer).start()
    second.pass_on([own_b[second.two, :, cols[0]], own_b[second.one, :, cols[1]]])
    for part, value in enumerate(second.own([own_b[z, :, cols[0]], own_b[z, :, cols[1]]])):
        total[OUT[0]:, cols[part]] = value
    arrived(h_got, r_h.at[1])
    total[:OUT[0], :] = own_a[yh, z] + h_got[...].astype(F32)
    me = z * 4 + yl * 2 + c
    for m in range(4):
        value = total[:, m * 128:(m + 1) * 128]
        squares[me, m:m + 1, :] = jnp.sum(value * value, axis=0, keepdims=True)
    for peer in group:
        copy_to(squares.at[me], squares.at[me], s_q.at[0], r_q.at[0], peer).start()
    low = lax.broadcasted_iota(jnp.int32, (WIDE, 128), 1) < 64

    def pair(m, part):
        at = pl.ds(pl.multiple_of(z * 288 + part * WIDE, 32), WIDE)
        a = xs[at, m * 256:m * 256 + 128].astype(F32)
        b = xs[at, m * 256 + 128:m * 256 + 256].astype(F32)
        upper, lower = pltpu.roll(a, 64, 1), pltpu.roll(b, 64, 1)
        return jnp.where(low, jnp.where(yh == 0, a, upper), jnp.where(yh == 0, lower, b))

    for part in range(PARTS):
        for m in range(4):
            fresh[part, m] = pair(m, part)
    arrived(squares.at[pl.ds(0, 15)], r_q.at[0])
    factor = lax.rsqrt(jnp.sum(squares[...], axis=0) * (1.0 / D) + EPS)
    starts, so_far = [], 0
    for j in range(16):
        starts.append(so_far)
        so_far = so_far + new_ref[j]
    here = pl.ds(x * 2, 2)
    for part in range(PARTS):
        rows_of = slice(part * WIDE, part * WIDE + WIDE)
        for m in range(4):
            value = total[rows_of, m * 128:(m + 1) * 128] * factor[m:m + 1, :] * gain[rows_of, :]
            fresh[part, m] = fresh[part, m] + value
        for n in range(8):
            sides = []
            for side in range(2):
                j = 2 * n + side
                within = lax.rem(x - starts[j] + 64, 4)
                i = jnp.minimum(lax.div(starts[j] + within - x, 4), 7)
                at = lax.div(i, 2)
                place = lax.rem(i + at, 2) * 4 + at
                value = fresh[part, lax.div(place, 2)]
                value = jnp.where(lax.rem(place, 2) == side, value, pltpu.roll(value, 64, 1))
                sides.append(jnp.where(within < new_ref[j], value, 0.0))
            f1[part, n] = jnp.where(low, sides[0], sides[1]).astype(BF)
        f1_got[part][here] = f1[part, here]
        for peer in others:
            copy_to(
                f1.at[part, pl.ds(peer["x"] * 2, 2)], f1_got[part].at[here], s_f.at[0], r_f.at[part], peer
            ).start()
    mine = [sum([jnp.where(x * 4 + n > m, new_ref[m], 0) for m in range(15)]) for n in range(4)]
    for part in range(PARTS):
        rows_of = slice(part * WIDE, part * WIDE + WIDE)
        arrived(f1_got[part].at[pl.ds(0, 6)], r_f.at[part])
        for e in range(8):
            dz, dy = e // 2, e % 2
            tz, ty = lax.rem(z + dz, 4), yl + dy - 2 * yl * dy
            sides = []
            for side in range(2):
                start = jnp.where(ty == 0, mine[side], mine[2 + side])
                sides.append(f1_got[part][lax.rem(start + tz, 4) * 2 + ty].astype(F32))
            value = jnp.where(low, sides[0], sides[1]).astype(BF)
            at = z * 2 + yl
            if e == 0:
                fin[at, c, rows_of, :] = value
            else:
                f2[part, e] = value
                copy_to(
                    f2.at[part, e], fin.at[at, c, rows_of], s_g.at[0], r_g.at[part], {"z": tz, "yl": ty}
                ).start()
    for part in range(PARTS):
        rows_of = slice(part * WIDE, part * WIDE + WIDE)
        arrived(fin.at[pl.ds(0, 7), c, rows_of], r_g.at[part])
        ref = fin.at[:, c, rows_of]
        copy_to(ref, ref, s_c.at[0], r_c.at[0], core).start()
    arrived(fin.at[:, c], r_c.at[0])
    first.sent()
    second.sent()
    gone(y_send, s_y.at[0])
    gone(y_relay, s_y.at[1])
    gone(h_send, s_h.at[0])
    gone(h_relay, s_h.at[1])
    gone(squares.at[pl.ds(0, 15)], s_q.at[0])
    gone(f1.at[:, pl.ds(0, 6)], s_f.at[0])
    gone(f2.at[:, pl.ds(0, 7)], s_g.at[0])
    gone(fin.at[:, c], s_c.at[0])


STAGE_IN = [
    VM((1152, 512), BF), VM((1152, 256), BF), VM((1152, 256), BF),
    VM((1152, 128), F32), VM((128, 128), F32), VM((64, 512), F32), VM((64, 512), F32),
    VM((576, 512), BF), VM((PARTS, 8, WIDE, 128), BF), VM((24, WIDE, 128), BF), VM((24, WIDE, 128), BF), VM((24, WIDE, 128), BF), VM((1152, 1024), BF), VM((16, 8, 128), F32),
    VM((2, 512, 512), F32), VM((2, 512, 512), F32), VM((512, 512), BF), VM((512, 512), BF), VM((2, 512, 512), F32),
    DMA((2,)), DMA((PARTS,)), DMA((4 * PARTS,)), DMA((PARTS,)), DMA((4 * PARTS,)), DMA((PARTS,)), DMA((PARTS,)),
    DMA((2,)), DMA((3,)), DMA((2,)), DMA((3,)), DMA((2 * PARTS,)), DMA((3 * PARTS,)), DMA((1,)), DMA((1,)),
    DMA((1,)), DMA((4,)), DMA((1,)), DMA((4,)),
]
STAGE_ATTEND = [
    VM((4, 256, 128), BF), VM((4, 256, 128), F32), VM((4, 256, 128), F32),
    DMA((1,)), DMA((2,)), DMA((1,)), DMA((1,)),
]
STAGE_OUT = (
    [VM((2, 2, OUT[0], 512), BF), VM((2, 2, OUT[0], 512), BF), VM((2, OUT[0], 512), BF), VM((2, OUT[0], 512), BF)]
    + [VM((2, 2, OUT[1], 256), BF), VM((2, 2, OUT[1], 256), BF), VM((2, OUT[1], 256), BF), VM((2, OUT[1], 256), BF)]
    + [VM((4, OUT[1], 512), BF)] * 3
    + [VM((OUT[0], 512), BF)] * 3
    + [VM((2, 4, OUT[0], 512), F32), VM((4, OUT[1], 512), F32), VM((288, 512), F32)]
    + [VM((16, 4, 128), F32), VM((PARTS, 4, WIDE, 128), F32)]
    + [VM((PARTS, 8, WIDE, 128), BF)] * 2
    + [VM((8, WIDE, 128), BF)] * PARTS
    + [DMA((2,)), DMA((3,)), DMA((2,)), DMA((3,))]
    + [DMA((2,)), DMA((3,)), DMA((2,)), DMA((2,)), DMA((1,)), DMA((1,)), DMA((1,)), DMA((PARTS,))]
    + [DMA((1,)), DMA((PARTS,)), DMA((1,)), DMA((1,))]
)
SHARED = [
    VM((256, 512), BF), VM((4, 256, 128), BF), VM((1152, 1024), BF), VM((1152, 512), BF), VM((16, 64, 512), BF),
    VM((288, 128), F32), VM((8, 256, 512), BF), DMA((4,)), DMA((6,)), DMA((1,)), DMA((2,)),
]


def kernel(old_ref, new_ref, order_ref, xt_in, pre_ref, post_ref, wq_in, wk_in, wv_in, wo_in, fin, *scratch):
    q, kv, xs, wo, ctx, gain_out, kvs, s_x, r_x, s_c, r_c = scratch[:11]
    scratch = scratch[11:]
    keys_values = KeysValues(kv, kvs, s_x, r_x, s_c, r_c)
    own_in, scratch = scratch[:len(STAGE_IN)], scratch[len(STAGE_IN):]
    own_attend, own_out = scratch[:len(STAGE_ATTEND)], scratch[len(STAGE_ATTEND):]
    end_in = stage_in(
        old_ref, order_ref, xt_in, pre_ref, post_ref, wq_in, wk_in, wv_in, wo_in, q, kv, xs, wo, gain_out, *own_in,
        keys_values,
    )
    end_attend = stage_attend(q, ctx, keys_values, kvs, *own_attend)
    end_in()
    stage_out(new_ref, ctx, xs, wo, gain_out, fin, *own_out)
    end_attend()


def run(old_blocks, new_blocks, order, xt, pre_gain, post_gain, w_query, w_key, w_value, w_out_t):
    smem = pl.BlockSpec(memory_space=pltpu.SMEM)
    vmem = pl.BlockSpec(memory_space=pltpu.VMEM)
    hbm = pl.BlockSpec(memory_space=pltpu.HBM)
    return pl.pallas_call(
        kernel,
        name="sublayer",
        out_shape=jax.ShapeDtypeStruct((8, 2, 288, 128), BF),
        in_specs=[smem, smem, smem, hbm, vmem, vmem, hbm, hbm, hbm, hbm],
        out_specs=vmem,
        scratch_shapes=SHARED + STAGE_IN + STAGE_ATTEND + STAGE_OUT,
        compiler_params=pltpu.CompilerParams(collective_id=0, has_side_effects=True, vmem_limit_bytes=62 * 2**20),
    )(old_blocks, new_blocks, order, xt, pre_gain, post_gain, w_query, w_key, w_value, w_out_t)


def per_device(
    x_old, old_blocks, new_blocks, order, pre_gain, post_gain, w_query, w_key, w_value, w_out_t
):
    c = lax.axis_index("c")
    fin = run(
        old_blocks, new_blocks, order, x_old.T, pre_gain.reshape(36, 128), post_gain.reshape(36, 128),
        w_query, w_key, w_value, w_out_t,
    )
    return lax.dynamic_slice(fin.reshape(16, 288, 128), (0, 0, c * 64), (16, 288, 64)).reshape(4608, 64).T


def solution(mesh):
    torus = Mesh(mesh.devices.reshape(4, 2, 2, 4, 2), ("x", "yl", "c", "z", "yh"))
    seq, tp = ("x", "yl", "c"), ("z", "yh")
    both = P(seq, tp)
    in_specs = (both, P(), P(), P(), P(), P(), both, both, both, both)
    return jax.shard_map(
        per_device, mesh=torus, in_specs=in_specs, out_specs=P(seq + tp, None), check_vma=False
    )
```

time: 125 us -> 122 us (0.976)
  Pallas kernels: 121 us -> 119 us
    pallas_call x1, Pallas kernels: 121 us -> 119 us  [run(): pl.pallas_call(kernel, name='sublayer', out_shape=jax.ShapeDtypeStruct((8...]
where the time goes in v4:
time: 122 us
  Pallas kernels  119 us (98%)
  local copies, waits for them, and re-layouts  2.94 us (2%)
    pallas_call x1, Pallas kernels, run(): pl.pallas_call(kernel, name='sublayer', out_shape=jax.ShapeDtypeStruct((8...  119 us

profile of v4, /device:TPU:1, one launch (start us, length us, event | category | flops | bytes accessed | tf_op | source)
XLA Modules:
  0.0 121.5 jit_solution(8567736991911282749)
XLA Ops:
  0.0 118.6 %sublayer.1 = bf16[8,2,288,128]{3,2,1,0:T(8,128)(2,1)} custom-call(s32[16]{0:T(128)} %old_ref.1, s32[16]{0:T(128)} %new_ref.1, s32[16]{0:T(128)} %order_ref.1, bf16[576,512]{1,0:T(8,128)(2,1)} %bitcast.8, f32[36,128]{1,0:T(8,128)} %bitcast.9, f32[36,128]{1,0:T(8,128)} %bitcast.10, bf16[288,512]{1,0:T(8,128)(2,1)} %wq_in.1, bf16[288,256]{1,0:T(8,128)(2,1)} %wk_in.1, ...), custom_call_target="tpu_custom_call" | custom-call | tf_op jit(solution)/shard_map/sublayer/pallas_call | solution.py:765
  118.6 1.7 %constant_dynamic-slice_fusion = bf16[16,288,64]{2,1,0:T(8,128)(2,1)S(1)} fusion(bf16[16,288,128]{2,1,0:T(8,128)(2,1)} %bitcast.7, s32[]{:T(128)S(6)} %select_n.3), kind=kLoop, calls=%fused_computation | loop fusion | bytes 1179652 | tf_op jit(solution)/shard_map/dynamic_slice | solution.py:784
  120.3 1.3 %copy.12 = bf16[4608,64]{0,1:T(8,128)(2,1)} copy(bf16[4608,64]{1,0:T(8,128)(2,1)S(1)} %bitcast.6) | data formatting | bytes 1179648 | tf_op jit(solution)/shard_map/reshape | solution.py:784

commit v5 on v4

--- a/solution.py
+++ b/solution.py
@@ -18,8 +18,9 @@
 F32 = jnp.float32
 VM = pltpu.VMEM
 OUT = (160, 128)
-PARTS = 3
-WIDE = 288 // PARTS
+IN = ((0, 32), (32, 64), (96, 96), (192, 96))
+BACK = ((0, 96), (96, 96), (192, 64), (256, 32))
+PARTS = 4
 DMA = pltpu.SemaphoreType.DMA
 
 
@@ -131,12 +132,11 @@
 def stage_in(
     old_ref, order_ref, xt_in, pre_ref, post_ref, wq_in, wk_in, wv_in, wo_in,
     q_out, kv_out, xs, wo, gain_out,
-    wq, wk, wv, gain, table, cos, sin, xt, slots, landed_0, landed_1, landed_2, normed, squares, near, other, to_y, from_y, mine,
+    wq, wk, wv, gain, table, cos, sin, xt, slots, landed, normed, squares, near, other, to_y, from_y, mine,
     s_w, s_one, r_one, s_two, r_two, s_three, r_three, s_wg, r_wg, s_og, r_og, s_z, r_z, s_q, r_q, s_c, r_c, s_y, r_y,
     keys_values,
 ):
     x, yl, c, z, yh = coords()
-    landed = (landed_0, landed_1, landed_2)
     ring_peers = [
         {"x": lax.rem(x + dx, 4), "c": c + dc - 2 * c * dc} for dx in range(4) for dc in range(2)
     ][1:]
@@ -144,7 +144,7 @@
     y_two = {"yl": 1 - yl, "yh": 1 - yh}
     group = [
         {"z": lax.rem(z + dz, 4), "yl": yl + dy - 2 * yl * dy, "c": c + dc - 2 * c * dc}
-        for dz in range(4) for dy in range(2) for dc in range(2)
+        for dz in (0, 2, 1, 3) for dy in range(2) for dc in range(2)
     ][1:]
     greet(ring_peers + [y_two] + group)
     into = pltpu.make_async_copy(xt_in, xt, s_w.at[1])
@@ -172,19 +172,19 @@
     for r in range(4):
         b = lax.rem(r - first + 64, 4)
         for h in range(2):
-            for half in range(PARTS):
-                at_rows = slice(h * 288 + half * WIDE, h * 288 + half * WIDE + WIDE)
+            for half, (begin, count) in enumerate(IN):
+                at_rows = slice(h * 288 + begin, h * 288 + begin + count)
                 part = [xt[at_rows, n * 128:(n + 1) * 128] for n in range(4)]
                 low = jnp.where(b == 0, part[0], part[1])
-                slots[half, r * 2 + h] = jnp.where(b < 2, low, jnp.where(b == 2, part[2], part[3]))
+                slots[half][r * 2 + h] = jnp.where(b < 2, low, jnp.where(b == 2, part[2], part[3]))
     here = x * 2 + c
     for half in range(PARTS):
-        landed[half][here] = slots[half, here]
+        landed[half][here] = slots[half][here]
     greeted(ring_peers + [y_two] + group)
     for half in range(PARTS):
         for d, peer in enumerate(ring_peers, 1):
             copy_to(
-                slots.at[half, peer["x"] * 2 + peer["c"]], landed[half].at[here],
+                slots[half].at[peer["x"] * 2 + peer["c"]], landed[half].at[here],
                 s_one.at[half], r_one.at[half * 4 + d // 2], peer,
             ).start()
     everything = wo.at[pl.ds(0, 864)]
@@ -216,18 +216,22 @@
             copy_to(slot_pair(half, dx, 0), slot_pair(half, dx, 1), s_two.at[half], r_two.at[n], y_two).start()
             copy = copy_to(slot_pair(half, dx, 0), slot_pair(half, dx, 2), s_three.at[half], r_three.at[half], y_one)
             pl.when(jnp.logical_not(straight))(copy.start)
-            if half == 2:
-                relay_y(dx)
+            if half >= 2:
+                relay_y(half * 4 - 8 + dx)
     me = z * 4 + yl * 2 + c
     first_buffer = jnp.where(straight, 0, 1)
 
     def part_rows(part):
-        return lambda chunk, half: rows(xs, chunk * 288 + part * WIDE + half * (WIDE // 2), WIDE // 2)
+        begin, count = IN[part]
+        return lambda chunk, half: rows(xs, chunk * 288 + begin + half * (count // 2), count // 2)
+
+    def some_rows(part):
+        return lambda n: xs.at[pl.ds(0, IN[part][1] // 2 * n)]
 
     gathers = [
         Gather4(
             [part_rows(part)], "z", z, some(s_z, 2 * part), some(r_z, 3 * part),
-            lambda n: xs.at[pl.ds(0, (WIDE // 2) * n)],
+            some_rows(part),
         )
         for part in range(PARTS)
     ]
@@ -243,26 +247,32 @@
         arrived(landed[half].at[pl.ds(16, 8)], r_three.at[half])
         for place in range(8):
             block = landed[half][sources[place]]
-            xs[pl.ds(pl.multiple_of(z * 288 + half * WIDE, 32), WIDE), place * 128:(place + 1) * 128] = block
+            begin, count = IN[half]
+            xs[pl.ds(pl.multiple_of(z * 288 + begin, 32), count), place * 128:(place + 1) * 128] = block
             wide = block.astype(F32)
             square = jnp.sum(wide * wide, axis=0, keepdims=True)
             if half > 0:
                 square = square + squares[me, place:place + 1, :]
             squares[me, place:place + 1, :] = square
+        if half == PARTS - 1:
+            for peer in group:
+                copy_to(squares.at[me], squares.at[me], s_q.at[0], r_q.at[0], peer).start()
         gathers[half].start()
 
-    for n in range(4, 12):
-        if n in (6, 10):
-            pick((n - 6) // 4)
+    pick(0)
+    for n in range(8, 16):
+        if n in (10, 14):
+            pick(1 + (n - 10) // 4)
+            if n == 10:
+                gathers[0].relay()
         relay_y(n)
-    pick(2)
+    pick(3)
+    gathers[1].relay()
     weights.relay()
     wo_all = Gather4(
         [out_rows], "x", x, some(s_og, 0), some(r_og, 0), lambda n: wo.at[pl.ds(0, 144 * n)]
     )
     wo_all.start()
-    for peer in group:
-        copy_to(squares.at[me], squares.at[me], s_q.at[0], r_q.at[0], peer).start()
     table[...] = jnp.zeros_like(table)
     table[0:36, :] = pre_ref[...]
     table[...] = table[...].T
@@ -271,7 +281,7 @@
     table[0:36, :] = post_ref[...]
     table[...] = table[...].T
     columns(gain_out, table, lambda n: z * 4 + yl * 2 + c, 1)
-    gathers[0].relay()
+    gathers[2].relay()
     half_head = HEAD // 2
     inverse = jnp.exp(
         lax.broadcasted_iota(jnp.int32, (half_head, 128), 0).astype(F32) * (-2.0 * math.log(10000.0) / HEAD)
@@ -281,8 +291,7 @@
         angle = inverse * place_of.astype(F32)
         cos[:, p * 128:(p + 1) * 128] = jnp.cos(angle)
         sin[:, p * 128:(p + 1) * 128] = jnp.sin(angle)
-    for part in (1, 2):
-        gathers[part].relay()
+    gathers[3].relay()
     arrived(squares.at[pl.ds(0, 15)], r_q.at[0])
     factor = lax.rsqrt(jnp.sum(squares[...], axis=0) * (1.0 / D) + EPS)
 
@@ -300,9 +309,11 @@
 
     pieces = {"q": (slice(0, 256), wq, 256), "k": (slice(256, 384), wk, 128), "v": (slice(384, 512), wv, 128)}
 
-    def corner(dst, y, core, late, names="qkv"):
-        low = lax.div(z, 2)
-        part = pl.ds(pl.multiple_of((1 - low if late else low) * 576, 16), 576)
+    def corner(dst, y, core, late, names="qkv", part=None):
+        if not late:
+            part = pl.ds(pl.multiple_of(lax.div(z, 2) * 576, 16), 576)
+        elif part is None:
+            part = pl.ds(pl.multiple_of(far * 288, 16), 288)
         right = normed[part, lanes(core * 512, 512)]
         for name in names:
             to, table_of, width = pieces[name]
@@ -324,12 +335,14 @@
     ]
     for dst, y, core in corners:
         corner(dst, y, core, False)
+    far = (3 - z) + 1 - 2 * lax.rem(3 - z, 2)
     norm(3 - z)
+    for dst, y, core in corners:
+        corner(dst, y, core, True, part=pl.ds(pl.multiple_of((3 - z) * 288, 16), 288))
     wo_all.relay()
     for one_part in gathers:
         one_part.far()
-    far = 3 - z
-    norm(far + 1 - 2 * lax.rem(far, 2))
+    norm(far)
     core = {"c": 1 - c}
 
     def over_core(n, name):
@@ -396,11 +409,13 @@
             turn_b = b * cos[:, cols] + a * sin[:, cols]
             q_out[part, cols] = (jnp.concatenate([turn_a, turn_b], axis=0) * scale_q).astype(BF)
 
-    def finish():
+    def out_weights():
         wo_all.near()
         wo_all.far()
+
+    def finish():
         for half in range(PARTS):
-            gone(slots.at[half, pl.ds(0, 7)], s_one.at[half])
+            gone(slots[half].at[pl.ds(0, 7)], s_one.at[half])
             gone(landed[half].at[pl.ds(0, 8)], s_two.at[half])
             gone(landed[half].at[pl.ds(0, 8)], s_three.at[half])
         gone(squares.at[pl.ds(0, 15)], s_q.at[0])
@@ -411,7 +426,7 @@
         for one_part in gathers:
             one_part.sent()
 
-    return finish
+    return out_weights, finish
 
 
 class KeysValues:
@@ -453,7 +468,7 @@
             gather.sent()
 
 
-def stage_attend(q_ref, ctx, keys_values, kvs, qs, acc, den, s_y, r_y, s_o, r_o):
+def stage_attend(q_ref, ctx, keys_values, kvs, early_sums, qs, acc, den, s_y, r_y, s_o, r_o):
     x, yl, c, z, yh = coords()
     core, y_one = {"c": 1 - c}, {"yl": 1 - yl}
     for p in range(4):
@@ -499,7 +514,7 @@
         arrived(ctx.at[pl.ds(0, 4), :, pl.ds(0, 256)], r_y.at[step])
         for half in range(2):
             ref = region(c, 1 - yl, half * 8 + 2 * step, 2)
-            copy_to(ref, ref, s_o.at[0], r_o.at[0], core).start()
+            copy_to(ref, ref, s_o.at[0], r_o.at[1], core).start()
 
     tiles([(0, 0), (1, 0), (1, 1)], c, (0, 2))
     keys_values.from_core(0)
@@ -513,8 +528,10 @@
     tiles([(3 - c, 2), (3, 3 - c)], 1 - c)
     put(1)
     pass_on(0)
+    arrived(ctx.at[pl.ds(0, 8), :, pl.ds(0, 256)], r_o.at[0])
+    early_sums()
     pass_on(1)
-    arrived(ctx.at[:, :, pl.ds(0, 256)], r_o.at[0])
+    arrived(ctx.at[pl.ds(0, 8), :, pl.ds(0, 256)], r_o.at[1])
 
     def finish():
         gone(ctx.at[pl.ds(0, 8), :, pl.ds(0, 256)], s_y.at[0])
@@ -562,11 +579,33 @@
         gone(self.more, self.s.at[1])
 
 
+class OutSums:
+    def __init__(self, ctx, wo, own_y, own_a, own_b):
+        _, yl, _, _, yh = coords()
+        self.ctx, self.wo, self.yl = ctx, wo, yl
+        self.all = [(own_y, 1 - yh, 1), (own_a.at[0], 0, 0), (own_a.at[1], 1, 0), (own_b, yh, 1)]
+
+    def product(self, n, y):
+        _, half, part = self.all[n]
+        left = self.wo[part * 4 * OUT[0]:part * 4 * OUT[0] + 4 * OUT[part], lanes(y * 256, 256)]
+        right = self.ctx[pl.ds(half * 8, 8), :, lanes(y * 256, 256)].reshape(512, 256)
+        value = lax.dot_general(left, right, (((1,), (1,)), ((), ())), preferred_element_type=F32)
+        return value.reshape(4, OUT[part], 512)
+
+    def early(self):
+        for n, (dst, _, _) in enumerate(self.all):
+            dst[...] = self.product(n, self.yl)
+
+    def late(self, n):
+        dst = self.all[n][0]
+        dst[...] = dst[...] + self.product(n, 1 - self.yl)
+
+
 def stage_out(
-    new_ref, ctx, xs, wo, gain, fin,
+    new_ref, ctx, xs, wo, gain, out_ref, out_sums, own_y, own_a, own_b,
     a_send, a_got, a_more, a_more_got, b_send, b_got, b_more, b_more_got,
-    y_send, y_relay, y_got, h_send, h_relay, h_got, own_a, own_b, total,
-    squares, fresh, f1, f2, f1_got_0, f1_got_1, f1_got_2,
+    y_send, y_relay, y_got, h_send, h_relay, h_got, total,
+    squares, fresh, f1, f2, f1_got, fin,
     a_s, a_r, b_s, b_r, s_y, r_y, s_h, r_h, s_q, r_q, s_f, r_f, s_g, r_g, s_c, r_c,
 ):
     x, yl, c, z, yh = coords()
@@ -574,27 +613,22 @@
     y_one, y_two = {"yl": 1 - yl}, {"yl": 1 - yl, "yh": 1 - yh}
     group = [
         {"z": lax.rem(z + dz, 4), "yl": yl + dy - 2 * yl * dy, "c": c + dc - 2 * c * dc}
-        for dz in range(4) for dy in range(2) for dc in range(2)
-    ][1:]
-    others = [{"x": lax.rem(x + dx, 4)} for dx in range(1, 4)]
-    f1_got = (f1_got_0, f1_got_1, f1_got_2)
-
-    def sums_of(half, part):
-        left = wo[part * 4 * OUT[0]:part * 4 * OUT[0] + 4 * OUT[part], :]
-        right = ctx[pl.ds(half * 8, 8)].reshape(512, 512)
-        value = lax.dot_general(left, right, (((1,), (1,)), ((), ())), preferred_element_type=F32)
-        return value.reshape(4, OUT[part], 512)
-
-    y_send[...] = sums_of(1 - yh, 1).astype(BF)
+        for dz in (0, 2, 1, 3) for dy in (0, 1) for dc in (0, 1)
+    ]
+    group = group[4:] + group[1:4]
+    others = [{"x": lax.rem(x + dx, 4)} for dx in (2, 1, 3)]
+
+    out_sums.late(0)
+    y_send[...] = own_y[...].astype(BF)
     for n in range(4):
         copy_to(y_send.at[n], y_relay.at[n], s_y.at[0], r_y.at[n // 2], y_two if n % 2 else y_one).start()
     first = Reduce4(z, a_send, a_got, a_more, a_more_got, a_s, a_r)
     for part in range(2):
-        own_a[part] = sums_of(part, 0)
+        out_sums.late(1 + part)
         first.give(part, 1, own_a[part, first.chunk(part, 1)].astype(BF))
     for part in range(2):
         first.give(part, 0, own_a[part, first.chunk(part, 0)].astype(BF))
-    own_b[...] = sums_of(yh, 1)
+    out_sums.late(3)
 
     def forward(step):
         arrived(y_relay.at[pl.ds(0, 2)], r_y.at[step])
@@ -631,10 +665,12 @@
         squares[me, m:m + 1, :] = jnp.sum(value * value, axis=0, keepdims=True)
     for peer in group:
         copy_to(squares.at[me], squares.at[me], s_q.at[0], r_q.at[0], peer).start()
-    low = lax.broadcasted_iota(jnp.int32, (WIDE, 128), 1) < 64
+    lane = lax.broadcasted_iota(jnp.int32, (96, 128), 1)
 
     def pair(m, part):
-        at = pl.ds(pl.multiple_of(z * 288 + part * WIDE, 32), WIDE)
+        begin, count = BACK[part]
+        low = lane[:count] < 64
+        at = pl.ds(pl.multiple_of(z * 288 + begin, 32), count)
         a = xs[at, m * 256:m * 256 + 128].astype(F32)
         b = xs[at, m * 256 + 128:m * 256 + 256].astype(F32)
         upper, lower = pltpu.roll(a, 64, 1), pltpu.roll(b, 64, 1)
@@ -642,7 +678,7 @@
 
     for part in range(PARTS):
         for m in range(4):
-            fresh[part, m] = pair(m, part)
+            fresh[part][m] = pair(m, part)
     arrived(squares.at[pl.ds(0, 15)], r_q.at[0])
     factor = lax.rsqrt(jnp.sum(squares[...], axis=0) * (1.0 / D) + EPS)
     starts, so_far = [], 0
@@ -650,11 +686,12 @@
         starts.append(so_far)
         so_far = so_far + new_ref[j]
     here = pl.ds(x * 2, 2)
-    for part in range(PARTS):
-        rows_of = slice(part * WIDE, part * WIDE + WIDE)
+    for part, (begin, count) in enumerate(BACK):
+        rows_of = slice(begin, begin + count)
+        low = lane[:count] < 64
         for m in range(4):
             value = total[rows_of, m * 128:(m + 1) * 128] * factor[m:m + 1, :] * gain[rows_of, :]
-            fresh[part, m] = fresh[part, m] + value
+            fresh[part][m] = fresh[part][m] + value
         for n in range(8):
             sides = []
             for side in range(2):
@@ -663,20 +700,21 @@
                 i = jnp.minimum(lax.div(starts[j] + within - x, 4), 7)
                 at = lax.div(i, 2)
                 place = lax.rem(i + at, 2) * 4 + at
-                value = fresh[part, lax.div(place, 2)]
+                value = fresh[part][lax.div(place, 2)]
                 value = jnp.where(lax.rem(place, 2) == side, value, pltpu.roll(value, 64, 1))
                 sides.append(jnp.where(within < new_ref[j], value, 0.0))
-            f1[part, n] = jnp.where(low, sides[0], sides[1]).astype(BF)
-        f1_got[part][here] = f1[part, here]
+            f1[part][n] = jnp.where(low, sides[0], sides[1]).astype(BF)
+        f1_got[part][here] = f1[part][here]
         for peer in others:
             copy_to(
-                f1.at[part, pl.ds(peer["x"] * 2, 2)], f1_got[part].at[here], s_f.at[0], r_f.at[part], peer
+                f1[part].at[pl.ds(peer["x"] * 2, 2)], f1_got[part].at[here], s_f.at[part], r_f.at[part], peer
             ).start()
     mine = [sum([jnp.where(x * 4 + n > m, new_ref[m], 0) for m in range(15)]) for n in range(4)]
-    for part in range(PARTS):
-        rows_of = slice(part * WIDE, part * WIDE + WIDE)
+    for part, (begin, count) in enumerate(BACK):
+        rows_of = slice(begin, begin + count)
+        low = lane[:count] < 64
         arrived(f1_got[part].at[pl.ds(0, 6)], r_f.at[part])
-        for e in range(8):
+        for e in (5, 4, 3, 7, 2, 6, 1, 0):
             dz, dy = e // 2, e % 2
             tz, ty = lax.rem(z + dz, 4), yl + dy - 2 * yl * dy
             sides = []
@@ -688,16 +726,22 @@
             if e == 0:
                 fin[at, c, rows_of, :] = value
             else:
-                f2[part, e] = value
+                f2[part][e] = value
                 copy_to(
-                    f2.at[part, e], fin.at[at, c, rows_of], s_g.at[0], r_g.at[part], {"z": tz, "yl": ty}
+                    f2[part].at[e], fin.at[at, c, rows_of], s_g.at[part], r_g.at[part], {"z": tz, "yl": ty}
                 ).start()
-    for part in range(PARTS):
-        rows_of = slice(part * WIDE, part * WIDE + WIDE)
+    for part, (begin, count) in enumerate(BACK):
+        rows_of = slice(begin, begin + count)
         arrived(fin.at[pl.ds(0, 7), c, rows_of], r_g.at[part])
         ref = fin.at[:, c, rows_of]
         copy_to(ref, ref, s_c.at[0], r_c.at[0], core).start()
     arrived(fin.at[:, c], r_c.at[0])
+    mine_of = lax.broadcasted_iota(jnp.int32, (64, 128), 0) + c * 64
+    pick = jnp.where(lane[:64] == mine_of, 1.0, 0.0).astype(BF)
+    for n in range(4):
+        block = fin[2 * n:2 * n + 2].reshape(1152, 128)
+        value = lax.dot_general(pick, block, (((1,), (1,)), ((), ())), preferred_element_type=F32)
+        out_ref[:, n * 1152:(n + 1) * 1152] = value.astype(BF)
     first.sent()
     second.sent()
     gone(y_send, s_y.at[0])
@@ -705,15 +749,16 @@
     gone(h_send, s_h.at[0])
     gone(h_relay, s_h.at[1])
     gone(squares.at[pl.ds(0, 15)], s_q.at[0])
-    gone(f1.at[:, pl.ds(0, 6)], s_f.at[0])
-    gone(f2.at[:, pl.ds(0, 7)], s_g.at[0])
+    for part in range(PARTS):
+        gone(f1[part].at[pl.ds(0, 6)], s_f.at[part])
+        gone(f2[part].at[pl.ds(0, 7)], s_g.at[part])
     gone(fin.at[:, c], s_c.at[0])
 
 
 STAGE_IN = [
     VM((1152, 512), BF), VM((1152, 256), BF), VM((1152, 256), BF),
     VM((1152, 128), F32), VM((128, 128), F32), VM((64, 512), F32), VM((64, 512), F32),
-    VM((576, 512), BF), VM((PARTS, 8, WIDE, 128), BF), VM((24, WIDE, 128), BF), VM((24, WIDE, 128), BF), VM((24, WIDE, 128), BF), VM((1152, 1024), BF), VM((16, 8, 128), F32),
+    VM((576, 512), BF), [VM((8, count, 128), BF) for _, count in IN], [VM((24, count, 128), BF) for _, count in IN], VM((1152, 1024), BF), VM((16, 8, 128), F32),
     VM((2, 512, 512), F32), VM((2, 512, 512), F32), VM((512, 512), BF), VM((512, 512), BF), VM((2, 512, 512), F32),
     DMA((2,)), DMA((PARTS,)), DMA((4 * PARTS,)), DMA((PARTS,)), DMA((4 * PARTS,)), DMA((PARTS,)), DMA((PARTS,)),
     DMA((2,)), DMA((3,)), DMA((2,)), DMA((3,)), DMA((2 * PARTS,)), DMA((3 * PARTS,)), DMA((1,)), DMA((1,)),
@@ -721,40 +766,46 @@
 ]
 STAGE_ATTEND = [
     VM((4, 256, 128), BF), VM((4, 256, 128), F32), VM((4, 256, 128), F32),
-    DMA((1,)), DMA((2,)), DMA((1,)), DMA((1,)),
+    DMA((1,)), DMA((2,)), DMA((1,)), DMA((2,)),
 ]
 STAGE_OUT = (
     [VM((2, 2, OUT[0], 512), BF), VM((2, 2, OUT[0], 512), BF), VM((2, OUT[0], 512), BF), VM((2, OUT[0], 512), BF)]
     + [VM((2, 2, OUT[1], 256), BF), VM((2, 2, OUT[1], 256), BF), VM((2, OUT[1], 256), BF), VM((2, OUT[1], 256), BF)]
     + [VM((4, OUT[1], 512), BF)] * 3
     + [VM((OUT[0], 512), BF)] * 3
-    + [VM((2, 4, OUT[0], 512), F32), VM((4, OUT[1], 512), F32), VM((288, 512), F32)]
-    + [VM((16, 4, 128), F32), VM((PARTS, 4, WIDE, 128), F32)]
-    + [VM((PARTS, 8, WIDE, 128), BF)] * 2
-    + [VM((8, WIDE, 128), BF)] * PARTS
+    + [VM((288, 512), F32), VM((16, 4, 128), F32), [VM((4, count, 128), F32) for _, count in BACK]]
+    + [[VM((8, count, 128), BF) for _, count in BACK]] * 3
+    + [VM((8, 2, 288, 128), BF)]
     + [DMA((2,)), DMA((3,)), DMA((2,)), DMA((3,))]
-    + [DMA((2,)), DMA((3,)), DMA((2,)), DMA((2,)), DMA((1,)), DMA((1,)), DMA((1,)), DMA((PARTS,))]
-    + [DMA((1,)), DMA((PARTS,)), DMA((1,)), DMA((1,))]
+    + [DMA((2,)), DMA((3,)), DMA((2,)), DMA((2,)), DMA((1,)), DMA((1,)), DMA((PARTS,)), DMA((PARTS,))]
+    + [DMA((PARTS,)), DMA((PARTS,)), DMA((1,)), DMA((1,))]
 )
 SHARED = [
     VM((256, 512), BF), VM((4, 256, 128), BF), VM((1152, 1024), BF), VM((1152, 512), BF), VM((16, 64, 512), BF),
     VM((288, 128), F32), VM((8, 256, 512), BF), DMA((4,)), DMA((6,)), DMA((1,)), DMA((2,)),
+    VM((4, OUT[1], 512), F32), VM((2, 4, OUT[0], 512), F32), VM((4, OUT[1], 512), F32),
 ]
 
 
-def kernel(old_ref, new_ref, order_ref, xt_in, pre_ref, post_ref, wq_in, wk_in, wv_in, wo_in, fin, *scratch):
-    q, kv, xs, wo, ctx, gain_out, kvs, s_x, r_x, s_c, r_c = scratch[:11]
-    scratch = scratch[11:]
+def kernel(old_ref, new_ref, order_ref, xt_in, pre_ref, post_ref, wq_in, wk_in, wv_in, wo_in, out_ref, *scratch):
+    q, kv, xs, wo, ctx, gain_out, kvs, s_x, r_x, s_c, r_c, own_y, own_a, own_b = scratch[:14]
+    scratch = scratch[14:]
+    out_sums = OutSums(ctx, wo, own_y, own_a, own_b)
     keys_values = KeysValues(kv, kvs, s_x, r_x, s_c, r_c)
     own_in, scratch = scratch[:len(STAGE_IN)], scratch[len(STAGE_IN):]
     own_attend, own_out = scratch[:len(STAGE_ATTEND)], scratch[len(STAGE_ATTEND):]
-    end_in = stage_in(
+    out_weights, end_in = stage_in(
         old_ref, order_ref, xt_in, pre_ref, post_ref, wq_in, wk_in, wv_in, wo_in, q, kv, xs, wo, gain_out, *own_in,
         keys_values,
     )
-    end_attend = stage_attend(q, ctx, keys_values, kvs, *own_attend)
+
+    def early_sums():
+        out_weights()
+        out_sums.early()
+
+    end_attend = stage_attend(q, ctx, keys_values, kvs, early_sums, *own_attend)
     end_in()
-    stage_out(new_ref, ctx, xs, wo, gain_out, fin, *own_out)
+    stage_out(new_ref, ctx, xs, wo, gain_out, out_ref, out_sums, own_y, own_a, own_b, *own_out)
     end_attend()
 
 
@@ -765,7 +816,7 @@
     return pl.pallas_call(
         kernel,
         name="sublayer",
-        out_shape=jax.ShapeDtypeStruct((8, 2, 288, 128), BF),
+        out_shape=jax.ShapeDtypeStruct((64, D), BF),
         in_specs=[smem, smem, smem, hbm, vmem, vmem, hbm, hbm, hbm, hbm],
         out_specs=vmem,
         scratch_shapes=SHARED + STAGE_IN + STAGE_ATTEND + STAGE_OUT,
@@ -776,12 +827,10 @@
 def per_device(
     x_old, old_blocks, new_blocks, order, pre_gain, post_gain, w_query, w_key, w_value, w_out_t
 ):
-    c = lax.axis_index("c")
-    fin = run(
+    return run(
         old_blocks, new_blocks, order, x_old.T, pre_gain.reshape(36, 128), post_gain.reshape(36, 128),
         w_query, w_key, w_value, w_out_t,
     )
-    return lax.dynamic_slice(fin.reshape(16, 288, 128), (0, 0, c * 64), (16, 288, 64)).reshape(4608, 64).T
 
 
 def solution(mesh):

time: 122 us -> 118 us (0.967)
  Pallas kernels: 119 us -> 116 us
    pallas_call x1, Pallas kernels: 119 us -> 116 us  [run(): pl.pallas_call(kernel, name='sublayer', out_shape=jax.ShapeDtypeStruct((6...]
    unnamed x0 -> x1, local copies, waits for them, and re-layouts: none -> 1.92 us
    dynamic_slice x1 -> x0, local copies, waits for them, and re-layouts: 1.66 us -> none  [per_device(): lax.dynamic_slice(fin.reshape(16, 288, 128), (0, 0, c * 64), (16, 288, 64))]
    reshape x1 -> x0, local copies, waits for them, and re-layouts: 1.27 us -> none  [per_device(): lax.dynamic_slice(fin.reshape(16, 288, 128), (0, 0, c * 64), (16, 288, 64))]
where the time goes in v5:
time: 118 us
  Pallas kernels  116 us (98%)
  local copies, waits for them, and re-layouts  1.92 us (2%)
    pallas_call x1, Pallas kernels, run(): pl.pallas_call(kernel, name='sublayer', out_shape=jax.ShapeDtypeStruct((6...  116 us

profile of v5, /device:TPU:1, one launch (start us, length us, event | category | flops | bytes accessed | tf_op | source)
XLA Modules:
  0.0 118.1 jit_solution(17954120965364563813)
XLA Ops:
  0.0 116.2 %sublayer.1 = bf16[64,4608]{1,0:T(8,128)(2,1)} custom-call(s32[16]{0:T(128)} %old_ref.1, s32[16]{0:T(128)} %new_ref.1, s32[16]{0:T(128)} %order_ref.1, bf16[576,512]{1,0:T(8,128)(2,1)} %bitcast.3, f32[36,128]{1,0:T(8,128)} %bitcast.4, f32[36,128]{1,0:T(8,128)} %bitcast.5, bf16[288,512]{1,0:T(8,128)(2,1)} %wq_in.1, bf16[288,256]{1,0:T(8,128)(2,1)} %wk_in.1, ...), custom_call_target="tpu_custom_call" | custom-call | tf_op jit(solution)/shard_map/sublayer/pallas_call | solution.py:816
  116.2 1.9 %copy.12 = bf16[64,4608]{1,0:T(8,128)(2,1)} copy(bf16[64,4608]{1,0:T(8,128)(2,1)} %sublayer.1) | data formatting | bytes 1179648

commit v6 on v5

--- a/solution.py
+++ b/solution.py
@@ -17,7 +17,7 @@
 BF = jnp.bfloat16
 F32 = jnp.float32
 VM = pltpu.VMEM
-OUT = (160, 128)
+OUT = (144, 144)
 IN = ((0, 32), (32, 64), (96, 96), (192, 96))
 BACK = ((0, 96), (96, 96), (192, 64), (256, 32))
 PARTS = 4
@@ -618,8 +618,11 @@
     group = group[4:] + group[1:4]
     others = [{"x": lax.rem(x + dx, 4)} for dx in (2, 1, 3)]
 
+    one, two = z + 1 - 2 * lax.rem(z, 2), 3 - z
+    wanted = (two + 1 - 2 * lax.rem(two, 2), one, two, z)
     out_sums.late(0)
-    y_send[...] = own_y[...].astype(BF)
+    for n in range(4):
+        y_send[n] = own_y[wanted[n]].astype(BF)
     for n in range(4):
         copy_to(y_send.at[n], y_relay.at[n], s_y.at[0], r_y.at[n // 2], y_two if n % 2 else y_one).start()
     first = Reduce4(z, a_send, a_got, a_more, a_more_got, a_s, a_r)
@@ -633,28 +636,35 @@
     def forward(step):
         arrived(y_relay.at[pl.ds(0, 2)], r_y.at[step])
         for n in (2 * step, 2 * step + 1):
-            copy_to(y_relay.at[n], y_got.at[n], s_y.at[1], r_y.at[2], y_one if n % 2 else y_two).start()
+            copy_to(y_relay.at[n], y_got.at[n], s_y.at[1], r_y.at[2 + step], y_one if n % 2 else y_two).start()
 
     forward(0)
     first.pass_on([own_a[0, first.two], own_a[1, first.one]])
     forward(1)
+    second = Reduce4(z, b_send, b_got, b_more, b_more_got, b_s, b_r)
+    cols = (slice(0, 256), slice(256, 512))
+
+    def over_y(step):
+        arrived(y_got.at[pl.ds(0, 2)], r_y.at[2 + step])
+        for n in (2 * step, 2 * step + 1):
+            own_b[wanted[n]] = own_b[wanted[n]] + y_got[n].astype(F32)
+
+    over_y(0)
+    second.give(0, 1, own_b[wanted[0], :, cols[0]].astype(BF))
+    second.give(1, 1, own_b[wanted[0], :, cols[1]].astype(BF))
+    second.give(0, 0, own_b[one, :, cols[0]].astype(BF))
     for part, value in enumerate(first.own([own_a[0, z], own_a[1, z]])):
         own_a[part, z] = value
     h_send[...] = own_a[1 - yh, z].astype(BF)
     spans = (slice(0, 80), slice(80, OUT[0]))
     for n, peer in enumerate((y_one, y_two)):
         copy_to(h_send.at[spans[n]], h_relay.at[spans[n]], s_h.at[0], r_h.at[0], peer).start()
-    second = Reduce4(z, b_send, b_got, b_more, b_more_got, b_s, b_r)
-    arrived(y_got, r_y.at[2])
-    own_b[...] = own_b[...] + y_got[...].astype(F32)
-    cols = (slice(0, 256), slice(256, 512))
-    for slot in (1, 0):
-        for part in range(2):
-            second.give(part, slot, own_b[second.chunk(part, slot), :, cols[part]].astype(BF))
+    over_y(1)
+    second.give(1, 0, own_b[two, :, cols[1]].astype(BF))
+    second.pass_on([own_b[two, :, cols[0]], own_b[one, :, cols[1]]])
     arrived(h_relay, r_h.at[0])
     for n, peer in enumerate((y_two, y_one)):
         copy_to(h_relay.at[spans[n]], h_got.at[spans[n]], s_h.at[1], r_h.at[1], peer).start()
-    second.pass_on([own_b[second.two, :, cols[0]], own_b[second.one, :, cols[1]]])
     for part, value in enumerate(second.own([own_b[z, :, cols[0]], own_b[z, :, cols[1]]])):
         total[OUT[0]:, cols[part]] = value
     arrived(h_got, r_h.at[1])
@@ -777,7 +787,7 @@
     + [[VM((8, count, 128), BF) for _, count in BACK]] * 3
     + [VM((8, 2, 288, 128), BF)]
     + [DMA((2,)), DMA((3,)), DMA((2,)), DMA((3,))]
-    + [DMA((2,)), DMA((3,)), DMA((2,)), DMA((2,)), DMA((1,)), DMA((1,)), DMA((PARTS,)), DMA((PARTS,))]
+    + [DMA((2,)), DMA((4,)), DMA((2,)), DMA((2,)), DMA((1,)), DMA((1,)), DMA((PARTS,)), DMA((PARTS,))]
     + [DMA((PARTS,)), DMA((PARTS,)), DMA((1,)), DMA((1,))]
 )
 SHARED = [

time: 118 us -> 117 us (level)
    pallas_call x1, Pallas kernels: 116 us -> 115 us  [run(): pl.pallas_call(kernel, name='sublayer', out_shape=jax.ShapeDtypeStruct((6...]
where the time goes in v6:
time: 117 us
  Pallas kernels  115 us (98%)
  local copies, waits for them, and re-layouts  1.92 us (2%)
    pallas_call x1, Pallas kernels, run(): pl.pallas_call(kernel, name='sublayer', out_shape=jax.ShapeDtypeStruct((6...  115 us

profile of v6, /device:TPU:1, one launch (start us, length us, event | category | flops | bytes accessed | tf_op | source)
XLA Modules:
  0.0 116.6 jit_solution(17155205621163556049)
XLA Ops:
  0.0 114.7 %sublayer.1 = bf16[64,4608]{1,0:T(8,128)(2,1)} custom-call(s32[16]{0:T(128)} %old_ref.1, s32[16]{0:T(128)} %new_ref.1, s32[16]{0:T(128)} %order_ref.1, bf16[576,512]{1,0:T(8,128)(2,1)} %bitcast.3, f32[36,128]{1,0:T(8,128)} %bitcast.4, f32[36,128]{1,0:T(8,128)} %bitcast.5, bf16[288,512]{1,0:T(8,128)(2,1)} %wq_in.1, bf16[288,256]{1,0:T(8,128)(2,1)} %wk_in.1, ...), custom_call_target="tpu_custom_call" | custom-call | tf_op jit(solution)/shard_map/sublayer/pallas_call | solution.py:826
  114.7 1.9 %copy.12 = bf16[64,4608]{1,0:T(8,128)(2,1)} copy(bf16[64,4608]{1,0:T(8,128)(2,1)} %sublayer.1) | data formatting | bytes 1179648

commit v7 on v6

--- a/solution.py
+++ b/solution.py
@@ -367,8 +367,9 @@
     for name in "kv":
         corner(*corners[0], True, name)
         over_core(0, name)
-    corner(*corners[1], True, "kv")
+    corner(*corners[1], True, "k")
     over_y("k")
+    corner(*corners[1], True, "v")
     corner(*corners[0], True, "q")
     over_core(0, "q")
     over_y("v")

time: 117 us -> 117 us (level)
  no operation moved by 1% of the time
where the time goes in v7:
time: 117 us
  Pallas kernels  115 us (98%)
  local copies, waits for them, and re-layouts  1.92 us (2%)
    pallas_call x1, Pallas kernels, run(): pl.pallas_call(kernel, name='sublayer', out_shape=jax.ShapeDtypeStruct((6...  115 us

profile of v7, /device:TPU:1, one launch (start us, length us, event | category | flops | bytes accessed | tf_op | source)
XLA Modules:
  0.0 116.6 jit_solution(2867291904488523074)
XLA Ops:
  0.0 114.7 %sublayer.1 = bf16[64,4608]{1,0:T(8,128)(2,1)} custom-call(s32[16]{0:T(128)} %old_ref.1, s32[16]{0:T(128)} %new_ref.1, s32[16]{0:T(128)} %order_ref.1, bf16[576,512]{1,0:T(8,128)(2,1)} %bitcast.3, f32[36,128]{1,0:T(8,128)} %bitcast.4, f32[36,128]{1,0:T(8,128)} %bitcast.5, bf16[288,512]{1,0:T(8,128)(2,1)} %wq_in.1, bf16[288,256]{1,0:T(8,128)(2,1)} %wk_in.1, ...), custom_call_target="tpu_custom_call" | custom-call | tf_op jit(solution)/shard_map/sublayer/pallas_call | solution.py:827
  114.7 1.9 %copy.12 = bf16[64,4608]{1,0:T(8,128)(2,1)} copy(bf16[64,4608]{1,0:T(8,128)(2,1)} %sublayer.1) | data formatting | bytes 1179648
